TPU v7x, 32 devices: a whole 2x2x4 slice. The times are simulated.
32 devices in a mesh: mem: 2 (over x), col: 16 (over z, y, core).
Axes of the slice: x: 2, y: 2, z: 4, core: 2. Of those that a mesh axis runs over, the one named last changes fastest.
Arguments:
- state_a: bfloat16 [64, 1048576], P('mem', 'col'), may hold values from -12 to 12
- state_b: bfloat16 [64, 1048576], P('mem', 'col'), may hold values from -12 to 12
- obs_index: int32 [2, 8192, 16], P(None, ('col', 'mem')), may hold values from 0 to 127
- observation_count: int32 [2, 8192], P(None, ('col', 'mem')), may hold values from 1 to 16, as said below
- obs_value: float32 [2, 8192, 16], P(None, ('col', 'mem')), may hold values from -32 to 32
- obs_weight: float32 [2, 8192, 16], P(None, ('col', 'mem')), may hold values from 0.02 to 0.2
Outputs:
- analysis_a: bfloat16 [64, 1048576], P(None, ('col', 'mem'))
- analysis_b: bfloat16 [64, 1048576], P(None, ('col', 'mem'))
- transform: float32 [64, 64], replicated
Inputs may be any that keep to these rules, and one draw needn't show every extreme that they name: Slot s of block b of group g is an observation when s < observation_count[g, b]; for each group, every aligned run of 256 blocks holds a block with all 16 slots live.
All inputs are finite; a program needn't handle non-finite values.
Results may differ from a plain program's by a relative error of at most 0.005.
Values may be sent and summed in bfloat16 or wider, within the bound.
No kernel may reach another device: no remote copies, remote signals or barrier semaphores. Data moves between devices by JAX's collectives and lax.ppermute only.
A program may use at most 64 MiB of HBM per device.

v0:
```python
import jax
import jax.numpy as jnp
from jax import lax
from jax.sharding import PartitionSpec as P

ITERS = 24


def inverse_root(amat):
    scale = jnp.sqrt(jnp.sum(amat * amat))
    eye = jnp.eye(amat.shape[0], dtype=jnp.float32)

    def forward_step(step, carry):
        yn, zn = carry
        tm = 1.5 * eye - 0.5 * jnp.dot(zn, yn, precision=lax.Precision.HIGHEST)
        return (
            jnp.dot(yn, tm, precision=lax.Precision.HIGHEST),
            jnp.dot(tm, zn, precision=lax.Precision.HIGHEST),
        )

    yn, zn = lax.fori_loop(0, ITERS, forward_step, (amat / scale, eye))
    return (zn, scale)


def make_transform(gram_product, cross, misfit, total):
    members = gram_product.shape[0]
    scl = (members - 1.0) / total
    gs = scl * gram_product
    bs = scl * cross
    qval = scl * misfit
    tval = jnp.trace(gs)
    rho = (1.0 + qval / (members - 1.0)) / (1.0 + tval / (members - 1.0))
    amat = (members - 1.0) / rho * jnp.eye(members, dtype=jnp.float32) + gs
    zn, scale = inverse_root(amat)
    pmat = jnp.dot(zn, zn, precision=lax.Precision.HIGHEST) / scale
    wbar = jnp.dot(pmat, bs, precision=lax.Precision.HIGHEST)
    return jnp.sqrt(members - 1.0) * zn / jnp.sqrt(scale) + wbar[:, None]


def shards(state_a, state_b, obs_index, observation_count, obs_value, obs_weight):
    members = state_a.shape[0]
    group_column_sets = state_a.shape[1]
    nmem = lax.axis_size("mem")
    piece = group_column_sets // nmem
    everyone = members * nmem
    nblk = obs_index.shape[1]
    slots = obs_index.shape[2]
    width = nblk * slots
    live = (
        lax.broadcasted_iota(jnp.int32, (2, nblk, slots), 2) < observation_count[:, :, None]
    ).astype(jnp.float32)
    live = live.reshape(2, width)
    weights = live * obs_weight.reshape(2, width)
    observed = obs_value.reshape(2, width)

    def observe(columns, index, blocks):
        lanes = lax.broadcasted_iota(jnp.int32, (blocks, slots, 128), 2)
        onehot = (index[:, :, None] == lanes).astype(jnp.bfloat16)
        taken = jnp.einsum(
            "kbc,bsc->kbs",
            columns.reshape(columns.shape[0], blocks, 128),
            onehot,
            preferred_element_type=jnp.float32,
        )
        return taken.reshape(columns.shape[0], blocks * slots)

    def statistics(hx, group):
        hmean = jnp.mean(hx, axis=0)
        anomaly_rows = hx - hmean[None]
        innov = observed[group] - hmean
        wt = weights[group]
        scaled_anomaly = anomaly_rows * wt[None]
        gram_product = jnp.einsum(
            "kn,ln->kl", scaled_anomaly, anomaly_rows, precision=lax.Precision.HIGHEST
        )
        cross = jnp.einsum("kn,n->k", scaled_anomaly, innov, precision=lax.Precision.HIGHEST)
        misfit = jnp.sum(wt * innov * innov)
        extra = jnp.stack([misfit, jnp.sum(live[group])])
        return (gram_product, cross, extra)

    def regroup(state):
        return state.reshape(members, nmem, piece)

    all_index = lax.all_gather(obs_index, "mem", axis=1, tiled=True)
    local_hx = jnp.stack(
        [observe(state_a, all_index[0], nmem * nblk), observe(state_b, all_index[1], nmem * nblk)]
    ).astype(jnp.bfloat16)
    moved_hx = lax.all_to_all(
        local_hx.reshape(2, members, nmem, width), "mem", split_axis=2, concat_axis=1, tiled=True
    )
    hx_all = moved_hx.reshape(2, everyone, width).astype(jnp.float32)
    first = statistics(hx_all[0], 0)
    second = statistics(hx_all[1], 1)
    gram_product, cross, extra = lax.psum(
        (first[0] + second[0], first[1] + second[1], first[2] + second[2]), ("mem", "col")
    )
    moved_a, moved_b = (
        lax.all_to_all(regroup(state_a), "mem", split_axis=1, concat_axis=0, tiled=True),
        lax.all_to_all(regroup(state_b), "mem", split_axis=1, concat_axis=0, tiled=True),
    )
    columns = [moved_a.reshape(everyone, piece), moved_b.reshape(everyone, piece)]
    misfit = extra[0]
    total = extra[1]
    transform = make_transform(gram_product, cross, misfit, total)
    wb = transform.astype(jnp.bfloat16)
    column_total = jnp.sum(wb.astype(jnp.float32), axis=0)
    ones = jnp.ones((everyone,), jnp.bfloat16)

    def analyse(cols):
        xmean = jnp.dot(ones, cols, preferred_element_type=jnp.float32) / everyone
        mixed = jnp.dot(wb.T, cols, preferred_element_type=jnp.float32)
        return (mixed + xmean[None, :] * (1.0 - column_total)[:, None]).astype(jnp.bfloat16)

    return (analyse(columns[0]), analyse(columns[1]), transform)


def solution(mesh):
    return jax.shard_map(
        shards,
        mesh=mesh,
        in_specs=(
            P("mem", "col"),
            P("mem", "col"),
            P(None, ("col", "mem"), None),
            P(None, ("col", "mem")),
            P(None, ("col", "mem"), None),
            P(None, ("col", "mem"), None),
        ),
        out_specs=(P(None, ("col", "mem")), P(None, ("col", "mem")), P()),
        check_vma=False,
    )
```

profile of v0, /device:TPU:0, one launch (start us, length us, event | category | flops | bytes accessed | tf_op | source)
XLA Modules:
  0.0 192.1 jit_solution(10022677384199641888)
XLA Ops:
  0.6 5.8 %all_gather.3 = s32[2,512,16]{1,2,0:T(8,128)S(1)} all-gather(s32[2,256,16]{1,2,0:T(8,128)} %param.10), channel_id=1, replica_groups=mesh['mem'=2,'col'=16] {'mem'}, dimensions={1}, use_global_device_ids=true | all-gather | bytes 98304 | tf_op jit(solution)/shard_map/all_gather | solution.py:84
  6.7 4.6 %fusion.16 = bf16[512,16,32]{2,1,0:T(8,128)(2,1)S(1)} fusion(s32[512,16]{1,0:T(8,128)S(1)} %copy.40, bf16[32,65536]{1,0:T(8,128)(2,1)} %param.9), kind=kOutput, calls=%fused_computation.23 | convolution fusion | flops 68419584 | bytes 4751360 | tf_op jit(solution)/shard_map/kbc,bsc->kbs/dot_general | solution.py:59
  11.3 0.8 copy.43
  12.1 4.6 %fusion.13 = bf16[512,16,32]{2,1,0:T(8,128)(2,1)S(1)} fusion(s32[512,16]{1,0:T(8,128)S(1)} %copy.38, bf16[32,65536]{1,0:T(8,128)(2,1)} %param.8), kind=kOutput, calls=%fused_computation.22 | convolution fusion | flops 68419584 | bytes 4751360 | tf_op jit(solution)/shard_map/kbc,bsc->kbs/dot_general | solution.py:59
  16.7 0.8 copy.42
  17.5 1.1 pad_maximum_fusion
  18.6 3.6 %all-to-all-start = ((bf16[2,32,2,4096]{3,1,0,2:T(8,128)(2,1)}), bf16[2,32,2,4096]{3,1,0,2:T(8,128)(2,1)S(1)}, u32[]{:S(2)}, u32[]{:S(2)}) async-start(bf16[2,32,2,4096]{3,1,0,2:T(8,128)(2,1)} %pad_maximum_fusion), calls=%async_computation | async-start | bytes 2097152 | tf_op jit(solution)/shard_map/all_to_all | solution.py:88
  23.2 0.7 slice_reduce_fusion
  24.2 4.6 %copy.70 = bf16[4,2,8,32768]{3,2,0,1:T(8,128)(2,1)} copy(bf16[4,2,8,32768]{3,2,1,0:T(8,128)(2,1)} %bitcast.125) | data formatting | bytes 8388608 | tf_op jit(solution)/shard_map/reshape | solution.py:82
  28.8 2.3 %copy.71 = bf16[4,2,8,32768]{3,2,0,1:T(8,128)(2,1)} copy(bf16[4,2,8,32768]{3,2,1,0:T(8,128)(2,1)S(1)} %bitcast.126) | data formatting | bytes 8388608 | tf_op jit(solution)/shard_map/reshape | solution.py:82
  31.2 4.0 %all-to-all-done = bf16[2,32,2,4096]{3,1,0,2:T(8,128)(2,1)S(1)} async-done(((bf16[2,32,2,4096]{3,1,0,2:T(8,128)(2,1)}), bf16[2,32,2,4096]{3,1,0,2:T(8,128)(2,1)S(1)}, u32[]{:S(2)}, u32[]{:S(2)}) %all-to-all-start) | async-done | bytes 1048608 | tf_op jit(solution)/shard_map/all_to_all | solution.py:88
  35.1 5.6 %all-to-all-start.2 = ((bf16[32,2,32768]{2,0,1:T(8,128)(2,1)}), bf16[32,2,32768]{2,0,1:T(8,128)(2,1)}, u32[]{:S(2)}, u32[]{:S(2)}) async-start(bf16[32,2,32768]{2,0,1:T(8,128)(2,1)} %bitcast.124), calls=%async_computation.2 | async-start | bytes 8388608 | tf_op jit(solution)/shard_map/all_to_all | solution.py:99
  41.0 0.3 slice_reduce_fusion.2
  41.3 0.6 fusion.38
  42.1 0.7 fusion.39
  43.0 2.6 %maximum_add_fusion = f32[2]{0:T(128)S(1)} fusion(f32[1]{0:T(128)} %bitcast.10, f32[1]{0:T(128)} %bitcast.9, f32[1]{0:T(128)} %bitcast.14, f32[1]{0:T(128)} %bitcast.13), kind=kLoop, calls=%fused_computation.71 | loop fusion | flops 6 | bytes 24 | tf_op jit(solution)/shard_map/add | solution.py:95
  45.8 0.9 convolution_bitcast_fusion.1
  46.7 1.0 fusion.19
  47.7 1.0 fusion.25
  48.7 1.0 convolution_add_fusion.2
  49.7 71.5 %all-reduce = (f32[64,64]{1,0:T(8,128)S(1)}, f32[2]{0:T(128)S(1)}, f32[64]{0:T(128)S(1)}) all-reduce(f32[64,64]{1,0:T(8,128)S(1)} %convolution_add_fusion.2, f32[2]{0:T(128)S(1)} %maximum_add_fusion, f32[64]{0:T(128)S(1)} %fusion.19), channel_id=1, replica_groups=mesh['mem'=2,'col'=16] {'mem','col'}, use_global_device_ids=true, to_apply=%region_7.0 | all-reduce | flops 4162 | bytes 33296 | tf_op jit(solution)/shard_map/psum | solution.py:94
  121.2 0.6 fusion.53
  123.1 0.6 select_reduce_fusion
  124.4 0.6 multiply_reduce_fusion
  125.8 5.8 %all-to-all-start.1 = ((bf16[32,2,32768]{2,0,1:T(8,128)(2,1)}), bf16[32,2,32768]{2,0,1:T(8,128)(2,1)}, u32[]{:S(2)}, u32[]{:S(2)}) async-start(bf16[32,2,32768]{2,0,1:T(8,128)(2,1)} %bitcast.123), calls=%async_computation.1 | async-start | bytes 8388608 | tf_op jit(solution)/shard_map/all_to_all | solution.py:98
  131.6 15.5 %while.13 = (s32[]{:T(128)}, f32[64,64]{0,1:T(8,128)S(1)}, f32[64,64]{1,0:T(8,128)S(1)}, s32[]{:T(128)}) while((s32[]{:T(128)}, f32[64,64]{0,1:T(8,128)S(1)}, f32[64,64]{1,0:T(8,128)S(1)}, s32[]{:T(128)}) %tuple.41), condition=%wide.region_11.12_spmd.clone, body=%wide.region_10.11_spmd.clone.sunk | while | flops 9453570 | bytes 213045 | solution.py:21
  132.0 0.2 convolution_bitcast_fusion.5
  147.5 2.8 %fusion.42 = f32[1,32768]{1,0:T(1,128)S(1)} fusion(bf16[64,32768]{1,0:T(8,128)(2,1)} %bitcast.35), kind=kOutput, calls=%fused_computation.74 | convolution fusion | flops 4194304 | bytes 4325376 | tf_op jit(solution)/shard_map/dot_general | solution.py:110
  150.4 27.9 %all-to-all-done.1 = bf16[32,2,32768]{2,0,1:T(8,128)(2,1)} async-done(((bf16[32,2,32768]{2,0,1:T(8,128)(2,1)}), bf16[32,2,32768]{2,0,1:T(8,128)(2,1)}, u32[]{:S(2)}, u32[]{:S(2)}) %all-to-all-start.1) | async-done | bytes 4194336 | tf_op jit(solution)/shard_map/all_to_all | solution.py:98
  178.3 2.8 %fusion.44 = f32[1,32768]{1,0:T(1,128)S(1)} fusion(bf16[64,32768]{1,0:T(8,128)(2,1)} %bitcast.29), kind=kOutput, calls=%fused_computation.76 | convolution fusion | flops 4194304 | bytes 4325376 | tf_op jit(solution)/shard_map/dot_general | solution.py:110
  181.1 5.5 %fusion.4 = bf16[64,32768]{1,0:T(8,128)(2,1)} fusion(bf16[64,32768]{1,0:T(8,128)(2,1)} %bitcast.35, f32[32768]{0:T(1024)S(1)} %broadcast_multiply_fusion, f32[64]{0:T(128)S(1)} %broadcast_subtract_fusion, f32[64,64]{1,0:T(8,128)S(1)} %get-tuple-element.60), kind=kOutput, calls=%fused_computation.8 | convolution fusion | flops 274731008 | bytes 8536320 | tf_op jit(solution)/shard_map/dot_general | solution.py:111
  186.6 5.5 %fusion.3 = bf16[64,32768]{1,0:T(8,128)(2,1)} fusion(bf16[64,32768]{1,0:T(8,128)(2,1)} %bitcast.29, f32[64]{0:T(128)S(1)} %broadcast_subtract_fusion, f32[32768]{0:T(1024)S(1)} %broadcast_multiply_fusion.1, f32[64,64]{1,0:T(8,128)S(1)} %get-tuple-element.60), kind=kOutput, calls=%fused_computation.7 | convolution fusion | flops 274731008 | bytes 8536320 | tf_op jit(solution)/shard_map/dot_general | solution.py:111
  (164 shorter events, 16.9 us)
Async XLA Ops:
  16.6 5.5 %copy-start.3 = (f32[2,256,16]{1,2,0:T(8,128)S(1)}, f32[2,256,16]{1,2,0:T(8,128)}, u32[]{:S(2)}) copy-start(f32[2,256,16]{1,2,0:T(8,128)} %param.12) | copy-start | bytes 98308
  16.7 6.1 %copy-start.2 = (f32[2,256,16]{1,2,0:T(8,128)S(1)}, f32[2,256,16]{1,2,0:T(8,128)}, u32[]{:S(2)}) copy-start(f32[2,256,16]{1,2,0:T(8,128)} %param.13) | copy-start | bytes 98308
  16.7 6.4 %copy-start.4 = (s32[2,256]{1,0:T(2,128)S(1)}, s32[2,256]{1,0:T(2,128)}, u32[]{:S(2)}) copy-start(s32[2,256]{1,0:T(2,128)} %param.11) | copy-start | bytes 6148
  18.6 16.6 %all-to-all-start = ((bf16[2,32,2,4096]{3,1,0,2:T(8,128)(2,1)}), bf16[2,32,2,4096]{3,1,0,2:T(8,128)(2,1)S(1)}, u32[]{:S(2)}, u32[]{:S(2)}) async-start(bf16[2,32,2,4096]{3,1,0,2:T(8,128)(2,1)} %pad_maximum_fusion), calls=%async_computation | async-start | bytes 2097152 | tf_op jit(solution)/shard_map/all_to_all | solution.py:88
  24.1 4.6 %copy-start = (bf16[32,65536]{1,0:T(8,128)(2,1)S(1)}, bf16[32,65536]{1,0:T(8,128)(2,1)}, u32[]{:S(2)}) copy-start(bf16[32,65536]{1,0:T(8,128)(2,1)} %param.8) | copy-start | bytes 12582916
  35.1 90.6 %all-to-all-start.2 = ((bf16[32,2,32768]{2,0,1:T(8,128)(2,1)}), bf16[32,2,32768]{2,0,1:T(8,128)(2,1)}, u32[]{:S(2)}, u32[]{:S(2)}) async-start(bf16[32,2,32768]{2,0,1:T(8,128)(2,1)} %bitcast.124), calls=%async_computation.2 | async-start | bytes 8388608 | tf_op jit(solution)/shard_map/all_to_all | solution.py:99
  125.8 52.5 %all-to-all-start.1 = ((bf16[32,2,32768]{2,0,1:T(8,128)(2,1)}), bf16[32,2,32768]{2,0,1:T(8,128)(2,1)}, u32[]{:S(2)}, u32[]{:S(2)}) async-start(bf16[32,2,32768]{2,0,1:T(8,128)(2,1)} %bitcast.123), calls=%async_computation.1 | async-start | bytes 8388608 | tf_op jit(solution)/shard_map/all_to_all | solution.py:98
  147.5 39.1 %copy-start.1 = (f32[64,64]{1,0:T(8,128)}, f32[64,64]{1,0:T(8,128)S(1)}, u32[]{:S(2)}) copy-start(f32[64,64]{1,0:T(8,128)S(1)} %get-tuple-element.60) | copy-start | bytes 49156
where the time goes:
time: 193 us; the launch traced here: 192 us
  blocking collectives  77.2 us (40%)
  matrix products  44 us (23%)
  waiting for transfers between devices  31.8 us (16%)
  starting transfers between devices  15 us (8%)
  local copies, waits for them, and re-layouts  11.2 us (6%)
  other arithmetic  7.89 us (4%)
  between operations  3.67 us (2%)
    psum x1, blocking collectives, shards(): lax.psum((first[0] + second[0], first[1] + second[1], first[2] + second[2...  71.5 us
    all_to_all x1, waiting for transfers between devices, shards(): lax.all_to_all(regroup(state_a), 'mem', split_axis=1, concat_axis=0, tile...  27.9 us
    dot_general x2, matrix products, analyse(): mixed = jnp.dot(wb.T, cols, preferred_element_type=jnp.float32)  11 us
    dot_general x2, matrix products, observe(): jnp.einsum('kbc,bsc->kbs', columns.reshape(columns.shape[0], blocks, 128)...  9.13 us
    reshape x2, local copies, waits for them, and re-layouts, regroup(): return state.reshape(members, nmem, piece)  6.94 us
    all_gather x1, blocking collectives, shards(): all_index = lax.all_gather(obs_index, 'mem', axis=1, tiled=True)  5.79 us
    all_to_all x1, starting transfers between devices, shards(): lax.all_to_all(regroup(state_a), 'mem', split_axis=1, concat_axis=0, tile...  5.79 us
    dot_general x2, matrix products, analyse(): xmean = jnp.dot(ones, cols, preferred_element_type=jnp.float32) / everyone  5.68 us
  transfers between devices with their start and end apart: 3, of which 2 were waited for; matrix products, arithmetic and copies ran while one was open for 19% of the time, Pallas kernels for 0%

commit v1 on v0

v1 whole, which is shorter than its diff:
```python
import functools

import jax
import jax.numpy as jnp
from jax import lax
from jax.experimental import pallas as pl
from jax.experimental.pallas import tpu as pltpu
from jax.sharding import PartitionSpec as P


ITERS = 24
LANES = 128

MESSAGES = (
    (0, 0, 1),
    (0, 1, 3),
    (0, 3, 5),
    (0, 5, 8),
    (1, 0, 4),
    (1, 4, 6),
    (1, 6, 7),
    (1, 7, 8),
)


def split(x):
    high = x.astype(jnp.bfloat16)
    rest = x - high.astype(jnp.float32)
    middle = rest.astype(jnp.bfloat16)
    return high, middle, (rest - middle.astype(jnp.float32)).astype(jnp.bfloat16)


def terms_dot(a, b):
    rows = a[0].shape[0]
    stacked = jnp.concatenate(a, axis=0)
    by_high = jnp.dot(stacked, b[0], preferred_element_type=jnp.float32)
    by_middle = jnp.dot(stacked[: 2 * rows], b[1], preferred_element_type=jnp.float32)
    by_low = jnp.dot(a[0], b[2], preferred_element_type=jnp.float32)
    second = by_high[rows : 2 * rows] + by_middle[:rows]
    third = by_high[2 * rows :] + by_middle[rows:] + by_low
    return by_high[:rows] + (second + third)


def gather_kernel(slots, base_ref, index_ref, a_ref, b_ref, out_ref):
    per = LANES // slots
    step = pl.program_id(0)
    width = out_ref.shape[2]
    rows = a_ref.shape[0]
    place = lax.broadcasted_iota(jnp.int32, (rows, LANES), 1) // slots
    for group, ref in enumerate((a_ref, b_ref)):
        for q in range(width // LANES):
            row = index_ref[group, pl.ds(step * (width // LANES) + q, 1), :]
            wanted = jnp.broadcast_to(row, (rows, LANES))
            acc = jnp.zeros((rows, LANES), jnp.float32)
            for j in range(per):
                start = (q * per + j) * LANES
                block = ref[:, start : start + LANES].astype(jnp.float32)
                taken = jnp.take_along_axis(block, wanted, axis=1, mode="promise_in_bounds")
                acc = jnp.where(place == j, taken, acc)
            out_ref[group, :, q * LANES : (q + 1) * LANES] = acc.astype(out_ref.dtype)


def gather(state_a, state_b, index, base, slots, piece):
    rows = state_a.shape[0]
    width = min(4096, piece)
    steps = piece // width
    observations = piece // LANES * slots
    state_spec = pl.BlockSpec((rows, width), lambda i, base: (0, base[0] * steps + i))
    return pl.pallas_call(
        functools.partial(gather_kernel, slots),
        out_shape=jax.ShapeDtypeStruct((2, rows, observations), jnp.bfloat16),
        grid_spec=pltpu.PrefetchScalarGridSpec(
            num_scalar_prefetch=1,
            grid=(steps,),
            in_specs=[
                pl.BlockSpec(index.shape, lambda i, base: (0, 0, 0)),
                state_spec,
                state_spec,
            ],
            out_specs=pl.BlockSpec((2, rows, observations // steps), lambda i, base: (0, 0, i)),
        ),
        compiler_params=pltpu.CompilerParams(dimension_semantics=("arbitrary",)),
        name="gather",
    )(base, index, state_a, state_b)


def stats_kernel(parts, me_ref, *refs):
    hx_refs = refs[:parts]
    value_ref, weight_ref, live_ref, out_ref, all_ref = refs[parts:]
    members = hx_refs[0].shape[1]
    everyone = members * parts
    me = me_ref[0]
    for j in range(parts):
        at = pl.multiple_of(lax.rem(me + j, parts) * members, members)
        all_ref[pl.ds(at, members), :] = hx_refs[j][0].astype(jnp.float32)
    hx = all_ref[...]
    hmean = jnp.sum(hx, axis=0, keepdims=True) / everyone
    anomaly = hx - hmean
    innov = value_ref[0] - hmean
    wt = weight_ref[0]
    scaled = anomaly * wt
    product = lax.dot_general(
        jnp.concatenate(split(scaled), axis=0),
        jnp.concatenate(split(anomaly), axis=0),
        (((1,), (1,)), ((), ())),
        preferred_element_type=jnp.float32,
    )

    def term(i, j):
        rows = product[i * everyone : (i + 1) * everyone]
        return rows[:, j * everyone : (j + 1) * everyone]

    gram = term(0, 0) + (term(0, 1) + term(1, 0) + (term(0, 2) + term(2, 0) + term(1, 1)))
    cross = jnp.sum(scaled * innov, axis=1, keepdims=True)
    misfit = jnp.sum(wt * innov * innov, axis=1, keepdims=True)
    total = jnp.sum(live_ref[0], axis=1, keepdims=True)
    lane = lax.broadcasted_iota(jnp.int32, (everyone, LANES - everyone), 1)
    side = jnp.where(lane == 0, cross, jnp.where(lane == 1, misfit, jnp.where(lane == 2, total, 0.0)))
    new = jnp.concatenate([gram, side], axis=1)
    first = (pl.program_id(0) == 0) & (pl.program_id(1) == 0)

    @pl.when(first)
    def _():
        out_ref[...] = new

    @pl.when(jnp.logical_not(first))
    def _():
        out_ref[...] += new


def statistics(parts, value, weight, live, me):
    members, observations = parts[0].shape[1:]
    everyone = members * len(parts)
    width = min(1024, observations)
    hx_spec = pl.BlockSpec((1, members, width), lambda g, i, me: (g, 0, i))
    row_spec = pl.BlockSpec((1, 1, width), lambda g, i, me: (g, 0, i))
    return pl.pallas_call(
        functools.partial(stats_kernel, len(parts)),
        out_shape=jax.ShapeDtypeStruct((everyone, LANES), jnp.float32),
        grid_spec=pltpu.PrefetchScalarGridSpec(
            num_scalar_prefetch=1,
            grid=(2, observations // width),
            in_specs=[hx_spec] * len(parts) + [row_spec] * 3,
            out_specs=pl.BlockSpec((everyone, LANES), lambda g, i, me: (0, 0)),
            scratch_shapes=[pltpu.VMEM((everyone, width), jnp.float32)],
        ),
        compiler_params=pltpu.CompilerParams(dimension_semantics=("arbitrary", "arbitrary")),
        name="statistics",
    )(me, *parts, value, weight, live)


def transform_kernel(members, me_ref, stats_ref, transform_ref, mixer_ref, rest_ref):
    stats = stats_ref[...]
    everyone = stats.shape[0]
    gram = stats[:, :everyone]
    cross = stats[:, everyone : everyone + 1]
    misfit = stats[0:1, everyone + 1 : everyone + 2]
    total = stats[0:1, everyone + 2 : everyone + 3]
    dof = everyone - 1.0
    row = lax.broadcasted_iota(jnp.int32, (everyone, everyone), 0)
    col = lax.broadcasted_iota(jnp.int32, (everyone, everyone), 1)
    eye = (row == col).astype(jnp.float32)
    scl = dof / total
    gs = scl * gram
    bs = scl * cross
    qval = scl * misfit

    def whole_sum(x):
        return jnp.sum(jnp.sum(x, axis=1, keepdims=True), axis=0, keepdims=True)

    tval = whole_sum(gs * eye)
    rho = (1.0 + qval / dof) / (1.0 + tval / dof)
    amat = dof / rho * eye + gs
    scale = jnp.sqrt(whole_sum(amat * amat))

    def forward_step(_, carry):
        yn, zn = (split(x) for x in carry)
        tm = split(1.5 * eye - 0.5 * terms_dot(zn, yn))
        return terms_dot(yn, tm), terms_dot(tm, zn)

    _, zn = lax.fori_loop(0, ITERS, forward_step, (amat / scale, eye))
    parts = split(zn)
    pmat = terms_dot(parts, parts) / scale
    wide = jnp.broadcast_to(bs, (everyone, LANES))
    wbar = terms_dot(split(pmat), split(wide))[:, 0:1]
    transform = jnp.sqrt(dof) * zn / jnp.sqrt(scale) + wbar
    transform_ref[...] = transform
    held = pltpu.roll(transform, lax.rem(everyone - me_ref[0] * members, everyone), 0)
    mixer = held.T.astype(jnp.bfloat16)
    column_total = jnp.sum(mixer.astype(jnp.float32), axis=1, keepdims=True)
    extra = mixer_ref.shape[0] - everyone
    mixer_ref[...] = jnp.concatenate([mixer, jnp.ones((extra, everyone), jnp.bfloat16)], axis=0)
    rest_ref[...] = jnp.broadcast_to((1.0 - column_total) / everyone, rest_ref.shape)


def make_transform(stats, members, me):
    everyone = stats.shape[0]
    return pl.pallas_call(
        functools.partial(transform_kernel, members),
        out_shape=(
            jax.ShapeDtypeStruct((everyone, everyone), jnp.float32),
            jax.ShapeDtypeStruct((everyone + 16, everyone), jnp.bfloat16),
            jax.ShapeDtypeStruct((everyone, LANES), jnp.float32),
        ),
        in_specs=[pl.BlockSpec(memory_space=pltpu.SMEM), pl.BlockSpec(memory_space=pltpu.VMEM)],
        out_specs=(pl.BlockSpec(memory_space=pltpu.VMEM),) * 3,
        name="transform",
    )(me, stats)


def analysis_kernel(parts, aliased, base_ref, mixer_ref, rest_ref, *refs):
    cols_refs = refs[:parts]
    out_ref = refs[parts + aliased]
    everyone = out_ref.shape[0]
    members = cols_refs[0].shape[0]
    if members % 16 == 0:
        cols = jnp.concatenate([ref[...] for ref in cols_refs], axis=0)
        mixed = jnp.dot(mixer_ref[...], cols, preferred_element_type=jnp.float32)
    else:
        cols = jnp.concatenate([ref[...].astype(jnp.float32) for ref in cols_refs], axis=0)
        mixed = jnp.dot(
            mixer_ref[...], cols.astype(jnp.bfloat16), preferred_element_type=jnp.float32
        )
    rest = rest_ref[:, 0:1]
    out = mixed[:everyone] + rest * mixed[everyone : everyone + 1]
    out_ref[...] = out.astype(out_ref.dtype)


def analyse(out, state, received, mixer, rest, base, first, piece):
    members, length = received[0].shape
    everyone = rest.shape[0]
    width = min(2048, length)
    steps = length // width
    skip = first // width
    whole = piece // width
    parts = len(received) + 1
    aliased = int(out is not None)
    in_specs = [
        pl.BlockSpec(mixer.shape, lambda i, base: (0, 0)),
        pl.BlockSpec(rest.shape, lambda i, base: (0, 0)),
        pl.BlockSpec((members, width), lambda i, base: (0, base[0] * whole + skip + i)),
    ] + [pl.BlockSpec((members, width), lambda i, base: (0, i))] * len(received)
    operands = [base, mixer, rest, state, *received]
    aliases = {}
    if aliased:
        in_specs.append(pl.BlockSpec(memory_space=pl.ANY))
        aliases = {len(operands): 0}
        operands.append(out)
    return pl.pallas_call(
        functools.partial(analysis_kernel, parts, aliased),
        out_shape=jax.ShapeDtypeStruct((everyone, piece), jnp.bfloat16),
        grid_spec=pltpu.PrefetchScalarGridSpec(
            num_scalar_prefetch=1,
            grid=(steps,),
            in_specs=in_specs,
            out_specs=pl.BlockSpec((everyone, width), lambda i, base: (0, skip + i)),
        ),
        input_output_aliases=aliases,
        compiler_params=pltpu.CompilerParams(dimension_semantics=("arbitrary",)),
        name="analysis",
    )(*operands)


def shards(state_a, state_b, obs_index, observation_count, obs_value, obs_weight):
    states = (state_a, state_b)
    members = state_a.shape[0]
    nmem = lax.axis_size("mem")
    ncol = lax.axis_size("col")
    piece = state_a.shape[1] // nmem
    nblk = obs_index.shape[1]
    slots = obs_index.shape[2]
    observations = nblk * slots
    unit = piece // 8
    me = lax.axis_index("mem")
    me_ref = me[None].astype(jnp.int32)
    shifts = range(1, nmem)

    def to_lower(array, shift):
        return lax.ppermute(array, "mem", [(i, (i - shift) % nmem) for i in range(nmem)])

    def to_upper(array, shift):
        return lax.ppermute(array, "mem", [(i, (i + shift) % nmem) for i in range(nmem)])

    def cut(message, source):
        group, lo, hi = message
        return [
            lax.dynamic_slice(
                source[group],
                (0, lax.rem(me + nmem - shift, nmem) * piece + lo * unit),
                (members, (hi - lo) * unit),
            )
            for shift in shifts
        ]

    index = obs_index.reshape(2, observations // LANES, LANES)
    others_index = [to_upper(index, shift) for shift in shifts]

    own_hx = gather(state_a, state_b, index, me_ref, slots, piece)
    sent_hx = [
        gather(state_a, state_b, idx, lax.rem(me_ref + nmem - shift, nmem), slots, piece)
        for idx, shift in zip(others_index, shifts)
    ]
    got_hx = [to_lower(x, shift) for x, shift in zip(sent_hx, shifts)]

    live = (
        lax.broadcasted_iota(jnp.int32, (2, nblk, slots), 2) < observation_count[:, :, None]
    ).astype(jnp.float32)
    weight = (live * obs_weight).reshape(2, 1, observations)
    live = live.reshape(2, 1, observations)
    value = obs_value.reshape(2, 1, observations)
    stats = statistics([own_hx, *got_hx], value, weight, live, me_ref)

    received = []
    for i, message in enumerate(MESSAGES):
        if i < len(MESSAGES) - 1:
            pieces = cut(message, states)
        else:
            pieces = cut(message, lax.optimization_barrier((*states, stats)))
        received.append([to_lower(x, shift) for x, shift in zip(pieces, shifts)])

    def all_sum(x, axis, size):
        step = 1
        while step < size:
            x = x + lax.ppermute(x, axis, [(i, i ^ step) for i in range(size)])
            step *= 2
        return x

    stats = all_sum(all_sum(stats, "mem", nmem), "col", ncol)
    transform, mixer, rest = make_transform(stats, members, me_ref)

    outs = [None, None]
    for (group, lo, hi), pieces in zip(MESSAGES, received):
        outs[group] = analyse(
            outs[group], states[group], pieces, mixer, rest, me_ref, lo * unit, piece
        )
    return (outs[0], outs[1], transform)


def solution(mesh):
    return jax.shard_map(
        shards,
        mesh=mesh,
        in_specs=(
            P("mem", "col"),
            P("mem", "col"),
            P(None, ("col", "mem"), None),
            P(None, ("col", "mem")),
            P(None, ("col", "mem"), None),
            P(None, ("col", "mem"), None),
        ),
        out_specs=(P(None, ("col", "mem")), P(None, ("col", "mem")), P()),
        check_vma=False,
    )
```

time: 193 us -> 132 us (0.68)
  blocking collectives: 77.2 us -> 0 us
  Pallas kernels: 0 us -> 60.6 us
  matrix products: 44 us -> 0 us
  local copies, waits for them, and re-layouts: 11.2 us -> 19 us
  other arithmetic: 7.89 us -> 2.82 us
  starting transfers between devices: 15 us -> 19.2 us
  waiting for transfers between devices: 31.8 us -> 28.4 us
  between operations: 3.67 us -> 0.8 us
    psum x1 -> x0, blocking collectives: 71.5 us -> none  [shards(): lax.psum((first[0] + second[0], first[1] + second[1], first[2] + second[2...]
    pallas_call x0 -> x12, Pallas kernels: none -> 60.6 us  [the longest x8 29.8 us: analyse(): pl.pallas_call(functools.partial(analysis_kernel, parts, aliased), out_sh...]
    dot_general x84 -> x0, matrix products: 44 us -> none  [the longest x2 11 us: analyse(): mixed = jnp.dot(wb.T, cols, preferred_element_type=jnp.float32)]
    all_to_all x3 -> x0, waiting for transfers between devices: 31.8 us -> none  [the longest x1 27.9 us: shards(): lax.all_to_all(regroup(state_a), 'mem', split_axis=1, concat_axis=0, tile...]
    ppermute x0 -> x15, waiting for transfers between devices: none -> 28.4 us  [the longest x9 27 us: to_lower(): lax.ppermute(array, 'mem', [(i, (i - shift) % nmem) for i in range(nmem)])]
    ppermute x0 -> x15, starting transfers between devices: none -> 19.2 us  [the longest x9 8.56 us: to_lower(): lax.ppermute(array, 'mem', [(i, (i - shift) % nmem) for i in range(nmem)])]
    all_to_all x3 -> x0, starting transfers between devices: 15 us -> none  [the longest x1 5.79 us: shards(): lax.all_to_all(regroup(state_a), 'mem', split_axis=1, concat_axis=0, tile...]
    dynamic_slice x0 -> x7, local copies, waits for them, and re-layouts: none -> 12.5 us  [cut(): lax.dynamic_slice(source[group], (0, lax.rem(me + nmem - shift, nmem) * p...]
  transfers between devices with their start and end apart: 3 -> 15, of which waited for: 2 -> 4; matrix products, arithmetic and copies ran while one was open for 19% -> 13% of each run, Pallas kernels for 0% -> 45%
where the time goes in v1:
time: 132 us; the launch traced here: 131 us
  Pallas kernels  60.6 us (46%)
  waiting for transfers between devices  28.4 us (22%)
  starting transfers between devices  19.2 us (15%)
  local copies, waits for them, and re-layouts  19 us (14%)
  other arithmetic  2.82 us (2%)
    pallas_call x8, Pallas kernels, analyse(): pl.pallas_call(functools.partial(analysis_kernel, parts, aliased), out_sh...  29.8 us
    ppermute x9, waiting for transfers between devices, to_lower(): lax.ppermute(array, 'mem', [(i, (i - shift) % nmem) for i in range(nmem)])  27 us
    pallas_call x2, Pallas kernels, gather(): pl.pallas_call(functools.partial(gather_kernel, slots), out_shape=jax.Sha...  13 us
    dynamic_slice x7, local copies, waits for them, and re-layouts, cut(): lax.dynamic_slice(source[group], (0, lax.rem(me + nmem - shift, nmem) * p...  12.5 us
    pallas_call x1, Pallas kernels, make_transform(): pl.pallas_call(functools.partial(transform_kernel, members), out_shape=(j...  10.8 us
    ppermute x9, starting transfers between devices, to_lower(): lax.ppermute(array, 'mem', [(i, (i - shift) % nmem) for i in range(nmem)])  8.56 us
    ppermute x5, starting transfers between devices, all_sum(): x = x + lax.ppermute(x, axis, [(i, i ^ step) for i in range(size)])  7.6 us
    pallas_call x1, Pallas kernels, statistics(): pl.pallas_call(functools.partial(stats_kernel, len(parts)), out_shape=jax...  6.98 us
  transfers between devices with their start and end apart: 15, of which 4 were waited for; matrix products, arithmetic and copies ran while one was open for 13% of the time, Pallas kernels for 45%

profile of v1, /device:TPU:0, one launch (start us, length us, event | category | flops | bytes accessed | tf_op | source)
XLA Modules:
  0.0 130.8 jit_solution(12379284561864219541)
XLA Ops:
  1.7 3.0 %collective-permute-start = (s32[2,32,128]{2,1,0:T(8,128)S(1)}, s32[2,32,128]{2,1,0:T(8,128)S(1)}, u32[]{:S(2)}, u32[]{:S(2)}) collective-permute-start(s32[2,32,128]{2,1,0:T(8,128)S(1)} %reshape.56.index_ref), channel_id=1, source_target_pairs={{0,16},{16,0},{1,17},{17,1},{2,18},{18,2},{3,19},{19,3},{4,20},{20... | collective-permute-start | bytes 98312 | tf_op jit(solution)/shard_map/ppermute | solution.py:282
  4.7 2.1 %constant_dynamic-slice_fusion.7 = bf16[32,12288]{1,0:T(8,128)(2,1)} fusion(bf16[32,65536]{1,0:T(8,128)(2,1)} %refs_0_.11, s32[]{:T(128)S(6)} %select_n.22), kind=kLoop, calls=%fused_computation.10 | loop fusion | bytes 1572868 | tf_op jit(solution)/shard_map/dynamic_slice | solution.py:287
  7.6 6.5 %gather.2.refs_0_ = bf16[2,32,4096]{2,1,0:T(8,128)(2,1)} custom-call(s32[1]{0:T(128)} %bitcast.base_ref.me_ref, s32[2,32,128]{2,1,0:T(8,128)} %copy-done.4, bf16[32,65536]{1,0:T(8,128)(2,1)} %refs_0_.11, bf16[32,65536]{1,0:T(8,128)(2,1)} %refs_0_.15), custom_call_target="tpu_custom_call" | custom-call | tf_op jit(solution)/shard_map/gather/pallas_call | solution.py:69
  17.0 6.5 %gather.3 = bf16[2,32,4096]{2,1,0:T(8,128)(2,1)} custom-call(s32[1]{0:T(128)S(6)} %rem.38.base_ref, s32[2,32,128]{2,1,0:T(8,128)} %copy-done.5, bf16[32,65536]{1,0:T(8,128)(2,1)} %refs_0_.11, bf16[32,65536]{1,0:T(8,128)(2,1)} %refs_0_.15), custom_call_target="tpu_custom_call" | custom-call | tf_op jit(solution)/shard_map/gather/pallas_call | solution.py:69
  23.5 2.0 %collective-permute-start.1 = (bf16[2,32,4096]{2,1,0:T(8,128)(2,1)}, bf16[2,32,4096]{2,1,0:T(8,128)(2,1)S(1)}, u32[]{:S(2)}, u32[]{:S(2)}) collective-permute-start(bf16[2,32,4096]{2,1,0:T(8,128)(2,1)} %gather.3), channel_id=1, source_target_pairs={{0,16},{16,0},{1,17},{17,1},{2,18},{18,2},{3,19},{19,3},{4,20},{20... | collective-permute-start | bytes 1572872 | tf_op jit(solution)/shard_map/ppermute | solution.py:279
  26.1 11.1 %collective-permute-done.1.refs_1_ = bf16[2,32,4096]{2,1,0:T(8,128)(2,1)S(1)} collective-permute-done((bf16[2,32,4096]{2,1,0:T(8,128)(2,1)}, bf16[2,32,4096]{2,1,0:T(8,128)(2,1)S(1)}, u32[]{:S(2)}, u32[]{:S(2)}) %collective-permute-start.1) | collective-permute-done | bytes 524320 | tf_op jit(solution)/shard_map/ppermute | solution.py:279
  38.0 7.0 %statistics.1 = f32[64,128]{1,0:T(8,128)} custom-call(s32[1]{0:T(128)} %bitcast.base_ref.me_ref, bf16[2,32,4096]{2,1,0:T(8,128)(2,1)} %gather.2.refs_0_, bf16[2,32,4096]{2,1,0:T(8,128)(2,1)} %copy-done.3, f32[2,1,4096]{2,1,0:T(1,128)} %reshape.59.refs_2_, f32[2,1,4096]{2,1,0:T(1,128)} %reshape.60.refs_3_, f32[2,1,4096]{2,1,0:T(1,128)} %compare_convert_fusion.refs_4_), custom_call_target="tpu_custom_call" | custom-call | tf_op jit(solution)/shard_map/statistics/pallas_call | solution.py:137
  45.0 1.6 %collective-permute-start.2 = (f32[64,128]{1,0:T(8,128)}, f32[64,128]{1,0:T(8,128)S(1)}, u32[]{:S(2)}, u32[]{:S(2)}) collective-permute-start(f32[64,128]{1,0:T(8,128)} %statistics.1), channel_id=1, source_target_pairs={{0,16},{16,0},{1,17},{17,1},{2,18},{18,2},{3,19},{19,3},{4,20},{20... | collective-permute-start | bytes 98312 | tf_op jit(solution)/shard_map/ppermute | solution.py:324
  46.6 2.2 %constant_dynamic-slice_fusion.5 = (bf16[32,8192]{1,0:T(8,128)(2,1)}, bf16[32,8192]{1,0:T(8,128)(2,1)}) fusion(bf16[32,65536]{1,0:T(8,128)(2,1)} %refs_0_.11, s32[]{:T(128)S(6)} %select_n.24, s32[]{:T(128)S(6)} %select_n.23), kind=kLoop, calls=%fused_computation.8 | loop fusion | bytes 2097160 | tf_op jit(solution)/shard_map/dynamic_slice | solution.py:287
  49.3 1.6 %collective-permute-start.9 = (bf16[32,8192]{1,0:T(8,128)(2,1)}, bf16[32,8192]{1,0:T(8,128)(2,1)}, u32[]{:S(2)}, u32[]{:S(2)}) collective-permute-start(bf16[32,8192]{1,0:T(8,128)(2,1)} %get-tuple-element.11), channel_id=1, source_target_pairs={{0,16},{16,0},{1,17},{17,1},{2,18},{18,2},{3,19},{19,3},{4,20},{20... | collective-permute-start | bytes 1572872 | tf_op jit(solution)/shard_map/ppermute | solution.py:279
  51.6 1.7 %constant_dynamic-slice_fusion.4 = bf16[32,4096]{1,0:T(8,128)(2,1)} fusion(bf16[32,65536]{1,0:T(8,128)(2,1)} %refs_0_.11, s32[]{:T(128)S(6)} %select_n.25), kind=kLoop, calls=%fused_computation.7 | loop fusion | bytes 524292 | tf_op jit(solution)/shard_map/dynamic_slice | solution.py:287
  53.8 1.7 %collective-permute-start.4 = (f32[64,128]{1,0:T(8,128)S(1)}, f32[64,128]{1,0:T(8,128)S(1)}, u32[]{:S(2)}, u32[]{:S(2)}) collective-permute-start(f32[64,128]{1,0:T(8,128)S(1)} %add.83), channel_id=1, source_target_pairs={{0,2},{1,3},{2,0},{3,1},{4,6},{5,7},{6,4},{7,5},{8,10},{9,11},{10,... | collective-permute-start | bytes 98312 | tf_op jit(solution)/shard_map/ppermute | solution.py:324
  55.4 1.3 constant_dynamic-slice_fusion
  56.8 1.0 collective-permute-done.4
  57.8 1.7 %collective-permute-start.5 = (f32[64,128]{1,0:T(8,128)S(1)}, f32[64,128]{1,0:T(8,128)S(1)}, u32[]{:S(2)}, u32[]{:S(2)}) collective-permute-start(f32[64,128]{1,0:T(8,128)S(1)} %add.84), channel_id=1, source_target_pairs={{0,4},{1,5},{2,6},{3,7},{4,0},{5,1},{6,2},{7,3},{8,12},{9,13},{10,... | collective-permute-start | bytes 98312 | tf_op jit(solution)/shard_map/ppermute | solution.py:324
  59.4 1.9 %constant_dynamic-slice_fusion.1 = bf16[32,8192]{1,0:T(8,128)(2,1)} fusion(bf16[32,65536]{1,0:T(8,128)(2,1)} %refs_0_.15, s32[]{:T(128)S(6)} %select_n.28), kind=kLoop, calls=%fused_computation.4 | loop fusion | bytes 1048580 | tf_op jit(solution)/shard_map/dynamic_slice | solution.py:287
  61.7 1.6 %collective-permute-start.14 = (bf16[32,16384]{1,0:T(8,128)(2,1)S(1)}, bf16[32,16384]{1,0:T(8,128)(2,1)S(1)}, u32[]{:S(2)}, u32[]{:S(2)}) collective-permute-start(bf16[32,16384]{1,0:T(8,128)(2,1)S(1)} %constant_dynamic-slice_fusion), channel_id=1, source_target_pairs={{0,16},{16,0},{1,17},{17,1},{2,18},{18,2},{3,19},{19,3},{4,20},{20... | collective-permute-start | bytes 3145736 | tf_op jit(solution)/shard_map/ppermute | solution.py:279
  63.3 1.7 %constant_dynamic-slice_fusion.2 = bf16[32,4096]{1,0:T(8,128)(2,1)} fusion(bf16[32,65536]{1,0:T(8,128)(2,1)} %refs_0_.15, s32[]{:T(128)S(6)} %select_n.27), kind=kLoop, calls=%fused_computation.5 | loop fusion | bytes 524292 | tf_op jit(solution)/shard_map/dynamic_slice | solution.py:287
  64.9 15.9 %collective-permute-done.10.refs_1_ = bf16[32,4096]{1,0:T(8,128)(2,1)} collective-permute-done((bf16[32,4096]{1,0:T(8,128)(2,1)}, bf16[32,4096]{1,0:T(8,128)(2,1)}, u32[]{:S(2)}, u32[]{:S(2)}) %collective-permute-start.10) | collective-permute-done | bytes 262176 | tf_op jit(solution)/shard_map/ppermute | solution.py:279
  81.2 2.7 %collective-permute-start.6 = (f32[64,128]{1,0:T(8,128)S(1)}, f32[64,128]{1,0:T(8,128)S(1)}, u32[]{:S(2)}, u32[]{:S(2)}) collective-permute-start(f32[64,128]{1,0:T(8,128)S(1)} %add.85), channel_id=1, source_target_pairs={{0,8},{1,9},{2,10},{3,11},{4,12},{5,13},{6,14},{7,15},{8,0},{9,1},... | collective-permute-start | bytes 98312 | tf_op jit(solution)/shard_map/ppermute | solution.py:324
  83.9 1.7 %constant_dynamic-slice_fusion.3 = bf16[32,4096]{1,0:T(8,128)(2,1)} fusion(bf16[32,65536]{1,0:T(8,128)(2,1)} %refs_0_.15, s32[]{:T(128)S(6)} %select_n.26), kind=kLoop, calls=%fused_computation.6 | loop fusion | bytes 524292 | tf_op jit(solution)/shard_map/dynamic_slice | solution.py:287
  85.6 1.5 %collective-permute-start.12 = (bf16[32,4096]{1,0:T(8,128)(2,1)}, bf16[32,4096]{1,0:T(8,128)(2,1)}, u32[]{:S(2)}, u32[]{:S(2)}) collective-permute-start(bf16[32,4096]{1,0:T(8,128)(2,1)} %constant_dynamic-slice_fusion.2), channel_id=1, source_target_pairs={{0,16},{16,0},{1,17},{17,1},{2,18},{18,2},{3,19},{19,3},{4,20},{20... | collective-permute-start | bytes 786440 | tf_op jit(solution)/shard_map/ppermute | solution.py:279
  88.3 10.8 %transform.1 = (f32[64,64]{1,0:T(8,128)}, bf16[80,64]{1,0:T(8,128)(2,1)}, f32[64,128]{1,0:T(8,128)}) custom-call(s32[1]{0:T(128)} %bitcast.base_ref.me_ref, f32[64,128]{1,0:T(8,128)} %add.86.stats_ref), custom_call_target="tpu_custom_call" | custom-call | tf_op jit(solution)/shard_map/transform/pallas_call | solution.py:198
  99.0 2.2 %analysis.8.refs_2_ = bf16[64,32768]{1,0:T(8,128)(2,1)} custom-call(s32[1]{0:T(128)} %bitcast.base_ref.me_ref, bf16[80,64]{1,0:T(8,128)(2,1)} %get-tuple-element.7.mixer_ref, f32[64,128]{1,0:T(8,128)} %get-tuple-element.8.rest_ref, bf16[32,65536]{1,0:T(8,128)(2,1)} %refs_0_.11, bf16[32,4096]{1,0:T(8,128)(2,1)} %collective-permute-done.10.refs_1_), custom_call_target="tpu_custom_call" | custom-call | tf_op jit(solution)/shard_map/analysis/pallas_call | solution.py:249
  101.2 3.9 %analysis.9.refs_2_ = bf16[64,32768]{1,0:T(8,128)(2,1)} custom-call(s32[1]{0:T(128)} %bitcast.base_ref.me_ref, bf16[80,64]{1,0:T(8,128)(2,1)} %get-tuple-element.7.mixer_ref, f32[64,128]{1,0:T(8,128)} %get-tuple-element.8.rest_ref, bf16[32,65536]{1,0:T(8,128)(2,1)} %refs_0_.11, ...), custom_call_target="tpu_custom_call", output_to_operand_aliasing={{}: (5, {})} | custom-call | tf_op jit(solution)/shard_map/analysis/pallas_call | solution.py:249
  105.1 3.9 %analysis.10.refs_2_ = bf16[64,32768]{1,0:T(8,128)(2,1)} custom-call(s32[1]{0:T(128)} %bitcast.base_ref.me_ref, bf16[80,64]{1,0:T(8,128)(2,1)} %get-tuple-element.7.mixer_ref, f32[64,128]{1,0:T(8,128)} %get-tuple-element.8.rest_ref, bf16[32,65536]{1,0:T(8,128)(2,1)} %refs_0_.11, bf16[32,8192]{1,0:T(8,128)(2,1)} %copy-done.2, ...), custom_call_target="tpu_custom_call", output_to_operand_aliasing={{}: (5, {})} | custom-call | tf_op jit(solution)/shard_map/analysis/pallas_call | solution.py:249
  109.8 5.2 %analysis.11 = bf16[64,32768]{1,0:T(8,128)(2,1)} custom-call(s32[1]{0:T(128)} %bitcast.base_ref.me_ref, bf16[80,64]{1,0:T(8,128)(2,1)} %get-tuple-element.7.mixer_ref, f32[64,128]{1,0:T(8,128)} %get-tuple-element.8.rest_ref, bf16[32,65536]{1,0:T(8,128)(2,1)} %refs_0_.11, bf16[32,12288]{1,0:T(8,128)(2,1)} %copy-done.1, ...), custom_call_target="tpu_custom_call", output_to_operand_aliasing={{}: (5, {})} | custom-call | tf_op jit(solution)/shard_map/analysis/pallas_call | solution.py:249
  115.0 1.0 copy-done
  116.0 6.5 %analysis.12.refs_2_ = bf16[64,32768]{1,0:T(8,128)(2,1)} custom-call(s32[1]{0:T(128)} %bitcast.base_ref.me_ref, bf16[80,64]{1,0:T(8,128)(2,1)} %get-tuple-element.7.mixer_ref, f32[64,128]{1,0:T(8,128)} %get-tuple-element.8.rest_ref, bf16[32,65536]{1,0:T(8,128)(2,1)} %refs_0_.15, bf16[32,16384]{1,0:T(8,128)(2,1)} %copy-done), custom_call_target="tpu_custom_call" | custom-call | tf_op jit(solution)/shard_map/analysis/pallas_call | solution.py:249
  122.5 3.9 %analysis.13.refs_2_ = bf16[64,32768]{1,0:T(8,128)(2,1)} custom-call(s32[1]{0:T(128)} %bitcast.base_ref.me_ref, bf16[80,64]{1,0:T(8,128)(2,1)} %get-tuple-element.7.mixer_ref, f32[64,128]{1,0:T(8,128)} %get-tuple-element.8.rest_ref, bf16[32,65536]{1,0:T(8,128)(2,1)} %refs_0_.15, ...), custom_call_target="tpu_custom_call", output_to_operand_aliasing={{}: (5, {})} | custom-call | tf_op jit(solution)/shard_map/analysis/pallas_call | solution.py:249
  126.4 2.2 %analysis.14.refs_2_ = bf16[64,32768]{1,0:T(8,128)(2,1)} custom-call(s32[1]{0:T(128)} %bitcast.base_ref.me_ref, bf16[80,64]{1,0:T(8,128)(2,1)} %get-tuple-element.7.mixer_ref, f32[64,128]{1,0:T(8,128)} %get-tuple-element.8.rest_ref, bf16[32,65536]{1,0:T(8,128)(2,1)} %refs_0_.15, ...), custom_call_target="tpu_custom_call", output_to_operand_aliasing={{}: (5, {})} | custom-call | tf_op jit(solution)/shard_map/analysis/pallas_call | solution.py:249
  128.6 2.2 %analysis.15 = bf16[64,32768]{1,0:T(8,128)(2,1)} custom-call(s32[1]{0:T(128)} %bitcast.base_ref.me_ref, bf16[80,64]{1,0:T(8,128)(2,1)} %get-tuple-element.7.mixer_ref, f32[64,128]{1,0:T(8,128)} %get-tuple-element.8.rest_ref, bf16[32,65536]{1,0:T(8,128)(2,1)} %refs_0_.15, ...), custom_call_target="tpu_custom_call", output_to_operand_aliasing={{}: (5, {})} | custom-call | tf_op jit(solution)/shard_map/analysis/pallas_call | solution.py:249
  (50 shorter events, 10.6 us)
Async XLA Ops:
  1.7 5.9 %copy-start.4 = (s32[2,32,128]{2,1,0:T(8,128)}, s32[2,32,128]{2,1,0:T(8,128)S(1)}, u32[]{:S(2)}) copy-start(s32[2,32,128]{2,1,0:T(8,128)S(1)} %reshape.56.index_ref) | copy-start | bytes 98308
  1.7 14.7 %collective-permute-start = (s32[2,32,128]{2,1,0:T(8,128)S(1)}, s32[2,32,128]{2,1,0:T(8,128)S(1)}, u32[]{:S(2)}, u32[]{:S(2)}) collective-permute-start(s32[2,32,128]{2,1,0:T(8,128)S(1)} %reshape.56.index_ref), channel_id=1, source_target_pairs={{0,16},{16,0},{1,17},{17,1},{2,18},{18,2},{3,19},{19,3},{4,20},{20... | collective-permute-start | bytes 98312 | tf_op jit(solution)/shard_map/ppermute | solution.py:282
  6.8 102.2 %collective-permute-start.7 = (bf16[32,12288]{1,0:T(8,128)(2,1)}, bf16[32,12288]{1,0:T(8,128)(2,1)S(1)}, u32[]{:S(2)}, u32[]{:S(2)}) collective-permute-start(bf16[32,12288]{1,0:T(8,128)(2,1)} %constant_dynamic-slice_fusion.7), channel_id=1, source_target_pairs={{0,16},{16,0},{1,17},{17,1},{2,18},{18,2},{3,19},{19,3},{4,20},{20... | collective-permute-start | bytes 2359304 | tf_op jit(solution)/shard_map/ppermute | solution.py:279
  7.6 6.5 %copy-start.6 = (f32[2,256,16]{1,2,0:T(8,128)S(1)}, f32[2,256,16]{1,2,0:T(8,128)}, u32[]{:S(2)}) copy-start(f32[2,256,16]{1,2,0:T(8,128)} %param.10) | copy-start | bytes 98308
  7.6 8.3 %copy-start.7 = (s32[2,256]{1,0:T(2,128)S(1)}, s32[2,256]{1,0:T(2,128)}, u32[]{:S(2)}) copy-start(s32[2,256]{1,0:T(2,128)} %param.9) | copy-start | bytes 6148
  16.3 0.6 copy-start.5
  23.5 13.7 %collective-permute-start.1 = (bf16[2,32,4096]{2,1,0:T(8,128)(2,1)}, bf16[2,32,4096]{2,1,0:T(8,128)(2,1)S(1)}, u32[]{:S(2)}, u32[]{:S(2)}) collective-permute-start(bf16[2,32,4096]{2,1,0:T(8,128)(2,1)} %gather.3), channel_id=1, source_target_pairs={{0,16},{16,0},{1,17},{17,1},{2,18},{18,2},{3,19},{19,3},{4,20},{20... | collective-permute-start | bytes 1572872 | tf_op jit(solution)/shard_map/ppermute | solution.py:279
  37.2 0.8 copy-start.3
  45.0 5.9 %collective-permute-start.2 = (f32[64,128]{1,0:T(8,128)}, f32[64,128]{1,0:T(8,128)S(1)}, u32[]{:S(2)}, u32[]{:S(2)}) collective-permute-start(f32[64,128]{1,0:T(8,128)} %statistics.1), channel_id=1, source_target_pairs={{0,16},{16,0},{1,17},{17,1},{2,18},{18,2},{3,19},{19,3},{4,20},{20... | collective-permute-start | bytes 98312 | tf_op jit(solution)/shard_map/ppermute | solution.py:324
  48.8 32.4 %collective-permute-start.8 = (bf16[32,8192]{1,0:T(8,128)(2,1)}, bf16[32,8192]{1,0:T(8,128)(2,1)S(1)}, u32[]{:S(2)}, u32[]{:S(2)}) collective-permute-start(bf16[32,8192]{1,0:T(8,128)(2,1)} %get-tuple-element.12), channel_id=1, source_target_pairs={{0,16},{16,0},{1,17},{17,1},{2,18},{18,2},{3,19},{19,3},{4,20},{20... | collective-permute-start | bytes 1572872 | tf_op jit(solution)/shard_map/ppermute | solution.py:279
  49.3 36.3 %collective-permute-start.9 = (bf16[32,8192]{1,0:T(8,128)(2,1)}, bf16[32,8192]{1,0:T(8,128)(2,1)}, u32[]{:S(2)}, u32[]{:S(2)}) collective-permute-start(bf16[32,8192]{1,0:T(8,128)(2,1)} %get-tuple-element.11), channel_id=1, source_target_pairs={{0,16},{16,0},{1,17},{17,1},{2,18},{18,2},{3,19},{19,3},{4,20},{20... | collective-permute-start | bytes 1572872 | tf_op jit(solution)/shard_map/ppermute | solution.py:279
  51.6 2.1 %collective-permute-start.3 = (f32[64,128]{1,0:T(8,128)S(1)}, f32[64,128]{1,0:T(8,128)S(1)}, u32[]{:S(2)}, u32[]{:S(2)}) collective-permute-start(f32[64,128]{1,0:T(8,128)S(1)} %add.82), channel_id=1, source_target_pairs={{0,1},{1,0},{2,3},{3,2},{4,5},{5,4},{6,7},{7,6},{8,9},{9,8},{10,11... | collective-permute-start | bytes 98312 | tf_op jit(solution)/shard_map/ppermute | solution.py:324
  53.3 27.5 %collective-permute-start.10 = (bf16[32,4096]{1,0:T(8,128)(2,1)}, bf16[32,4096]{1,0:T(8,128)(2,1)}, u32[]{:S(2)}, u32[]{:S(2)}) collective-permute-start(bf16[32,4096]{1,0:T(8,128)(2,1)} %constant_dynamic-slice_fusion.4), channel_id=1, source_target_pairs={{0,16},{16,0},{1,17},{17,1},{2,18},{18,2},{3,19},{19,3},{4,20},{20... | collective-permute-start | bytes 786440 | tf_op jit(solution)/shard_map/ppermute | solution.py:279
  53.8 4.0 %collective-permute-start.4 = (f32[64,128]{1,0:T(8,128)S(1)}, f32[64,128]{1,0:T(8,128)S(1)}, u32[]{:S(2)}, u32[]{:S(2)}) collective-permute-start(f32[64,128]{1,0:T(8,128)S(1)} %add.83), channel_id=1, source_target_pairs={{0,2},{1,3},{2,0},{3,1},{4,6},{5,7},{6,4},{7,5},{8,10},{9,11},{10,... | collective-permute-start | bytes 98312 | tf_op jit(solution)/shard_map/ppermute | solution.py:324
  57.8 3.9 %collective-permute-start.5 = (f32[64,128]{1,0:T(8,128)S(1)}, f32[64,128]{1,0:T(8,128)S(1)}, u32[]{:S(2)}, u32[]{:S(2)}) collective-permute-start(f32[64,128]{1,0:T(8,128)S(1)} %add.84), channel_id=1, source_target_pairs={{0,4},{1,5},{2,6},{3,7},{4,0},{5,1},{6,2},{7,3},{8,12},{9,13},{10,... | collective-permute-start | bytes 98312 | tf_op jit(solution)/shard_map/ppermute | solution.py:324
  61.7 53.3 %collective-permute-start.14 = (bf16[32,16384]{1,0:T(8,128)(2,1)S(1)}, bf16[32,16384]{1,0:T(8,128)(2,1)S(1)}, u32[]{:S(2)}, u32[]{:S(2)}) collective-permute-start(bf16[32,16384]{1,0:T(8,128)(2,1)S(1)} %constant_dynamic-slice_fusion), channel_id=1, source_target_pairs={{0,16},{16,0},{1,17},{17,1},{2,18},{18,2},{3,19},{19,3},{4,20},{20... | collective-permute-start | bytes 3145736 | tf_op jit(solution)/shard_map/ppermute | solution.py:279
  80.8 41.7 %collective-permute-start.13 = (bf16[32,8192]{1,0:T(8,128)(2,1)}, bf16[32,8192]{1,0:T(8,128)(2,1)}, u32[]{:S(2)}, u32[]{:S(2)}) collective-permute-start(bf16[32,8192]{1,0:T(8,128)(2,1)} %constant_dynamic-slice_fusion.1), channel_id=1, source_target_pairs={{0,16},{16,0},{1,17},{17,1},{2,18},{18,2},{3,19},{19,3},{4,20},{20... | collective-permute-start | bytes 1572872 | tf_op jit(solution)/shard_map/ppermute | solution.py:279
  81.2 20.0 %copy-start.2 = (bf16[32,8192]{1,0:T(8,128)(2,1)}, bf16[32,8192]{1,0:T(8,128)(2,1)S(1)}, u32[]{:S(2)}) copy-start(bf16[32,8192]{1,0:T(8,128)(2,1)S(1)} %collective-permute-done.8.refs_1_) | copy-start | bytes 1572868
  81.2 5.9 %collective-permute-start.6 = (f32[64,128]{1,0:T(8,128)S(1)}, f32[64,128]{1,0:T(8,128)S(1)}, u32[]{:S(2)}, u32[]{:S(2)}) collective-permute-start(f32[64,128]{1,0:T(8,128)S(1)} %add.85), channel_id=1, source_target_pairs={{0,8},{1,9},{2,10},{3,11},{4,12},{5,13},{6,14},{7,15},{8,0},{9,1},... | collective-permute-start | bytes 98312 | tf_op jit(solution)/shard_map/ppermute | solution.py:324
  85.6 40.8 %collective-permute-start.12 = (bf16[32,4096]{1,0:T(8,128)(2,1)}, bf16[32,4096]{1,0:T(8,128)(2,1)}, u32[]{:S(2)}, u32[]{:S(2)}) collective-permute-start(bf16[32,4096]{1,0:T(8,128)(2,1)} %constant_dynamic-slice_fusion.2), channel_id=1, source_target_pairs={{0,16},{16,0},{1,17},{17,1},{2,18},{18,2},{3,19},{19,3},{4,20},{20... | collective-permute-start | bytes 786440 | tf_op jit(solution)/shard_map/ppermute | solution.py:279
  87.1 41.5 %collective-permute-start.11 = (bf16[32,4096]{1,0:T(8,128)(2,1)}, bf16[32,4096]{1,0:T(8,128)(2,1)}, u32[]{:S(2)}, u32[]{:S(2)}) collective-permute-start(bf16[32,4096]{1,0:T(8,128)(2,1)} %constant_dynamic-slice_fusion.3), channel_id=1, source_target_pairs={{0,16},{16,0},{1,17},{17,1},{2,18},{18,2},{3,19},{19,3},{4,20},{20... | collective-permute-start | bytes 786440 | tf_op jit(solution)/shard_map/ppermute | solution.py:279
  108.9 0.9 copy-start.1
  115.0 1.0 copy-start

commit v2 on v1

--- a/solution.py
+++ b/solution.py
@@ -1,4 +1,5 @@
 import functools
+import math
 
 import jax
 import jax.numpy as jnp
@@ -9,18 +10,18 @@
 
 
 ITERS = 24
+VMEM = 16 * 1024 * 1024
 LANES = 128
 
 MESSAGES = (
-    (0, 0, 1),
-    (0, 1, 3),
-    (0, 3, 5),
-    (0, 5, 8),
+    (0, 0, 2),
+    (0, 2, 4),
+    (0, 4, 8),
     (1, 0, 4),
     (1, 4, 6),
-    (1, 6, 7),
-    (1, 7, 8),
+    (1, 6, 8),
 )
+CALLS = ((0, 1, 2), (3,), (4,), (5,))
 
 
 def split(x):
@@ -204,42 +205,49 @@
         ),
         in_specs=[pl.BlockSpec(memory_space=pltpu.SMEM), pl.BlockSpec(memory_space=pltpu.VMEM)],
         out_specs=(pl.BlockSpec(memory_space=pltpu.VMEM),) * 3,
+        compiler_params=pltpu.CompilerParams(vmem_limit_bytes=VMEM),
         name="transform",
     )(me, stats)
 
 
-def analysis_kernel(parts, aliased, base_ref, mixer_ref, rest_ref, *refs):
-    cols_refs = refs[:parts]
-    out_ref = refs[parts + aliased]
-    everyone = out_ref.shape[0]
-    members = cols_refs[0].shape[0]
-    if members % 16 == 0:
-        cols = jnp.concatenate([ref[...] for ref in cols_refs], axis=0)
-        mixed = jnp.dot(mixer_ref[...], cols, preferred_element_type=jnp.float32)
-    else:
-        cols = jnp.concatenate([ref[...].astype(jnp.float32) for ref in cols_refs], axis=0)
-        mixed = jnp.dot(
-            mixer_ref[...], cols.astype(jnp.bfloat16), preferred_element_type=jnp.float32
-        )
+def analysis_kernel(bounds, sources, aliased, base_ref, mixer_ref, rest_ref, own_ref, *refs):
+    out_ref = refs[len(bounds) * sources + aliased]
+    everyone, width = out_ref.shape
+    members = own_ref.shape[0]
+    step = pl.program_id(0)
     rest = rest_ref[:, 0:1]
-    out = mixed[:everyone] + rest * mixed[everyone : everyone + 1]
-    out_ref[...] = out.astype(out_ref.dtype)
-
-
-def analyse(out, state, received, mixer, rest, base, first, piece):
-    members, length = received[0].shape
+    for i, (lo, hi) in enumerate(bounds):
+
+        @pl.when((step >= lo) & (step < hi))
+        def _(i=i, lo=lo):
+            at = pl.ds(pl.multiple_of((step - lo) * width, width), width)
+            cols = [own_ref[...]]
+            cols += [ref[:, at] for ref in refs[i * sources : (i + 1) * sources]]
+            if members % 16:
+                cols = [x.astype(jnp.float32) for x in cols]
+            cols = jnp.concatenate(cols, axis=0).astype(jnp.bfloat16)
+            mixed = jnp.dot(mixer_ref[...], cols, preferred_element_type=jnp.float32)
+            out = mixed[:everyone] + rest * mixed[everyone : everyone + 1]
+            out_ref[...] = out.astype(out_ref.dtype)
+
+
+def analyse(out, state, messages, mixer, rest, base, piece):
+    members = state.shape[0]
     everyone = rest.shape[0]
-    width = min(2048, length)
-    steps = length // width
+    first, last = messages[0][0], messages[-1][1]
+    width = 2 * piece // 8
+    for lo, hi, _ in messages:
+        width = math.gcd(width, hi - lo)
     skip = first // width
     whole = piece // width
-    parts = len(received) + 1
+    bounds = tuple((lo // width - skip, hi // width - skip) for lo, hi, _ in messages)
+    received = [x for _, _, pieces in messages for x in pieces]
     aliased = int(out is not None)
     in_specs = [
         pl.BlockSpec(mixer.shape, lambda i, base: (0, 0)),
         pl.BlockSpec(rest.shape, lambda i, base: (0, 0)),
         pl.BlockSpec((members, width), lambda i, base: (0, base[0] * whole + skip + i)),
-    ] + [pl.BlockSpec((members, width), lambda i, base: (0, i))] * len(received)
+    ] + [pl.BlockSpec(memory_space=pltpu.VMEM)] * len(received)
     operands = [base, mixer, rest, state, *received]
     aliases = {}
     if aliased:
@@ -247,16 +255,20 @@
         aliases = {len(operands): 0}
         operands.append(out)
     return pl.pallas_call(
-        functools.partial(analysis_kernel, parts, aliased),
+        functools.partial(
+            analysis_kernel, bounds, len(received) // len(messages), aliased
+        ),
         out_shape=jax.ShapeDtypeStruct((everyone, piece), jnp.bfloat16),
         grid_spec=pltpu.PrefetchScalarGridSpec(
             num_scalar_prefetch=1,
-            grid=(steps,),
+            grid=((last - first) // width,),
             in_specs=in_specs,
             out_specs=pl.BlockSpec((everyone, width), lambda i, base: (0, skip + i)),
         ),
         input_output_aliases=aliases,
-        compiler_params=pltpu.CompilerParams(dimension_semantics=("arbitrary",)),
+        compiler_params=pltpu.CompilerParams(
+            dimension_semantics=("arbitrary",), vmem_limit_bytes=VMEM
+        ),
         name="analysis",
     )(*operands)
 
@@ -292,8 +304,10 @@
             for shift in shifts
         ]
 
-    index = obs_index.reshape(2, observations // LANES, LANES)
-    others_index = [to_upper(index, shift) for shift in shifts]
+    others_index = [to_upper(obs_index, shift) for shift in shifts]
+    index, *others_index = (
+        x.reshape(2, observations // LANES, LANES) for x in (obs_index, *others_index)
+    )
 
     own_hx = gather(state_a, state_b, index, me_ref, slots, piece)
     sent_hx = [
@@ -329,9 +343,13 @@
     transform, mixer, rest = make_transform(stats, members, me_ref)
 
     outs = [None, None]
-    for (group, lo, hi), pieces in zip(MESSAGES, received):
+    for call in CALLS:
+        group = MESSAGES[call[0]][0]
+        messages = [
+            (MESSAGES[m][1] * unit, MESSAGES[m][2] * unit, received[m]) for m in call
+        ]
         outs[group] = analyse(
-            outs[group], states[group], pieces, mixer, rest, me_ref, lo * unit, piece
+            outs[group], states[group], messages, mixer, rest, me_ref, piece
         )
     return (outs[0], outs[1], transform)
 

time: 132 us -> 148 us (1.12)
  waiting for transfers between devices: 28.4 us -> 72.5 us
  Pallas kernels: 60.6 us -> 38.5 us
  starting transfers between devices: 19.2 us -> 14.8 us
    ppermute x9 -> x7, waiting for transfers between devices: 27 us -> 68.5 us  [to_lower(): lax.ppermute(array, 'mem', [(i, (i - shift) % nmem) for i in range(nmem)])]
    pallas_call x8 -> x4, Pallas kernels: 29.8 us -> 8.66 us  [analyse(): pl.pallas_call(functools.partial(analysis_kernel, bounds, len(received) /...]
    dynamic_slice x7 -> x5, local copies, waits for them, and re-layouts: 12.5 us -> 8.92 us  [cut(): lax.dynamic_slice(source[group], (0, lax.rem(me + nmem - shift, nmem) * p...]
    ppermute x9 -> x7, starting transfers between devices: 8.56 us -> 5.37 us  [to_lower(): lax.ppermute(array, 'mem', [(i, (i - shift) % nmem) for i in range(nmem)])]
    ppermute x5, waiting for transfers between devices: 1.4 us -> 4.04 us  [all_sum(): x = x + lax.ppermute(x, axis, [(i, i ^ step) for i in range(size)])]
    unnamed x18 -> x10, local copies, waits for them, and re-layouts: 4.3 us -> 4.74 us
  transfers between devices with their start and end apart: 15 -> 13, of which waited for: 4 -> 8; matrix products, arithmetic and copies ran while one was open for 13% -> 11% of each run, Pallas kernels for 45% -> 16%
where the time goes in v2:
time: 148 us; the launch traced here: 147 us
  waiting for transfers between devices  72.5 us (49%)
  Pallas kernels  38.5 us (26%)
  local copies, waits for them, and re-layouts  18 us (12%)
  starting transfers between devices  14.8 us (10%)
  other arithmetic  2.2 us (1%)
    ppermute x7, waiting for transfers between devices, to_lower(): lax.ppermute(array, 'mem', [(i, (i - shift) % nmem) for i in range(nmem)])  68.5 us
    pallas_call x2, Pallas kernels, gather(): pl.pallas_call(functools.partial(gather_kernel, slots), out_shape=jax.Sha...  13 us
    pallas_call x1, Pallas kernels, make_transform(): pl.pallas_call(functools.partial(transform_kernel, members), out_shape=(j...  9.84 us
    dynamic_slice x5, local copies, waits for them, and re-layouts, cut(): lax.dynamic_slice(source[group], (0, lax.rem(me + nmem - shift, nmem) * p...  8.92 us
    pallas_call x4, Pallas kernels, analyse(): pl.pallas_call(functools.partial(analysis_kernel, bounds, len(received) /...  8.66 us
    pallas_call x1, Pallas kernels, statistics(): pl.pallas_call(functools.partial(stats_kernel, len(parts)), out_shape=jax...  6.98 us
    ppermute x5, starting transfers between devices, all_sum(): x = x + lax.ppermute(x, axis, [(i, i ^ step) for i in range(size)])  6.42 us
    ppermute x7, starting transfers between devices, to_lower(): lax.ppermute(array, 'mem', [(i, (i - shift) % nmem) for i in range(nmem)])  5.37 us
  transfers between devices with their start and end apart: 13, of which 8 were waited for; matrix products, arithmetic and copies ran while one was open for 11% of the time, Pallas kernels for 16%

profile of v2, /device:TPU:0, one launch (start us, length us, event | category | flops | bytes accessed | tf_op | source)
XLA Modules:
  0.0 146.8 jit_solution(815608883606466472)
XLA Ops:
  0.6 3.0 %collective-permute-start = (s32[2,256,16]{1,2,0:T(8,128)}, s32[2,256,16]{1,2,0:T(8,128)S(1)}, u32[]{:S(2)}, u32[]{:S(2)}) collective-permute-start(s32[2,256,16]{1,2,0:T(8,128)} %param.8), channel_id=1, source_target_pairs={{0,16},{16,0},{1,17},{17,1},{2,18},{18,2},{3,19},{19,3},{4,20},{20... | collective-permute-start | bytes 98312 | tf_op jit(solution)/shard_map/ppermute | solution.py:294
  4.4 0.9 copy.24
  6.1 0.8 lt.33.clone
  8.0 0.9 copy.26
  9.7 6.5 %gather.2.refs_0_ = bf16[2,32,4096]{2,1,0:T(8,128)(2,1)} custom-call(s32[1]{0:T(128)} %bitcast.base_ref.me_ref, s32[2,32,128]{2,1,0:T(8,128)} %reshape.59.index_ref, bf16[32,65536]{1,0:T(8,128)(2,1)} %own_ref.4, bf16[32,65536]{1,0:T(8,128)(2,1)} %own_ref.7), custom_call_target="tpu_custom_call" | custom-call | tf_op jit(solution)/shard_map/gather/pallas_call | solution.py:70
  17.1 6.5 %gather.3 = bf16[2,32,4096]{2,1,0:T(8,128)(2,1)} custom-call(s32[1]{0:T(128)S(6)} %rem.36.base_ref, s32[2,32,128]{2,1,0:T(8,128)} %reshape.60.index_ref, bf16[32,65536]{1,0:T(8,128)(2,1)} %own_ref.4, bf16[32,65536]{1,0:T(8,128)(2,1)} %own_ref.7), custom_call_target="tpu_custom_call" | custom-call | tf_op jit(solution)/shard_map/gather/pallas_call | solution.py:70
  24.2 12.9 %collective-permute-done.1.refs_1_ = bf16[2,32,4096]{2,1,0:T(8,128)(2,1)S(1)} collective-permute-done((bf16[2,32,4096]{2,1,0:T(8,128)(2,1)}, bf16[2,32,4096]{2,1,0:T(8,128)(2,1)S(1)}, u32[]{:S(2)}, u32[]{:S(2)}) %collective-permute-start.1) | collective-permute-done | bytes 524320 | tf_op jit(solution)/shard_map/ppermute | solution.py:291
  38.0 7.0 %statistics.1 = f32[64,128]{1,0:T(8,128)} custom-call(s32[1]{0:T(128)} %bitcast.base_ref.me_ref, bf16[2,32,4096]{2,1,0:T(8,128)(2,1)} %gather.2.refs_0_, bf16[2,32,4096]{2,1,0:T(8,128)(2,1)} %copy-done.3, f32[2,1,4096]{2,1,0:T(1,128)} %reshape.63.refs_2_, f32[2,1,4096]{2,1,0:T(1,128)} %reshape.64.refs_3_, f32[2,1,4096]{2,1,0:T(1,128)} %compare_convert_fusion.refs_4_), custom_call_target="tpu_custom_call" | custom-call | tf_op jit(solution)/shard_map/statistics/pallas_call | solution.py:138
  45.2 3.8 %collective-permute-done.2 = f32[64,128]{1,0:T(8,128)S(1)} collective-permute-done((f32[64,128]{1,0:T(8,128)}, f32[64,128]{1,0:T(8,128)S(1)}, u32[]{:S(2)}, u32[]{:S(2)}) %collective-permute-start.2) | collective-permute-done | bytes 32800 | tf_op jit(solution)/shard_map/ppermute | solution.py:338
  49.8 2.3 %constant_dynamic-slice_fusion = bf16[32,16384]{1,0:T(8,128)(2,1)} fusion(bf16[32,65536]{1,0:T(8,128)(2,1)} %own_ref.7, s32[]{:T(128)S(6)} %select_n.14), kind=kLoop, calls=%fused_computation.3 | loop fusion | bytes 2097156 | tf_op jit(solution)/shard_map/dynamic_slice | solution.py:299
  52.4 1.8 %collective-permute-start.4 = (f32[64,128]{1,0:T(8,128)S(1)}, f32[64,128]{1,0:T(8,128)S(1)}, u32[]{:S(2)}, u32[]{:S(2)}) collective-permute-start(f32[64,128]{1,0:T(8,128)S(1)} %add.59), channel_id=1, source_target_pairs={{0,2},{1,3},{2,0},{3,1},{4,6},{5,7},{6,4},{7,5},{8,10},{9,11},{10,... | collective-permute-start | bytes 98312 | tf_op jit(solution)/shard_map/ppermute | solution.py:338
  54.2 1.1 constant_dynamic-slice_fusion.1
  55.3 1.6 %collective-permute-start.11 = (bf16[32,8192]{1,0:T(8,128)(2,1)S(1)}, bf16[32,8192]{1,0:T(8,128)(2,1)S(1)}, u32[]{:S(2)}, u32[]{:S(2)}) collective-permute-start(bf16[32,8192]{1,0:T(8,128)(2,1)S(1)} %constant_dynamic-slice_fusion.1), channel_id=1, source_target_pairs={{0,16},{16,0},{1,17},{17,1},{2,18},{18,2},{3,19},{19,3},{4,20},{20... | collective-permute-start | bytes 1572872 | tf_op jit(solution)/shard_map/ppermute | solution.py:291
  56.9 1.6 %collective-permute-start.5 = (f32[64,128]{1,0:T(8,128)S(1)}, f32[64,128]{1,0:T(8,128)S(1)}, u32[]{:S(2)}, u32[]{:S(2)}) collective-permute-start(f32[64,128]{1,0:T(8,128)S(1)} %add.60), channel_id=1, source_target_pairs={{0,4},{1,5},{2,6},{3,7},{4,0},{5,1},{6,2},{7,3},{8,12},{9,13},{10,... | collective-permute-start | bytes 98312 | tf_op jit(solution)/shard_map/ppermute | solution.py:338
  58.5 2.2 %constant_dynamic-slice_fusion.4 = (bf16[32,8192]{1,0:T(8,128)(2,1)}, bf16[32,8192]{1,0:T(8,128)(2,1)}) fusion(bf16[32,65536]{1,0:T(8,128)(2,1)} %own_ref.4, s32[]{:T(128)S(6)} %select_n.15, s32[]{:T(128)S(6)} %select_n.14), kind=kLoop, calls=%fused_computation.7 | loop fusion | bytes 2097160 | tf_op jit(solution)/shard_map/dynamic_slice | solution.py:299
  60.8 1.2 collective-permute-start.7
  61.9 0.8 collective-permute-start.8
  62.8 2.7 %collective-permute-start.6 = (f32[64,128]{1,0:T(8,128)S(1)}, f32[64,128]{1,0:T(8,128)S(1)}, u32[]{:S(2)}, u32[]{:S(2)}) collective-permute-start(f32[64,128]{1,0:T(8,128)S(1)} %add.61), channel_id=1, source_target_pairs={{0,8},{1,9},{2,10},{3,11},{4,12},{5,13},{6,14},{7,15},{8,0},{9,1},... | collective-permute-start | bytes 98312 | tf_op jit(solution)/shard_map/ppermute | solution.py:338
  65.5 2.3 %constant_dynamic-slice_fusion.3 = bf16[32,16384]{1,0:T(8,128)(2,1)} fusion(bf16[32,65536]{1,0:T(8,128)(2,1)} %own_ref.4, s32[]{:T(128)S(6)} %select_n.16), kind=kLoop, calls=%fused_computation.6 | loop fusion | bytes 2097156 | tf_op jit(solution)/shard_map/dynamic_slice | solution.py:299
  67.9 1.2 collective-permute-start.9
  69.1 1.1 constant_dynamic-slice_fusion.2
  70.2 8.2 %collective-permute-done.12.refs_0_ = bf16[32,16384]{1,0:T(8,128)(2,1)S(1)} collective-permute-done((bf16[32,16384]{1,0:T(8,128)(2,1)}, bf16[32,16384]{1,0:T(8,128)(2,1)S(1)}, u32[]{:S(2)}, u32[]{:S(2)}) %collective-permute-start.12) | collective-permute-done | bytes 1048608 | tf_op jit(solution)/shard_map/ppermute | solution.py:291
  78.6 9.8 %transform.1 = (f32[64,64]{1,0:T(8,128)}, bf16[80,64]{1,0:T(8,128)(2,1)S(1)}, f32[64,128]{1,0:T(8,128)S(1)}) custom-call(s32[1]{0:T(128)} %bitcast.base_ref.me_ref, f32[64,128]{1,0:T(8,128)S(1)} %add.62.stats_ref), custom_call_target="tpu_custom_call" | custom-call | tf_op jit(solution)/shard_map/transform/pallas_call | solution.py:199
  88.5 2.2 %copy-done = bf16[32,65536]{1,0:T(8,128)(2,1)S(1)} copy-done((bf16[32,65536]{1,0:T(8,128)(2,1)S(1)}, bf16[32,65536]{1,0:T(8,128)(2,1)}, u32[]{:S(2)}) %copy-start) | copy-done | bytes 4194328
  90.7 2.1 %analysis.5.refs_1_ = bf16[64,32768]{1,0:T(8,128)(2,1)} custom-call(s32[1]{0:T(128)} %bitcast.base_ref.me_ref, bf16[80,64]{1,0:T(8,128)(2,1)S(1)} %get-tuple-element.7.mixer_ref, f32[64,128]{1,0:T(8,128)S(1)} %get-tuple-element.8.rest_ref, bf16[32,65536]{1,0:T(8,128)(2,1)S(1)} %copy-done, bf16[32,16384]{1,0:T(8,128)(2,1)S(1)} %collective-permute-done.12.refs_0_), custom_call_target="tpu_custom_call" | custom-call | tf_op jit(solution)/shard_map/analysis/pallas_call | solution.py:257
  92.7 1.5 %analysis.6.refs_1_ = bf16[64,32768]{1,0:T(8,128)(2,1)} custom-call(s32[1]{0:T(128)} %bitcast.base_ref.me_ref, bf16[80,64]{1,0:T(8,128)(2,1)S(1)} %get-tuple-element.7.mixer_ref, f32[64,128]{1,0:T(8,128)S(1)} %get-tuple-element.8.rest_ref, bf16[32,65536]{1,0:T(8,128)(2,1)S(1)} %copy-done, ...), custom_call_target="tpu_custom_call", output_to_operand_aliasing={{}: (5, {})} | custom-call | tf_op jit(solution)/shard_map/analysis/pallas_call | solution.py:257
  94.2 6.6 %collective-permute-done.7.refs_0_ = bf16[32,8192]{1,0:T(8,128)(2,1)S(1)} collective-permute-done((bf16[32,8192]{1,0:T(8,128)(2,1)}, bf16[32,8192]{1,0:T(8,128)(2,1)S(1)}, u32[]{:S(2)}, u32[]{:S(2)}) %collective-permute-start.7) | collective-permute-done | bytes 524320 | tf_op jit(solution)/shard_map/ppermute | solution.py:291
  100.8 11.2 %collective-permute-done.8.refs_1_ = bf16[32,8192]{1,0:T(8,128)(2,1)S(1)} collective-permute-done((bf16[32,8192]{1,0:T(8,128)(2,1)}, bf16[32,8192]{1,0:T(8,128)(2,1)S(1)}, u32[]{:S(2)}, u32[]{:S(2)}) %collective-permute-start.8) | collective-permute-done | bytes 524320 | tf_op jit(solution)/shard_map/ppermute | solution.py:291
  112.0 22.5 %collective-permute-done.9.refs_2_ = bf16[32,16384]{1,0:T(8,128)(2,1)S(1)} collective-permute-done((bf16[32,16384]{1,0:T(8,128)(2,1)}, bf16[32,16384]{1,0:T(8,128)(2,1)S(1)}, u32[]{:S(2)}, u32[]{:S(2)}) %collective-permute-start.9) | collective-permute-done | bytes 1048608 | tf_op jit(solution)/shard_map/ppermute | solution.py:291
  134.5 3.6 %analysis.4 = bf16[64,32768]{1,0:T(8,128)(2,1)} custom-call(s32[1]{0:T(128)} %bitcast.base_ref.me_ref, bf16[80,64]{1,0:T(8,128)(2,1)S(1)} %get-tuple-element.7.mixer_ref, f32[64,128]{1,0:T(8,128)S(1)} %get-tuple-element.8.rest_ref, bf16[32,65536]{1,0:T(8,128)(2,1)S(1)} %copy-done.2, bf16[32,8192]{1,0:T(8,128)(2,1)S(1)} %collective-permute-done.7.refs_0_, ...), custom_call_target="tpu_custom_call" | custom-call | tf_op jit(solution)/shard_map/analysis/pallas_call | solution.py:257
  138.1 7.1 %collective-permute-done.10.refs_0_ = bf16[32,8192]{1,0:T(8,128)(2,1)S(1)} collective-permute-done((bf16[32,8192]{1,0:T(8,128)(2,1)S(1)}, bf16[32,8192]{1,0:T(8,128)(2,1)S(1)}, u32[]{:S(2)}, u32[]{:S(2)}) %collective-permute-start.10) | collective-permute-done | bytes 524320 | tf_op jit(solution)/shard_map/ppermute | solution.py:291
  145.3 1.5 %analysis.7 = bf16[64,32768]{1,0:T(8,128)(2,1)} custom-call(s32[1]{0:T(128)} %bitcast.base_ref.me_ref, bf16[80,64]{1,0:T(8,128)(2,1)S(1)} %get-tuple-element.7.mixer_ref, f32[64,128]{1,0:T(8,128)S(1)} %get-tuple-element.8.rest_ref, bf16[32,65536]{1,0:T(8,128)(2,1)S(1)} %copy-done.1, ...), custom_call_target="tpu_custom_call", output_to_operand_aliasing={{}: (5, {})} | custom-call | tf_op jit(solution)/shard_map/analysis/pallas_call | solution.py:257
  (34 shorter events, 7.7 us)
Async XLA Ops:
  0.6 15.6 %collective-permute-start = (s32[2,256,16]{1,2,0:T(8,128)}, s32[2,256,16]{1,2,0:T(8,128)S(1)}, u32[]{:S(2)}, u32[]{:S(2)}) collective-permute-start(s32[2,256,16]{1,2,0:T(8,128)} %param.8), channel_id=1, source_target_pairs={{0,16},{16,0},{1,17},{17,1},{2,18},{18,2},{3,19},{19,3},{4,20},{20... | collective-permute-start | bytes 98312 | tf_op jit(solution)/shard_map/ppermute | solution.py:294
  23.6 13.6 %collective-permute-start.1 = (bf16[2,32,4096]{2,1,0:T(8,128)(2,1)}, bf16[2,32,4096]{2,1,0:T(8,128)(2,1)S(1)}, u32[]{:S(2)}, u32[]{:S(2)}) collective-permute-start(bf16[2,32,4096]{2,1,0:T(8,128)(2,1)} %gather.3), channel_id=1, source_target_pairs={{0,16},{16,0},{1,17},{17,1},{2,18},{18,2},{3,19},{19,3},{4,20},{20... | collective-permute-start | bytes 1572872 | tf_op jit(solution)/shard_map/ppermute | solution.py:291
  37.2 0.8 copy-start.3
  44.9 4.1 %collective-permute-start.2 = (f32[64,128]{1,0:T(8,128)}, f32[64,128]{1,0:T(8,128)S(1)}, u32[]{:S(2)}, u32[]{:S(2)}) collective-permute-start(f32[64,128]{1,0:T(8,128)} %statistics.1), channel_id=1, source_target_pairs={{0,16},{16,0},{1,17},{17,1},{2,18},{18,2},{3,19},{19,3},{4,20},{20... | collective-permute-start | bytes 98312 | tf_op jit(solution)/shard_map/ppermute | solution.py:338
  49.8 2.6 %collective-permute-start.3 = (f32[64,128]{1,0:T(8,128)S(1)}, f32[64,128]{1,0:T(8,128)S(1)}, u32[]{:S(2)}, u32[]{:S(2)}) collective-permute-start(f32[64,128]{1,0:T(8,128)S(1)} %add.58), channel_id=1, source_target_pairs={{0,1},{1,0},{2,3},{3,2},{4,5},{5,4},{6,7},{7,6},{8,9},{9,8},{10,11... | collective-permute-start | bytes 98312 | tf_op jit(solution)/shard_map/ppermute | solution.py:338
  52.1 26.2 %collective-permute-start.12 = (bf16[32,16384]{1,0:T(8,128)(2,1)}, bf16[32,16384]{1,0:T(8,128)(2,1)S(1)}, u32[]{:S(2)}, u32[]{:S(2)}) collective-permute-start(bf16[32,16384]{1,0:T(8,128)(2,1)} %constant_dynamic-slice_fusion), channel_id=1, source_target_pairs={{0,16},{16,0},{1,17},{17,1},{2,18},{18,2},{3,19},{19,3},{4,20},{20... | collective-permute-start | bytes 3145736 | tf_op jit(solution)/shard_map/ppermute | solution.py:291
  52.4 4.5 %collective-permute-start.4 = (f32[64,128]{1,0:T(8,128)S(1)}, f32[64,128]{1,0:T(8,128)S(1)}, u32[]{:S(2)}, u32[]{:S(2)}) collective-permute-start(f32[64,128]{1,0:T(8,128)S(1)} %add.59), channel_id=1, source_target_pairs={{0,2},{1,3},{2,0},{3,1},{4,6},{5,7},{6,4},{7,5},{8,10},{9,11},{10,... | collective-permute-start | bytes 98312 | tf_op jit(solution)/shard_map/ppermute | solution.py:338
  55.3 37.4 %collective-permute-start.11 = (bf16[32,8192]{1,0:T(8,128)(2,1)S(1)}, bf16[32,8192]{1,0:T(8,128)(2,1)S(1)}, u32[]{:S(2)}, u32[]{:S(2)}) collective-permute-start(bf16[32,8192]{1,0:T(8,128)(2,1)S(1)} %constant_dynamic-slice_fusion.1), channel_id=1, source_target_pairs={{0,16},{16,0},{1,17},{17,1},{2,18},{18,2},{3,19},{19,3},{4,20},{20... | collective-permute-start | bytes 1572872 | tf_op jit(solution)/shard_map/ppermute | solution.py:291
  56.9 5.9 %collective-permute-start.5 = (f32[64,128]{1,0:T(8,128)S(1)}, f32[64,128]{1,0:T(8,128)S(1)}, u32[]{:S(2)}, u32[]{:S(2)}) collective-permute-start(f32[64,128]{1,0:T(8,128)S(1)} %add.60), channel_id=1, source_target_pairs={{0,4},{1,5},{2,6},{3,7},{4,0},{5,1},{6,2},{7,3},{8,12},{9,13},{10,... | collective-permute-start | bytes 98312 | tf_op jit(solution)/shard_map/ppermute | solution.py:338
  60.8 40.0 %collective-permute-start.7 = (bf16[32,8192]{1,0:T(8,128)(2,1)}, bf16[32,8192]{1,0:T(8,128)(2,1)S(1)}, u32[]{:S(2)}, u32[]{:S(2)}) collective-permute-start(bf16[32,8192]{1,0:T(8,128)(2,1)} %get-tuple-element.12), channel_id=1, source_target_pairs={{0,16},{16,0},{1,17},{17,1},{2,18},{18,2},{3,19},{19,3},{4,20},{20... | collective-permute-start | bytes 1572872 | tf_op jit(solution)/shard_map/ppermute | solution.py:291
  61.9 50.1 %collective-permute-start.8 = (bf16[32,8192]{1,0:T(8,128)(2,1)}, bf16[32,8192]{1,0:T(8,128)(2,1)S(1)}, u32[]{:S(2)}, u32[]{:S(2)}) collective-permute-start(bf16[32,8192]{1,0:T(8,128)(2,1)} %get-tuple-element.11), channel_id=1, source_target_pairs={{0,16},{16,0},{1,17},{17,1},{2,18},{18,2},{3,19},{19,3},{4,20},{20... | collective-permute-start | bytes 1572872 | tf_op jit(solution)/shard_map/ppermute | solution.py:291
  62.8 5.1 %collective-permute-start.6 = (f32[64,128]{1,0:T(8,128)S(1)}, f32[64,128]{1,0:T(8,128)S(1)}, u32[]{:S(2)}, u32[]{:S(2)}) collective-permute-start(f32[64,128]{1,0:T(8,128)S(1)} %add.61), channel_id=1, source_target_pairs={{0,8},{1,9},{2,10},{3,11},{4,12},{5,13},{6,14},{7,15},{8,0},{9,1},... | collective-permute-start | bytes 98312 | tf_op jit(solution)/shard_map/ppermute | solution.py:338
  67.9 66.6 %collective-permute-start.9 = (bf16[32,16384]{1,0:T(8,128)(2,1)}, bf16[32,16384]{1,0:T(8,128)(2,1)S(1)}, u32[]{:S(2)}, u32[]{:S(2)}) collective-permute-start(bf16[32,16384]{1,0:T(8,128)(2,1)} %constant_dynamic-slice_fusion.3), channel_id=1, source_target_pairs={{0,16},{16,0},{1,17},{17,1},{2,18},{18,2},{3,19},{19,3},{4,20},{20... | collective-permute-start | bytes 3145736 | tf_op jit(solution)/shard_map/ppermute | solution.py:291
  78.3 67.0 %collective-permute-start.10 = (bf16[32,8192]{1,0:T(8,128)(2,1)S(1)}, bf16[32,8192]{1,0:T(8,128)(2,1)S(1)}, u32[]{:S(2)}, u32[]{:S(2)}) collective-permute-start(bf16[32,8192]{1,0:T(8,128)(2,1)S(1)} %constant_dynamic-slice_fusion.2), channel_id=1, source_target_pairs={{0,16},{16,0},{1,17},{17,1},{2,18},{18,2},{3,19},{19,3},{4,20},{20... | collective-permute-start | bytes 1572872 | tf_op jit(solution)/shard_map/ppermute | solution.py:291
  88.5 2.2 %copy-start = (bf16[32,65536]{1,0:T(8,128)(2,1)S(1)}, bf16[32,65536]{1,0:T(8,128)(2,1)}, u32[]{:S(2)}) copy-start(bf16[32,65536]{1,0:T(8,128)(2,1)} %own_ref.7) | copy-start | bytes 12582916
  92.7 41.8 %copy-start.2 = (bf16[32,65536]{1,0:T(8,128)(2,1)S(1)}, bf16[32,65536]{1,0:T(8,128)(2,1)}, u32[]{:S(2)}) copy-start(bf16[32,65536]{1,0:T(8,128)(2,1)} %own_ref.4) | copy-start | bytes 12582916
  94.2 51.1 %copy-start.1 = (bf16[32,65536]{1,0:T(8,128)(2,1)S(1)}, bf16[32,65536]{1,0:T(8,128)(2,1)}, u32[]{:S(2)}) copy-start(bf16[32,65536]{1,0:T(8,128)(2,1)} %own_ref.7) | copy-start | bytes 12582916

commit v3 on v2

--- a/solution.py
+++ b/solution.py
@@ -14,14 +14,17 @@
 LANES = 128
 
 MESSAGES = (
-    (0, 0, 2),
-    (0, 2, 4),
-    (0, 4, 8),
-    (1, 0, 4),
+    (0, 0, 3),
+    (0, 3, 6),
+    (0, 6, 8),
+    (1, 0, 1),
+    (1, 1, 4),
     (1, 4, 6),
     (1, 6, 8),
 )
-CALLS = ((0, 1, 2), (3,), (4,), (5,))
+READ = (0, 1, 2)
+SENT_GROUP = 1
+CALLS = ((0, 1, 2), (3, 4), (5,), (6,))
 
 
 def split(x):
@@ -42,63 +45,59 @@
     return by_high[:rows] + (second + third)
 
 
-def gather_kernel(slots, base_ref, index_ref, a_ref, b_ref, out_ref):
+def take_rows(slots, ref, wanted_rows):
     per = LANES // slots
-    step = pl.program_id(0)
-    width = out_ref.shape[2]
-    rows = a_ref.shape[0]
+    rows = ref.shape[0]
     place = lax.broadcasted_iota(jnp.int32, (rows, LANES), 1) // slots
-    for group, ref in enumerate((a_ref, b_ref)):
-        for q in range(width // LANES):
-            row = index_ref[group, pl.ds(step * (width // LANES) + q, 1), :]
-            wanted = jnp.broadcast_to(row, (rows, LANES))
-            acc = jnp.zeros((rows, LANES), jnp.float32)
-            for j in range(per):
-                start = (q * per + j) * LANES
-                block = ref[:, start : start + LANES].astype(jnp.float32)
-                taken = jnp.take_along_axis(block, wanted, axis=1, mode="promise_in_bounds")
-                acc = jnp.where(place == j, taken, acc)
-            out_ref[group, :, q * LANES : (q + 1) * LANES] = acc.astype(out_ref.dtype)
-
-
-def gather(state_a, state_b, index, base, slots, piece):
-    rows = state_a.shape[0]
+    for q, row in enumerate(wanted_rows):
+        wanted = jnp.broadcast_to(row, (rows, LANES))
+        acc = jnp.zeros((rows, LANES), jnp.float32)
+        for j in range(per):
+            start = (q * per + j) * LANES
+            block = ref[:, start : start + LANES].astype(jnp.float32)
+            taken = jnp.take_along_axis(block, wanted, axis=1, mode="promise_in_bounds")
+            acc = jnp.where(place == j, taken, acc)
+        yield q, acc
+
+
+def gather_kernel(slots, groups, base_ref, index_ref, *refs):
+    out_ref = refs[-1]
+    lines = out_ref.shape[2] // LANES
+    first = pl.program_id(0) * lines
+    for i, group in enumerate(groups):
+        rows = [index_ref[group, pl.ds(first + q, 1), :] for q in range(lines)]
+        for q, taken in take_rows(slots, refs[i], rows):
+            out_ref[i, :, q * LANES : (q + 1) * LANES] = taken.astype(out_ref.dtype)
+
+
+def gather(states, groups, index, base, slots, piece):
+    rows = states[0].shape[0]
     width = min(4096, piece)
     steps = piece // width
     observations = piece // LANES * slots
     state_spec = pl.BlockSpec((rows, width), lambda i, base: (0, base[0] * steps + i))
     return pl.pallas_call(
-        functools.partial(gather_kernel, slots),
-        out_shape=jax.ShapeDtypeStruct((2, rows, observations), jnp.bfloat16),
+        functools.partial(gather_kernel, slots, groups),
+        out_shape=jax.ShapeDtypeStruct((len(groups), rows, observations), jnp.bfloat16),
         grid_spec=pltpu.PrefetchScalarGridSpec(
             num_scalar_prefetch=1,
             grid=(steps,),
-            in_specs=[
-                pl.BlockSpec(index.shape, lambda i, base: (0, 0, 0)),
-                state_spec,
-                state_spec,
-            ],
-            out_specs=pl.BlockSpec((2, rows, observations // steps), lambda i, base: (0, 0, i)),
-        ),
-        compiler_params=pltpu.CompilerParams(dimension_semantics=("arbitrary",)),
+            in_specs=[pl.BlockSpec(index.shape, lambda i, base: (0, 0, 0))]
+            + [state_spec] * len(groups),
+            out_specs=pl.BlockSpec(
+                (len(groups), rows, observations // steps), lambda i, base: (0, 0, i)
+            ),
+        ),
+        compiler_params=pltpu.CompilerParams(dimension_semantics=("arbitrary",), vmem_limit_bytes=VMEM),
         name="gather",
-    )(base, index, state_a, state_b)
-
-
-def stats_kernel(parts, me_ref, *refs):
-    hx_refs = refs[:parts]
-    value_ref, weight_ref, live_ref, out_ref, all_ref = refs[parts:]
-    members = hx_refs[0].shape[1]
-    everyone = members * parts
-    me = me_ref[0]
-    for j in range(parts):
-        at = pl.multiple_of(lax.rem(me + j, parts) * members, members)
-        all_ref[pl.ds(at, members), :] = hx_refs[j][0].astype(jnp.float32)
-    hx = all_ref[...]
+    )(base, index, *[states[group] for group in groups])
+
+
+def add_statistics(hx, value, wt, live, total_ref, so_far_ref):
+    everyone = hx.shape[0]
     hmean = jnp.sum(hx, axis=0, keepdims=True) / everyone
     anomaly = hx - hmean
-    innov = value_ref[0] - hmean
-    wt = weight_ref[0]
+    innov = value - hmean
     scaled = anomaly * wt
     product = lax.dot_general(
         jnp.concatenate(split(scaled), axis=0),
@@ -114,40 +113,92 @@
     gram = term(0, 0) + (term(0, 1) + term(1, 0) + (term(0, 2) + term(2, 0) + term(1, 1)))
     cross = jnp.sum(scaled * innov, axis=1, keepdims=True)
     misfit = jnp.sum(wt * innov * innov, axis=1, keepdims=True)
-    total = jnp.sum(live_ref[0], axis=1, keepdims=True)
+    count = jnp.sum(live, axis=1, keepdims=True)
     lane = lax.broadcasted_iota(jnp.int32, (everyone, LANES - everyone), 1)
-    side = jnp.where(lane == 0, cross, jnp.where(lane == 1, misfit, jnp.where(lane == 2, total, 0.0)))
+    side = jnp.where(lane == 0, cross, jnp.where(lane == 1, misfit, jnp.where(lane == 2, count, 0.0)))
     new = jnp.concatenate([gram, side], axis=1)
-    first = (pl.program_id(0) == 0) & (pl.program_id(1) == 0)
-
-    @pl.when(first)
+
+    @pl.when(pl.program_id(0) == 0)
     def _():
-        out_ref[...] = new
-
-    @pl.when(jnp.logical_not(first))
+        total_ref[...] = new if so_far_ref is None else so_far_ref[...] + new
+
+    @pl.when(pl.program_id(0) > 0)
     def _():
-        out_ref[...] += new
-
-
-def statistics(parts, value, weight, live, me):
-    members, observations = parts[0].shape[1:]
-    everyone = members * len(parts)
-    width = min(1024, observations)
-    hx_spec = pl.BlockSpec((1, members, width), lambda g, i, me: (g, 0, i))
-    row_spec = pl.BlockSpec((1, 1, width), lambda g, i, me: (g, 0, i))
+        total_ref[...] += new
+
+
+def statistics_kernel(parts, slots, group, first, lines, started, me_ref, *refs):
+    part_refs = refs[:parts]
+    refs = refs[parts:]
+    value_ref, weight_ref, live_ref = refs[:3]
+    refs = refs[3:]
+    index_ref = None
+    if lines:
+        index_ref, *refs = refs
+    so_far_ref = None
+    if started:
+        so_far_ref, *refs = refs
+    total_ref, all_ref = refs
+    members = part_refs[0].shape[-2]
+    me = me_ref[0]
+
+    def place(j):
+        return pl.ds(pl.multiple_of(lax.rem(me + j, parts) * members, members), members)
+
+    all_ref[place(0), :] = part_refs[0][0].astype(jnp.float32)
+    for j in range(1, parts):
+        if not lines:
+            all_ref[place(j), :] = part_refs[j][0].astype(jnp.float32)
+            continue
+        at = first + pl.program_id(0) * lines
+        rows = [index_ref[group, pl.ds(at + q, 1), :] for q in range(lines)]
+        for q, taken in take_rows(slots, part_refs[j], rows):
+            all_ref[place(j), q * LANES : (q + 1) * LANES] = taken
+    add_statistics(
+        all_ref[...], value_ref[0], weight_ref[0], live_ref[0], total_ref, so_far_ref
+    )
+
+
+def statistics(own, others, value, weight, live, me, group, lo, hi, so_far, index=None, slots=0):
+    members = own.shape[1]
+    parts = 1 + len(others)
+    everyone = members * parts
+    if index is None:
+        width = math.gcd(hi - lo, 1024)
+        lines = 0
+        other_spec = pl.BlockSpec((1, members, width), lambda i, me: (0, 0, i))
+    else:
+        width = math.gcd(hi - lo, 512)
+        lines = width // LANES
+        other_spec = pl.BlockSpec(
+            (members, width // slots * LANES), lambda i, me: (0, i)
+        )
+    skip = lo // width
+    in_specs = [pl.BlockSpec((1, members, width), lambda i, me: (group, 0, skip + i))]
+    in_specs += [other_spec] * len(others)
+    in_specs += [pl.BlockSpec((1, 1, width), lambda i, me: (group, 0, skip + i))] * 3
+    operands = [own, *others, value, weight, live]
+    if index is not None:
+        in_specs.append(pl.BlockSpec(index.shape, lambda i, me: (0, 0, 0)))
+        operands.append(index)
+    if so_far is not None:
+        in_specs.append(pl.BlockSpec((everyone, LANES), lambda i, me: (0, 0)))
+        operands.append(so_far)
     return pl.pallas_call(
-        functools.partial(stats_kernel, len(parts)),
+        functools.partial(
+            statistics_kernel, parts, slots, group, lo // LANES, lines, so_far is not None
+        ),
         out_shape=jax.ShapeDtypeStruct((everyone, LANES), jnp.float32),
         grid_spec=pltpu.PrefetchScalarGridSpec(
             num_scalar_prefetch=1,
-            grid=(2, observations // width),
-            in_specs=[hx_spec] * len(parts) + [row_spec] * 3,
-            out_specs=pl.BlockSpec((everyone, LANES), lambda g, i, me: (0, 0)),
+            grid=((hi - lo) // width,),
+            in_specs=in_specs,
+            out_specs=pl.BlockSpec((everyone, LANES), lambda i, me: (0, 0)),
             scratch_shapes=[pltpu.VMEM((everyone, width), jnp.float32)],
         ),
-        compiler_params=pltpu.CompilerParams(dimension_semantics=("arbitrary", "arbitrary")),
+        compiler_params=pltpu.CompilerParams(dimension_semantics=("arbitrary",), vmem_limit_bytes=VMEM),
         name="statistics",
-    )(me, *parts, value, weight, live)
+    )(me, *operands)
 
 
 def transform_kernel(members, me_ref, stats_ref, transform_ref, mixer_ref, rest_ref):
@@ -309,9 +360,11 @@
         x.reshape(2, observations // LANES, LANES) for x in (obs_index, *others_index)
     )
 
-    own_hx = gather(state_a, state_b, index, me_ref, slots, piece)
+    own_hx = gather(states, (0, 1), index, me_ref, slots, piece)
     sent_hx = [
-        gather(state_a, state_b, idx, lax.rem(me_ref + nmem - shift, nmem), slots, piece)
+        gather(
+            states, (SENT_GROUP,), idx, lax.rem(me_ref + nmem - shift, nmem), slots, piece
+        )
         for idx, shift in zip(others_index, shifts)
     ]
     got_hx = [to_lower(x, shift) for x, shift in zip(sent_hx, shifts)]
@@ -322,15 +375,32 @@
     weight = (live * obs_weight).reshape(2, 1, observations)
     live = live.reshape(2, 1, observations)
     value = obs_value.reshape(2, 1, observations)
-    stats = statistics([own_hx, *got_hx], value, weight, live, me_ref)
-
-    received = []
-    for i, message in enumerate(MESSAGES):
-        if i < len(MESSAGES) - 1:
-            pieces = cut(message, states)
-        else:
-            pieces = cut(message, lax.optimization_barrier((*states, stats)))
-        received.append([to_lower(x, shift) for x, shift in zip(pieces, shifts)])
+
+    received = {}
+
+    def send(i, pieces):
+        received[i] = [to_lower(x, shift) for x, shift in zip(pieces, shifts)]
+
+    for i, message in enumerate(MESSAGES[:-1]):
+        pieces = cut(message, states)
+        send(i, pieces)
+
+    def read(i, so_far):
+        group, lo, hi = MESSAGES[i]
+        lo, hi = (x * observations // 8 for x in (lo, hi))
+        return statistics(
+            own_hx, received[i], value, weight, live, me_ref, group, lo, hi, so_far, index, slots
+        )
+
+    stats = read(READ[0], None)
+    stats = statistics(
+        own_hx, got_hx, value, weight, live, me_ref, SENT_GROUP, 0, observations, stats
+    )
+    for i in READ[1:]:
+        stats = read(i, stats)
+
+    pieces = cut(MESSAGES[-1], lax.optimization_barrier((*states, stats)))
+    send(len(MESSAGES) - 1, pieces)
 
     def all_sum(x, axis, size):
         step = 1

time: 148 us -> 141 us (0.953)
  waiting for transfers between devices: 72.5 us -> 62.4 us
  starting transfers between devices: 14.8 us -> 19.7 us
  local copies, waits for them, and re-layouts: 18 us -> 22 us
  Pallas kernels: 38.5 us -> 35.4 us
  other arithmetic: 2.2 us -> 0.07 us
    ppermute x7 -> x8, waiting for transfers between devices: 68.5 us -> 29.6 us  [to_lower(): lax.ppermute(array, 'mem', [(i, (i - shift) % nmem) for i in range(nmem)])]
    ppermute x5, waiting for transfers between devices: 4.04 us -> 23.8 us  [all_sum(): x = x + lax.ppermute(x, axis, [(i, i ^ step) for i in range(size)])]
    ppermute x1, waiting for transfers between devices: 0.01 us -> 9 us  [to_upper(): lax.ppermute(array, 'mem', [(i, (i + shift) % nmem) for i in range(nmem)])]
    ppermute x7 -> x8, starting transfers between devices: 5.37 us -> 11.3 us  [to_lower(): lax.ppermute(array, 'mem', [(i, (i - shift) % nmem) for i in range(nmem)])]
    pallas_call x3 -> x6, Pallas kernels: 20 us -> 15 us  [the longest x4 9.35 us: statistics(): pl.pallas_call(functools.partial(statistics_kernel, parts, slots, group,...]
    unnamed x10 -> x20, local copies, waits for them, and re-layouts: 4.74 us -> 9.72 us
    ppermute x1, starting transfers between devices: 3.03 us -> 0.02 us  [to_upper(): lax.ppermute(array, 'mem', [(i, (i + shift) % nmem) for i in range(nmem)])]
    ppermute x5, starting transfers between devices: 6.42 us -> 8.44 us  [all_sum(): x = x + lax.ppermute(x, axis, [(i, i ^ step) for i in range(size)])]
  transfers between devices with their start and end apart: 13 -> 14, of which waited for: 8 -> 7; matrix products, arithmetic and copies ran while one was open for 11% -> 8% of each run, Pallas kernels for 16% -> 24%
where the time goes in v3:
time: 141 us
  waiting for transfers between devices  62.4 us (44%)
  Pallas kernels  35.4 us (25%)
  local copies, waits for them, and re-layouts  22 us (16%)
  starting transfers between devices  19.7 us (14%)
    ppermute x8, waiting for transfers between devices, to_lower(): lax.ppermute(array, 'mem', [(i, (i - shift) % nmem) for i in range(nmem)])  29.6 us
    ppermute x5, waiting for transfers between devices, all_sum(): x = x + lax.ppermute(x, axis, [(i, i ^ step) for i in range(size)])  23.8 us
    ppermute x8, starting transfers between devices, to_lower(): lax.ppermute(array, 'mem', [(i, (i - shift) % nmem) for i in range(nmem)])  11.3 us
    pallas_call x4, Pallas kernels, analyse(): pl.pallas_call(functools.partial(analysis_kernel, bounds, len(received) /...  10.6 us
    pallas_call x1, Pallas kernels, make_transform(): pl.pallas_call(functools.partial(transform_kernel, members), out_shape=(j...  9.84 us
    unnamed x20, local copies, waits for them, and re-layouts  9.72 us
    pallas_call x4, Pallas kernels, statistics(): pl.pallas_call(functools.partial(statistics_kernel, parts, slots, group,...  9.35 us
    ppermute x1, waiting for transfers between devices, to_upper(): lax.ppermute(array, 'mem', [(i, (i + shift) % nmem) for i in range(nmem)])  9 us
  transfers between devices with their start and end apart: 14, of which 7 were waited for; matrix products, arithmetic and copies ran while one was open for 8% of the time, Pallas kernels for 24%

profile of v3, /device:TPU:0, one launch (start us, length us, event | category | flops | bytes accessed | tf_op | source)
XLA Modules:
  0.0 140.6 jit_solution(15503241910641189991)
XLA Ops:
  0.7 2.6 %constant_dynamic-slice_fusion.4 = (bf16[32,12288]{1,0:T(8,128)(2,1)}, bf16[32,12288]{1,0:T(8,128)(2,1)}) fusion(bf16[32,65536]{1,0:T(8,128)(2,1)} %own_ref.4, s32[]{:T(128)S(6)} %select_n.19, s32[]{:T(128)S(6)} %select_n.18), kind=kLoop, calls=%fused_computation.7 | loop fusion | bytes 3145736 | tf_op jit(solution)/shard_map/dynamic_slice | solution.py:350
  3.3 3.0 %collective-permute-start.4 = (bf16[32,12288]{1,0:T(8,128)(2,1)}, bf16[32,12288]{1,0:T(8,128)(2,1)S(1)}, u32[]{:S(2)}, u32[]{:S(2)}) collective-permute-start(bf16[32,12288]{1,0:T(8,128)(2,1)} %get-tuple-element.11), channel_id=1, source_target_pairs={{0,16},{16,0},{1,17},{17,1},{2,18},{18,2},{3,19},{19,3},{4,20},{20... | collective-permute-start | bytes 2359304 | tf_op jit(solution)/shard_map/ppermute | solution.py:342
  6.3 2.0 %collective-permute-start.1 = (bf16[32,12288]{1,0:T(8,128)(2,1)}, bf16[32,12288]{1,0:T(8,128)(2,1)S(1)}, u32[]{:S(2)}, u32[]{:S(2)}) collective-permute-start(bf16[32,12288]{1,0:T(8,128)(2,1)} %get-tuple-element.12), channel_id=1, source_target_pairs={{0,16},{16,0},{1,17},{17,1},{2,18},{18,2},{3,19},{19,3},{4,20},{20... | collective-permute-start | bytes 2359304 | tf_op jit(solution)/shard_map/ppermute | solution.py:342
  8.3 1.9 %constant_dynamic-slice_fusion.6 = bf16[32,8192]{1,0:T(8,128)(2,1)} fusion(bf16[32,65536]{1,0:T(8,128)(2,1)} %own_ref.4, s32[]{:T(128)S(6)} %select_n.17), kind=kLoop, calls=%fused_computation.9 | loop fusion | bytes 1048580 | tf_op jit(solution)/shard_map/dynamic_slice | solution.py:350
  10.2 2.1 %constant_dynamic-slice_fusion = bf16[32,12288]{1,0:T(8,128)(2,1)} fusion(bf16[32,65536]{1,0:T(8,128)(2,1)} %own_ref.7, s32[]{:T(128)S(6)} %select_n.21), kind=kLoop, calls=%fused_computation.3 | loop fusion | bytes 1572868 | tf_op jit(solution)/shard_map/dynamic_slice | solution.py:350
  12.3 2.0 %collective-permute-start.13 = (bf16[32,12288]{1,0:T(8,128)(2,1)}, bf16[32,12288]{1,0:T(8,128)(2,1)S(1)}, u32[]{:S(2)}, u32[]{:S(2)}) collective-permute-start(bf16[32,12288]{1,0:T(8,128)(2,1)} %constant_dynamic-slice_fusion), channel_id=1, source_target_pairs={{0,16},{16,0},{1,17},{17,1},{2,18},{18,2},{3,19},{19,3},{4,20},{20... | collective-permute-start | bytes 2359304 | tf_op jit(solution)/shard_map/ppermute | solution.py:342
  14.3 1.9 %constant_dynamic-slice_fusion.2 = bf16[32,8192]{1,0:T(8,128)(2,1)} fusion(bf16[32,65536]{1,0:T(8,128)(2,1)} %own_ref.7, s32[]{:T(128)S(6)} %select_n.20), kind=kLoop, calls=%fused_computation.5 | loop fusion | bytes 1048580 | tf_op jit(solution)/shard_map/dynamic_slice | solution.py:350
  16.5 9.0 %collective-permute-done.2 = s32[2,256,16]{1,2,0:T(8,128)S(1)} collective-permute-done((s32[2,256,16]{1,2,0:T(8,128)}, s32[2,256,16]{1,2,0:T(8,128)S(1)}, u32[]{:S(2)}, u32[]{:S(2)}) %collective-permute-start.2) | collective-permute-done | bytes 32800 | tf_op jit(solution)/shard_map/ppermute | solution.py:345
  25.8 2.2 %copy-done = bf16[32,65536]{1,0:T(8,128)(2,1)S(1)} copy-done((bf16[32,65536]{1,0:T(8,128)(2,1)S(1)}, bf16[32,65536]{1,0:T(8,128)(2,1)}, u32[]{:S(2)}) %copy-start) | copy-done | bytes 4194328
  28.0 3.3 %gather.3 = bf16[1,32,4096]{2,1,0:T(8,128)(2,1)} custom-call(s32[1]{0:T(128)S(6)} %rem.43.base_ref, s32[2,32,128]{2,1,0:T(8,128)S(1)} %reshape.62.index_ref, bf16[32,65536]{1,0:T(8,128)(2,1)S(1)} %copy-done), custom_call_target="tpu_custom_call" | custom-call | tf_op jit(solution)/shard_map/gather/pallas_call | solution.py:79
  31.3 2.0 %collective-permute-start.3 = (bf16[1,32,4096]{2,1,0:T(8,128)(2,1)}, bf16[1,32,4096]{2,1,0:T(8,128)(2,1)}, u32[]{:S(2)}, u32[]{:S(2)}) collective-permute-start(bf16[1,32,4096]{2,1,0:T(8,128)(2,1)} %gather.3), channel_id=1, source_target_pairs={{0,16},{16,0},{1,17},{17,1},{2,18},{18,2},{3,19},{19,3},{4,20},{20... | collective-permute-start | bytes 786440 | tf_op jit(solution)/shard_map/ppermute | solution.py:342
  33.7 2.2 %copy-done.1 = bf16[32,65536]{1,0:T(8,128)(2,1)S(1)} copy-done((bf16[32,65536]{1,0:T(8,128)(2,1)S(1)}, bf16[32,65536]{1,0:T(8,128)(2,1)}, u32[]{:S(2)}) %copy-start.1) | copy-done | bytes 4194328
  35.8 2.2 %copy-done.3 = bf16[32,65536]{1,0:T(8,128)(2,1)S(1)} copy-done((bf16[32,65536]{1,0:T(8,128)(2,1)S(1)}, bf16[32,65536]{1,0:T(8,128)(2,1)}, u32[]{:S(2)}) %copy-start.3) | copy-done | bytes 4194328
  38.0 2.3 %gather.2.refs_0_ = bf16[2,32,4096]{2,1,0:T(8,128)(2,1)S(1)} custom-call(s32[1]{0:T(128)} %bitcast.base_ref.me_ref, s32[2,32,128]{2,1,0:T(8,128)S(1)} %reshape.59.index_ref.refs_5_, bf16[32,65536]{1,0:T(8,128)(2,1)S(1)} %copy-done.3, bf16[32,65536]{1,0:T(8,128)(2,1)S(1)} %copy-done.1), custom_call_target="tpu_custom_call" | custom-call | tf_op jit(solution)/shard_map/gather/pallas_call | solution.py:79
  44.4 2.2 %statistics.4.refs_5_ = f32[64,128]{1,0:T(8,128)S(1)} custom-call(s32[1]{0:T(128)} %bitcast.base_ref.me_ref, bf16[2,32,4096]{2,1,0:T(8,128)(2,1)S(1)} %gather.2.refs_0_, bf16[32,12288]{1,0:T(8,128)(2,1)S(1)} %collective-permute-done.4.refs_1_.refs_0_, f32[2,1,4096]{2,1,0:T(1,128)S(1)} %reshape.63.refs_2_, f32[2,1,4096]{2,1,0:T(1,128)S(1)} %reshape.64.refs_3_, ...), custom_call_target="tpu_custom_call" | custom-call | tf_op jit(solution)/shard_map/statistics/pallas_call | solution.py:187
  46.6 29.6 %collective-permute-done.3.refs_1_ = bf16[1,32,4096]{2,1,0:T(8,128)(2,1)} collective-permute-done((bf16[1,32,4096]{2,1,0:T(8,128)(2,1)}, bf16[1,32,4096]{2,1,0:T(8,128)(2,1)}, u32[]{:S(2)}, u32[]{:S(2)}) %collective-permute-start.3) | collective-permute-done | bytes 262176 | tf_op jit(solution)/shard_map/ppermute | solution.py:342
  76.2 3.4 %statistics.5.refs_6_ = f32[64,128]{1,0:T(8,128)S(1)} custom-call(s32[1]{0:T(128)} %bitcast.base_ref.me_ref, bf16[2,32,4096]{2,1,0:T(8,128)(2,1)S(1)} %gather.2.refs_0_, bf16[1,32,4096]{2,1,0:T(8,128)(2,1)} %collective-permute-done.3.refs_1_, f32[2,1,4096]{2,1,0:T(1,128)S(1)} %reshape.63.refs_2_, f32[2,1,4096]{2,1,0:T(1,128)S(1)} %reshape.64.refs_3_, ...), custom_call_target="tpu_custom_call" | custom-call | tf_op jit(solution)/shard_map/statistics/pallas_call | solution.py:187
  79.6 2.2 %statistics.6.refs_6_ = f32[64,128]{1,0:T(8,128)S(1)} custom-call(s32[1]{0:T(128)} %bitcast.base_ref.me_ref, bf16[2,32,4096]{2,1,0:T(8,128)(2,1)S(1)} %gather.2.refs_0_, bf16[32,12288]{1,0:T(8,128)(2,1)S(1)} %collective-permute-done.1.refs_1_, f32[2,1,4096]{2,1,0:T(1,128)S(1)} %reshape.63.refs_2_, f32[2,1,4096]{2,1,0:T(1,128)S(1)} %reshape.64.refs_3_, ...), custom_call_target="tpu_custom_call" | custom-call | tf_op jit(solution)/shard_map/statistics/pallas_call | solution.py:187
  81.9 1.5 %statistics.7 = f32[64,128]{1,0:T(8,128)S(1)} custom-call(s32[1]{0:T(128)} %bitcast.base_ref.me_ref, bf16[2,32,4096]{2,1,0:T(8,128)(2,1)S(1)} %gather.2.refs_0_, bf16[32,8192]{1,0:T(8,128)(2,1)S(1)} %collective-permute-done.refs_1_.refs_2_, f32[2,1,4096]{2,1,0:T(1,128)S(1)} %reshape.63.refs_2_, f32[2,1,4096]{2,1,0:T(1,128)S(1)} %reshape.64.refs_3_, ...), custom_call_target="tpu_custom_call" | custom-call | tf_op jit(solution)/shard_map/statistics/pallas_call | solution.py:187
  83.4 2.1 %collective-permute-start.10 = (bf16[32,8192]{1,0:T(8,128)(2,1)S(1)}, bf16[32,8192]{1,0:T(8,128)(2,1)S(1)}, u32[]{:S(2)}, u32[]{:S(2)}) collective-permute-start(bf16[32,8192]{1,0:T(8,128)(2,1)S(1)} %constant_dynamic-slice_fusion.3), channel_id=1, source_target_pairs={{0,16},{16,0},{1,17},{17,1},{2,18},{18,2},{3,19},{19,3},{4,20},{20... | collective-permute-start | bytes 1572872 | tf_op jit(solution)/shard_map/ppermute | solution.py:342
  85.6 2.0 %collective-permute-start.5 = (f32[64,128]{1,0:T(8,128)S(1)}, f32[64,128]{1,0:T(8,128)S(1)}, u32[]{:S(2)}, u32[]{:S(2)}) collective-permute-start(f32[64,128]{1,0:T(8,128)S(1)} %statistics.7), channel_id=1, source_target_pairs={{0,16},{16,0},{1,17},{17,1},{2,18},{18,2},{3,19},{19,3},{4,20},{20... | collective-permute-start | bytes 98312 | tf_op jit(solution)/shard_map/ppermute | solution.py:408
  87.6 16.4 %collective-permute-done.5 = f32[64,128]{1,0:T(8,128)S(1)} collective-permute-done((f32[64,128]{1,0:T(8,128)S(1)}, f32[64,128]{1,0:T(8,128)S(1)}, u32[]{:S(2)}, u32[]{:S(2)}) %collective-permute-start.5) | collective-permute-done | bytes 32800 | tf_op jit(solution)/shard_map/ppermute | solution.py:408
  105.3 1.8 %collective-permute-start.7 = (f32[64,128]{1,0:T(8,128)S(1)}, f32[64,128]{1,0:T(8,128)S(1)}, u32[]{:S(2)}, u32[]{:S(2)}) collective-permute-start(f32[64,128]{1,0:T(8,128)S(1)} %add.73), channel_id=1, source_target_pairs={{0,2},{1,3},{2,0},{3,1},{4,6},{5,7},{6,4},{7,5},{8,10},{9,11},{10,... | collective-permute-start | bytes 98312 | tf_op jit(solution)/shard_map/ppermute | solution.py:408
  107.0 2.1 %collective-permute-done.7 = f32[64,128]{1,0:T(8,128)S(1)} collective-permute-done((f32[64,128]{1,0:T(8,128)S(1)}, f32[64,128]{1,0:T(8,128)S(1)}, u32[]{:S(2)}, u32[]{:S(2)}) %collective-permute-start.7) | collective-permute-done | bytes 32800 | tf_op jit(solution)/shard_map/ppermute | solution.py:408
  109.2 1.8 %collective-permute-start.8 = (f32[64,128]{1,0:T(8,128)S(1)}, f32[64,128]{1,0:T(8,128)S(1)}, u32[]{:S(2)}, u32[]{:S(2)}) collective-permute-start(f32[64,128]{1,0:T(8,128)S(1)} %add.74), channel_id=1, source_target_pairs={{0,4},{1,5},{2,6},{3,7},{4,0},{5,1},{6,2},{7,3},{8,12},{9,13},{10,... | collective-permute-start | bytes 98312 | tf_op jit(solution)/shard_map/ppermute | solution.py:408
  111.0 2.1 %collective-permute-done.8 = f32[64,128]{1,0:T(8,128)S(1)} collective-permute-done((f32[64,128]{1,0:T(8,128)S(1)}, f32[64,128]{1,0:T(8,128)S(1)}, u32[]{:S(2)}, u32[]{:S(2)}) %collective-permute-start.8) | collective-permute-done | bytes 32800 | tf_op jit(solution)/shard_map/ppermute | solution.py:408
  113.1 2.8 %collective-permute-start.9 = (f32[64,128]{1,0:T(8,128)S(1)}, f32[64,128]{1,0:T(8,128)S(1)}, u32[]{:S(2)}, u32[]{:S(2)}) collective-permute-start(f32[64,128]{1,0:T(8,128)S(1)} %add.75), channel_id=1, source_target_pairs={{0,8},{1,9},{2,10},{3,11},{4,12},{5,13},{6,14},{7,15},{8,0},{9,1},... | collective-permute-start | bytes 98312 | tf_op jit(solution)/shard_map/ppermute | solution.py:408
  115.9 2.0 %collective-permute-done.9 = f32[64,128]{1,0:T(8,128)S(1)} collective-permute-done((f32[64,128]{1,0:T(8,128)S(1)}, f32[64,128]{1,0:T(8,128)S(1)}, u32[]{:S(2)}, u32[]{:S(2)}) %collective-permute-start.9) | collective-permute-done | bytes 32800 | tf_op jit(solution)/shard_map/ppermute | solution.py:408
  117.9 9.8 %transform.1 = (f32[64,64]{1,0:T(8,128)}, bf16[80,64]{1,0:T(8,128)(2,1)S(1)}, f32[64,128]{1,0:T(8,128)S(1)}) custom-call(s32[1]{0:T(128)} %bitcast.base_ref.me_ref, f32[64,128]{1,0:T(8,128)S(1)} %add.76.stats_ref), custom_call_target="tpu_custom_call" | custom-call | tf_op jit(solution)/shard_map/transform/pallas_call | solution.py:250
  127.8 2.2 %copy-done.4 = bf16[32,65536]{1,0:T(8,128)(2,1)S(1)} copy-done((bf16[32,65536]{1,0:T(8,128)(2,1)S(1)}, bf16[32,65536]{1,0:T(8,128)(2,1)}, u32[]{:S(2)}) %copy-start.4) | copy-done | bytes 4194328
  130.0 5.0 %analysis.4 = bf16[64,32768]{1,0:T(8,128)(2,1)} custom-call(s32[1]{0:T(128)} %bitcast.base_ref.me_ref, bf16[80,64]{1,0:T(8,128)(2,1)S(1)} %get-tuple-element.7.mixer_ref, f32[64,128]{1,0:T(8,128)S(1)} %get-tuple-element.8.rest_ref, bf16[32,65536]{1,0:T(8,128)(2,1)S(1)} %copy-done.4, bf16[32,12288]{1,0:T(8,128)(2,1)S(1)} %collective-permute-done.4.refs_1_.refs_0_, ...), custom_call_target="tpu_custom_call" | custom-call | tf_op jit(solution)/shard_map/analysis/pallas_call | solution.py:308
  134.9 2.7 %analysis.5.refs_1_ = bf16[64,32768]{1,0:T(8,128)(2,1)} custom-call(s32[1]{0:T(128)} %bitcast.base_ref.me_ref, bf16[80,64]{1,0:T(8,128)(2,1)S(1)} %get-tuple-element.7.mixer_ref, f32[64,128]{1,0:T(8,128)S(1)} %get-tuple-element.8.rest_ref, bf16[32,65536]{1,0:T(8,128)(2,1)S(1)} %copy-done.2, bf16[32,4096]{1,0:T(8,128)(2,1)S(1)} %collective-permute-done.12.refs_0_, ...), custom_call_target="tpu_custom_call" | custom-call | tf_op jit(solution)/shard_map/analysis/pallas_call | solution.py:308
  (50 shorter events, 9.3 us)
Async XLA Ops:
  0.6 15.5 %copy-start.8 = (s32[2,256]{1,0:T(2,128)S(1)}, s32[2,256]{1,0:T(2,128)}, u32[]{:S(2)}) copy-start(s32[2,256]{1,0:T(2,128)} %param.9) | copy-start | bytes 6148
  3.3 41.0 %collective-permute-start.4 = (bf16[32,12288]{1,0:T(8,128)(2,1)}, bf16[32,12288]{1,0:T(8,128)(2,1)S(1)}, u32[]{:S(2)}, u32[]{:S(2)}) collective-permute-start(bf16[32,12288]{1,0:T(8,128)(2,1)} %get-tuple-element.11), channel_id=1, source_target_pairs={{0,16},{16,0},{1,17},{17,1},{2,18},{18,2},{3,19},{19,3},{4,20},{20... | collective-permute-start | bytes 2359304 | tf_op jit(solution)/shard_map/ppermute | solution.py:342
  6.2 19.3 %collective-permute-start.2 = (s32[2,256,16]{1,2,0:T(8,128)}, s32[2,256,16]{1,2,0:T(8,128)S(1)}, u32[]{:S(2)}, u32[]{:S(2)}) collective-permute-start(s32[2,256,16]{1,2,0:T(8,128)} %param.8), channel_id=1, source_target_pairs={{0,16},{16,0},{1,17},{17,1},{2,18},{18,2},{3,19},{19,3},{4,20},{20... | collective-permute-start | bytes 98312 | tf_op jit(solution)/shard_map/ppermute | solution.py:345
  6.3 73.3 %collective-permute-start.1 = (bf16[32,12288]{1,0:T(8,128)(2,1)}, bf16[32,12288]{1,0:T(8,128)(2,1)S(1)}, u32[]{:S(2)}, u32[]{:S(2)}) collective-permute-start(bf16[32,12288]{1,0:T(8,128)(2,1)} %get-tuple-element.12), channel_id=1, source_target_pairs={{0,16},{16,0},{1,17},{17,1},{2,18},{18,2},{3,19},{19,3},{4,20},{20... | collective-permute-start | bytes 2359304 | tf_op jit(solution)/shard_map/ppermute | solution.py:342
  10.2 71.7 %collective-permute-start = (bf16[32,8192]{1,0:T(8,128)(2,1)}, bf16[32,8192]{1,0:T(8,128)(2,1)S(1)}, u32[]{:S(2)}, u32[]{:S(2)}) collective-permute-start(bf16[32,8192]{1,0:T(8,128)(2,1)} %constant_dynamic-slice_fusion.6), channel_id=1, source_target_pairs={{0,16},{16,0},{1,17},{17,1},{2,18},{18,2},{3,19},{19,3},{4,20},{20... | collective-permute-start | bytes 1572872 | tf_op jit(solution)/shard_map/ppermute | solution.py:342
  10.2 23.2 %copy-start.5 = (s32[2,256,16]{1,2,0:T(8,128)S(1)}, s32[2,256,16]{1,2,0:T(8,128)}, u32[]{:S(2)}) copy-start(s32[2,256,16]{1,2,0:T(8,128)} %param.8) | copy-start | bytes 98308
  12.3 122.7 %collective-permute-start.13 = (bf16[32,12288]{1,0:T(8,128)(2,1)}, bf16[32,12288]{1,0:T(8,128)(2,1)S(1)}, u32[]{:S(2)}, u32[]{:S(2)}) collective-permute-start(bf16[32,12288]{1,0:T(8,128)(2,1)} %constant_dynamic-slice_fusion), channel_id=1, source_target_pairs={{0,16},{16,0},{1,17},{17,1},{2,18},{18,2},{3,19},{19,3},{4,20},{20... | collective-permute-start | bytes 2359304 | tf_op jit(solution)/shard_map/ppermute | solution.py:342
  25.8 2.2 %copy-start = (bf16[32,65536]{1,0:T(8,128)(2,1)S(1)}, bf16[32,65536]{1,0:T(8,128)(2,1)}, u32[]{:S(2)}) copy-start(bf16[32,65536]{1,0:T(8,128)(2,1)} %own_ref.7) | copy-start | bytes 12582916
  31.3 44.9 %collective-permute-start.3 = (bf16[1,32,4096]{2,1,0:T(8,128)(2,1)}, bf16[1,32,4096]{2,1,0:T(8,128)(2,1)}, u32[]{:S(2)}, u32[]{:S(2)}) collective-permute-start(bf16[1,32,4096]{2,1,0:T(8,128)(2,1)} %gather.3), channel_id=1, source_target_pairs={{0,16},{16,0},{1,17},{17,1},{2,18},{18,2},{3,19},{19,3},{4,20},{20... | collective-permute-start | bytes 786440 | tf_op jit(solution)/shard_map/ppermute | solution.py:342
  33.7 2.2 %copy-start.1 = (bf16[32,65536]{1,0:T(8,128)(2,1)S(1)}, bf16[32,65536]{1,0:T(8,128)(2,1)}, u32[]{:S(2)}) copy-start(bf16[32,65536]{1,0:T(8,128)(2,1)} %own_ref.7) | copy-start | bytes 12582916
  35.8 2.2 %copy-start.3 = (bf16[32,65536]{1,0:T(8,128)(2,1)S(1)}, bf16[32,65536]{1,0:T(8,128)(2,1)}, u32[]{:S(2)}) copy-start(bf16[32,65536]{1,0:T(8,128)(2,1)} %own_ref.4) | copy-start | bytes 12582916
  38.0 2.3 %copy-start.7 = (f32[2,256,16]{1,2,0:T(8,128)S(1)}, f32[2,256,16]{1,2,0:T(8,128)}, u32[]{:S(2)}) copy-start(f32[2,256,16]{1,2,0:T(8,128)} %param.11) | copy-start | bytes 98308
  38.0 4.3 %copy-start.6 = (f32[2,256,16]{1,2,0:T(8,128)S(1)}, f32[2,256,16]{1,2,0:T(8,128)}, u32[]{:S(2)}) copy-start(f32[2,256,16]{1,2,0:T(8,128)} %param.10) | copy-start | bytes 98308
  44.3 39.1 %copy-start.2 = (bf16[32,65536]{1,0:T(8,128)(2,1)S(1)}, bf16[32,65536]{1,0:T(8,128)(2,1)}, u32[]{:S(2)}) copy-start(bf16[32,65536]{1,0:T(8,128)(2,1)} %own_ref.7) | copy-start | bytes 12582916
  44.3 93.3 %collective-permute-start.11 = (bf16[32,8192]{1,0:T(8,128)(2,1)}, bf16[32,8192]{1,0:T(8,128)(2,1)S(1)}, u32[]{:S(2)}, u32[]{:S(2)}) collective-permute-start(bf16[32,8192]{1,0:T(8,128)(2,1)} %constant_dynamic-slice_fusion.2), channel_id=1, source_target_pairs={{0,16},{16,0},{1,17},{17,1},{2,18},{18,2},{3,19},{19,3},{4,20},{20... | collective-permute-start | bytes 1572872 | tf_op jit(solution)/shard_map/ppermute | solution.py:342
  83.4 55.7 %collective-permute-start.10 = (bf16[32,8192]{1,0:T(8,128)(2,1)S(1)}, bf16[32,8192]{1,0:T(8,128)(2,1)S(1)}, u32[]{:S(2)}, u32[]{:S(2)}) collective-permute-start(bf16[32,8192]{1,0:T(8,128)(2,1)S(1)} %constant_dynamic-slice_fusion.3), channel_id=1, source_target_pairs={{0,16},{16,0},{1,17},{17,1},{2,18},{18,2},{3,19},{19,3},{4,20},{20... | collective-permute-start | bytes 1572872 | tf_op jit(solution)/shard_map/ppermute | solution.py:342
  85.5 49.4 %collective-permute-start.12 = (bf16[32,4096]{1,0:T(8,128)(2,1)S(1)}, bf16[32,4096]{1,0:T(8,128)(2,1)S(1)}, u32[]{:S(2)}, u32[]{:S(2)}) collective-permute-start(bf16[32,4096]{1,0:T(8,128)(2,1)S(1)} %constant_dynamic-slice_fusion.1), channel_id=1, source_target_pairs={{0,16},{16,0},{1,17},{17,1},{2,18},{18,2},{3,19},{19,3},{4,20},{20... | collective-permute-start | bytes 786440 | tf_op jit(solution)/shard_map/ppermute | solution.py:342
  85.6 18.4 %collective-permute-start.5 = (f32[64,128]{1,0:T(8,128)S(1)}, f32[64,128]{1,0:T(8,128)S(1)}, u32[]{:S(2)}, u32[]{:S(2)}) collective-permute-start(f32[64,128]{1,0:T(8,128)S(1)} %statistics.7), channel_id=1, source_target_pairs={{0,16},{16,0},{1,17},{17,1},{2,18},{18,2},{3,19},{19,3},{4,20},{20... | collective-permute-start | bytes 98312 | tf_op jit(solution)/shard_map/ppermute | solution.py:408
  104.0 1.2 collective-permute-start.6
  105.3 3.9 %collective-permute-start.7 = (f32[64,128]{1,0:T(8,128)S(1)}, f32[64,128]{1,0:T(8,128)S(1)}, u32[]{:S(2)}, u32[]{:S(2)}) collective-permute-start(f32[64,128]{1,0:T(8,128)S(1)} %add.73), channel_id=1, source_target_pairs={{0,2},{1,3},{2,0},{3,1},{4,6},{5,7},{6,4},{7,5},{8,10},{9,11},{10,... | collective-permute-start | bytes 98312 | tf_op jit(solution)/shard_map/ppermute | solution.py:408
  109.2 3.9 %collective-permute-start.8 = (f32[64,128]{1,0:T(8,128)S(1)}, f32[64,128]{1,0:T(8,128)S(1)}, u32[]{:S(2)}, u32[]{:S(2)}) collective-permute-start(f32[64,128]{1,0:T(8,128)S(1)} %add.74), channel_id=1, source_target_pairs={{0,4},{1,5},{2,6},{3,7},{4,0},{5,1},{6,2},{7,3},{8,12},{9,13},{10,... | collective-permute-start | bytes 98312 | tf_op jit(solution)/shard_map/ppermute | solution.py:408
  113.1 4.8 %collective-permute-start.9 = (f32[64,128]{1,0:T(8,128)S(1)}, f32[64,128]{1,0:T(8,128)S(1)}, u32[]{:S(2)}, u32[]{:S(2)}) collective-permute-start(f32[64,128]{1,0:T(8,128)S(1)} %add.75), channel_id=1, source_target_pairs={{0,8},{1,9},{2,10},{3,11},{4,12},{5,13},{6,14},{7,15},{8,0},{9,1},... | collective-permute-start | bytes 98312 | tf_op jit(solution)/shard_map/ppermute | solution.py:408
  127.8 2.2 %copy-start.4 = (bf16[32,65536]{1,0:T(8,128)(2,1)S(1)}, bf16[32,65536]{1,0:T(8,128)(2,1)}, u32[]{:S(2)}) copy-start(bf16[32,65536]{1,0:T(8,128)(2,1)} %own_ref.4) | copy-start | bytes 12582916

commit v4 on v3

--- a/solution.py
+++ b/solution.py
@@ -11,20 +11,23 @@
 
 ITERS = 24
 VMEM = 16 * 1024 * 1024
+MOST_VMEM = 50 * 1024 * 1024
 LANES = 128
 
 MESSAGES = (
-    (0, 0, 3),
-    (0, 3, 6),
+    (0, 0, 2),
+    (0, 2, 4),
+    (0, 4, 6),
     (0, 6, 8),
     (1, 0, 1),
-    (1, 1, 4),
-    (1, 4, 6),
-    (1, 6, 8),
+    (1, 1, 2),
+    (1, 2, 5),
+    (1, 5, 7),
+    (1, 7, 8),
 )
-READ = (0, 1, 2)
-SENT_GROUP = 1
-CALLS = ((0, 1, 2), (3, 4), (5,), (6,))
+READ = (0, 1, 2, 3, 4)
+SENT = (1, 1)
+CALLS = ((0, 1, 2, 3), (4, 5, 6), (7,), (8,))
 
 
 def split(x):
@@ -43,6 +46,29 @@
     second = by_high[rows : 2 * rows] + by_middle[:rows]
     third = by_high[2 * rows :] + by_middle[rows:] + by_low
     return by_high[:rows] + (second + third)
+
+
+def cut_kernel(base_ref, state_ref, out_ref):
+    out_ref[...] = state_ref[...]
+
+
+def cut_first(state, base, lo, hi, piece):
+    members, length = state.shape[0], hi - lo
+    whole = piece // length
+    return pl.pallas_call(
+        cut_kernel,
+        out_shape=jax.ShapeDtypeStruct((members, length), state.dtype),
+        grid_spec=pltpu.PrefetchScalarGridSpec(
+            num_scalar_prefetch=1,
+            grid=(1,),
+            in_specs=[
+                pl.BlockSpec((members, length), lambda i, base: (0, base[0] * whole + lo // length))
+            ],
+            out_specs=pl.BlockSpec(memory_space=pltpu.VMEM),
+        ),
+        compiler_params=pltpu.CompilerParams(vmem_limit_bytes=MOST_VMEM),
+        name="cut",
+    )(base, state)
 
 
 def take_rows(slots, ref, wanted_rows):
@@ -60,24 +86,24 @@
         yield q, acc
 
 
-def gather_kernel(slots, groups, base_ref, index_ref, *refs):
+def gather_kernel(slots, groups, skip, base_ref, index_ref, *refs):
     out_ref = refs[-1]
     lines = out_ref.shape[2] // LANES
-    first = pl.program_id(0) * lines
+    first = (skip + pl.program_id(0)) * lines
     for i, group in enumerate(groups):
         rows = [index_ref[group, pl.ds(first + q, 1), :] for q in range(lines)]
         for q, taken in take_rows(slots, refs[i], rows):
             out_ref[i, :, q * LANES : (q + 1) * LANES] = taken.astype(out_ref.dtype)
 
 
-def gather(states, groups, index, base, slots, piece):
+def gather(states, groups, index, base, slots, piece, eighth=0):
     rows = states[0].shape[0]
-    width = min(4096, piece)
-    steps = piece // width
-    observations = piece // LANES * slots
-    state_spec = pl.BlockSpec((rows, width), lambda i, base: (0, base[0] * steps + i))
+    width = piece // 8
+    steps = 8 - eighth
+    observations = width // LANES * slots * steps
+    state_spec = pl.BlockSpec((rows, width), lambda i, base: (0, base[0] * 8 + eighth + i))
     return pl.pallas_call(
-        functools.partial(gather_kernel, slots, groups),
+        functools.partial(gather_kernel, slots, groups, eighth),
         out_shape=jax.ShapeDtypeStruct((len(groups), rows, observations), jnp.bfloat16),
         grid_spec=pltpu.PrefetchScalarGridSpec(
             num_scalar_prefetch=1,
@@ -164,11 +190,11 @@
     parts = 1 + len(others)
     everyone = members * parts
     if index is None:
-        width = math.gcd(hi - lo, 1024)
+        width = math.gcd(math.gcd(lo, hi), 1024)
         lines = 0
         other_spec = pl.BlockSpec((1, members, width), lambda i, me: (0, 0, i))
     else:
-        width = math.gcd(hi - lo, 512)
+        width = math.gcd(math.gcd(lo, hi), 512)
         lines = width // LANES
         other_spec = pl.BlockSpec(
             (members, width // slots * LANES), lambda i, me: (0, i)
@@ -288,7 +314,7 @@
     first, last = messages[0][0], messages[-1][1]
     width = 2 * piece // 8
     for lo, hi, _ in messages:
-        width = math.gcd(width, hi - lo)
+        width = math.gcd(width, lo, hi)
     skip = first // width
     whole = piece // width
     bounds = tuple((lo // width - skip, hi // width - skip) for lo, hi, _ in messages)
@@ -360,11 +386,14 @@
         x.reshape(2, observations // LANES, LANES) for x in (obs_index, *others_index)
     )
 
+    group, lo, hi = MESSAGES[0]
+    first_pieces = [
+        cut_first(states[group], lax.rem(me_ref + nmem - shift, nmem), lo * unit, hi * unit, piece)
+        for shift in shifts
+    ]
     own_hx = gather(states, (0, 1), index, me_ref, slots, piece)
     sent_hx = [
-        gather(
-            states, (SENT_GROUP,), idx, lax.rem(me_ref + nmem - shift, nmem), slots, piece
-        )
+        gather(states, SENT[:1], idx, lax.rem(me_ref + nmem - shift, nmem), slots, piece, SENT[1])
         for idx, shift in zip(others_index, shifts)
     ]
     got_hx = [to_lower(x, shift) for x, shift in zip(sent_hx, shifts)]
@@ -381,8 +410,10 @@
     def send(i, pieces):
         received[i] = [to_lower(x, shift) for x, shift in zip(pieces, shifts)]
 
-    for i, message in enumerate(MESSAGES[:-1]):
-        pieces = cut(message, states)
+    send(0, first_pieces)
+    sources = lax.optimization_barrier((*states, sent_hx))
+    for i, message in enumerate(MESSAGES[1:-1], 1):
+        pieces = cut(message, sources)
         send(i, pieces)
 
     def read(i, so_far):
@@ -394,7 +425,16 @@
 
     stats = read(READ[0], None)
     stats = statistics(
-        own_hx, got_hx, value, weight, live, me_ref, SENT_GROUP, 0, observations, stats
+        own_hx,
+        got_hx,
+        value,
+        weight,
+        live,
+        me_ref,
+        SENT[0],
+        SENT[1] * observations // 8,
+        observations,
+        stats,
     )
     for i in READ[1:]:
         stats = read(i, stats)

time: 141 us -> 141 us (level)
  waiting for transfers between devices: 62.4 us -> 75.3 us
  local copies, waits for them, and re-layouts: 22 us -> 9.62 us
    ppermute x5, waiting for transfers between devices: 23.8 us -> 43.7 us  [all_sum(): x = x + lax.ppermute(x, axis, [(i, i ^ step) for i in range(size)])]
    dynamic_slice x6 -> x5, local copies, waits for them, and re-layouts: 8.5 us -> 1.61 us  [cut(): lax.dynamic_slice(source[group], (0, lax.rem(me + nmem - shift, nmem) * p...]
    ppermute x1, waiting for transfers between devices: 9 us -> 4.4 us  [to_upper(): lax.ppermute(array, 'mem', [(i, (i + shift) % nmem) for i in range(nmem)])]
    ppermute x8 -> x10, starting transfers between devices: 11.3 us -> 14.5 us  [to_lower(): lax.ppermute(array, 'mem', [(i, (i - shift) % nmem) for i in range(nmem)])]
    unnamed x20, local copies, waits for them, and re-layouts: 9.72 us -> 6.82 us
    ppermute x5, starting transfers between devices: 8.44 us -> 5.88 us  [all_sum(): x = x + lax.ppermute(x, axis, [(i, i ^ step) for i in range(size)])]
    ppermute x8 -> x10, waiting for transfers between devices: 29.6 us -> 27.1 us  [to_lower(): lax.ppermute(array, 'mem', [(i, (i - shift) % nmem) for i in range(nmem)])]
    pallas_call x2 -> x3, Pallas kernels: 5.63 us -> 4.73 us  [the longest x2 3.63 us: gather(): pl.pallas_call(functools.partial(gather_kernel, slots, groups, eighth), o...]
  transfers between devices with their start and end apart: 14 -> 16, of which waited for: 7 -> 11; matrix products, arithmetic and copies ran while one was open for 8% -> 2% of each run, Pallas kernels for 24% -> 23%
where the time goes in v4:
time: 141 us
  waiting for transfers between devices  75.3 us (53%)
  Pallas kernels  34.5 us (24%)
  starting transfers between devices  20.5 us (15%)
  local copies, waits for them, and re-layouts  9.62 us (7%)
    ppermute x5, waiting for transfers between devices, all_sum(): x = x + lax.ppermute(x, axis, [(i, i ^ step) for i in range(size)])  43.7 us
    ppermute x10, waiting for transfers between devices, to_lower(): lax.ppermute(array, 'mem', [(i, (i - shift) % nmem) for i in range(nmem)])  27.1 us
    ppermute x10, starting transfers between devices, to_lower(): lax.ppermute(array, 'mem', [(i, (i - shift) % nmem) for i in range(nmem)])  14.5 us
    pallas_call x6, Pallas kernels, statistics(): pl.pallas_call(functools.partial(statistics_kernel, parts, slots, group,...  10.1 us
    pallas_call x1, Pallas kernels, make_transform(): pl.pallas_call(functools.partial(transform_kernel, members), out_shape=(j...  9.84 us
    pallas_call x4, Pallas kernels, analyse(): pl.pallas_call(functools.partial(analysis_kernel, bounds, len(received) /...  9.78 us
    unnamed x20, local copies, waits for them, and re-layouts  6.82 us
    ppermute x5, starting transfers between devices, all_sum(): x = x + lax.ppermute(x, axis, [(i, i ^ step) for i in range(size)])  5.88 us
  transfers between devices with their start and end apart: 16, of which 11 were waited for; matrix products, arithmetic and copies ran while one was open for 2% of the time, Pallas kernels for 23%

profile of v4, /device:TPU:0, one launch (start us, length us, event | category | flops | bytes accessed | tf_op | source)
XLA Modules:
  0.0 140.9 jit_solution(8613249431978619323)
XLA Ops:
  1.8 3.0 %collective-permute-start.6 = (bf16[32,8192]{1,0:T(8,128)(2,1)S(1)}, bf16[32,8192]{1,0:T(8,128)(2,1)S(1)}, u32[]{:S(2)}, u32[]{:S(2)}) collective-permute-start(bf16[32,8192]{1,0:T(8,128)(2,1)S(1)} %cut.1), channel_id=1, source_target_pairs={{0,16},{16,0},{1,17},{17,1},{2,18},{18,2},{3,19},{19,3},{4,20},{20... | collective-permute-start | bytes 1572872 | tf_op jit(solution)/shard_map/ppermute | solution.py:368
  6.3 2.2 %copy-done = bf16[32,65536]{1,0:T(8,128)(2,1)S(1)} copy-done((bf16[32,65536]{1,0:T(8,128)(2,1)S(1)}, bf16[32,65536]{1,0:T(8,128)(2,1)}, u32[]{:S(2)}) %copy-start) | copy-done | bytes 4194328
  8.5 2.2 %copy-done.3 = bf16[32,65536]{1,0:T(8,128)(2,1)S(1)} copy-done((bf16[32,65536]{1,0:T(8,128)(2,1)S(1)}, bf16[32,65536]{1,0:T(8,128)(2,1)}, u32[]{:S(2)}) %copy-start.3) | copy-done | bytes 4194328
  10.7 2.3 %gather.2.refs_0_ = bf16[2,32,4096]{2,1,0:T(8,128)(2,1)S(1)} custom-call(s32[1]{0:T(128)} %bitcast.base_ref.me_ref, s32[2,32,128]{2,1,0:T(8,128)S(1)} %reshape.59.index_ref.refs_5_, bf16[32,65536]{1,0:T(8,128)(2,1)S(1)} %copy-done.3, bf16[32,65536]{1,0:T(8,128)(2,1)S(1)} %copy-done), custom_call_target="tpu_custom_call" | custom-call | tf_op jit(solution)/shard_map/gather/pallas_call | solution.py:105
  13.0 4.4 %collective-permute-done = s32[2,256,16]{1,2,0:T(8,128)S(1)} collective-permute-done((s32[2,256,16]{1,2,0:T(8,128)S(1)}, s32[2,256,16]{1,2,0:T(8,128)S(1)}, u32[]{:S(2)}, u32[]{:S(2)}) %collective-permute-start) | collective-permute-done | bytes 32800 | tf_op jit(solution)/shard_map/ppermute | solution.py:371
  17.7 2.2 %copy-done.1 = bf16[32,65536]{1,0:T(8,128)(2,1)S(1)} copy-done((bf16[32,65536]{1,0:T(8,128)(2,1)S(1)}, bf16[32,65536]{1,0:T(8,128)(2,1)}, u32[]{:S(2)}) %copy-start.1) | copy-done | bytes 4194328
  21.2 1.8 %collective-permute-start.5 = (bf16[1,32,3584]{2,1,0:T(8,128)(2,1)S(1)}, bf16[1,32,3584]{2,1,0:T(8,128)(2,1)S(1)}, u32[]{:S(2)}, u32[]{:S(2)}) collective-permute-start(bf16[1,32,3584]{2,1,0:T(8,128)(2,1)S(1)} %gather.3), channel_id=1, source_target_pairs={{0,16},{16,0},{1,17},{17,1},{2,18},{18,2},{3,19},{19,3},{4,20},{20... | collective-permute-start | bytes 688136 | tf_op jit(solution)/shard_map/ppermute | solution.py:368
  24.8 1.7 %collective-permute-start.3 = (bf16[32,8192]{1,0:T(8,128)(2,1)S(1)}, bf16[32,8192]{1,0:T(8,128)(2,1)S(1)}, u32[]{:S(2)}, u32[]{:S(2)}) collective-permute-start(bf16[32,8192]{1,0:T(8,128)(2,1)S(1)} %get-tuple-element.18), channel_id=1, source_target_pairs={{0,16},{16,0},{1,17},{17,1},{2,18},{18,2},{3,19},{19,3},{4,20},{20... | collective-permute-start | bytes 1572872 | tf_op jit(solution)/shard_map/ppermute | solution.py:368
  27.0 2.8 %collective-permute-done.5.refs_1_ = bf16[1,32,3584]{2,1,0:T(8,128)(2,1)S(1)} collective-permute-done((bf16[1,32,3584]{2,1,0:T(8,128)(2,1)S(1)}, bf16[1,32,3584]{2,1,0:T(8,128)(2,1)S(1)}, u32[]{:S(2)}, u32[]{:S(2)}) %collective-permute-start.5) | collective-permute-done | bytes 229408 | tf_op jit(solution)/shard_map/ppermute | solution.py:368
  29.8 1.7 %collective-permute-start.1 = (bf16[32,4096]{1,0:T(8,128)(2,1)S(1)}, bf16[32,4096]{1,0:T(8,128)(2,1)S(1)}, u32[]{:S(2)}, u32[]{:S(2)}) collective-permute-start(bf16[32,4096]{1,0:T(8,128)(2,1)S(1)} %get-tuple-element.16), channel_id=1, source_target_pairs={{0,16},{16,0},{1,17},{17,1},{2,18},{18,2},{3,19},{19,3},{4,20},{20... | collective-permute-start | bytes 786440 | tf_op jit(solution)/shard_map/ppermute | solution.py:368
  31.8 1.5 %statistics.6.refs_5_ = f32[64,128]{1,0:T(8,128)S(1)} custom-call(s32[1]{0:T(128)} %bitcast.base_ref.me_ref, bf16[2,32,4096]{2,1,0:T(8,128)(2,1)S(1)} %gather.2.refs_0_, bf16[32,8192]{1,0:T(8,128)(2,1)S(1)} %collective-permute-done.6.refs_1_.refs_0_, f32[2,1,4096]{2,1,0:T(1,128)S(1)} %reshape.63.refs_2_, f32[2,1,4096]{2,1,0:T(1,128)S(1)} %reshape.64.refs_3_, ...), custom_call_target="tpu_custom_call" | custom-call | tf_op jit(solution)/shard_map/statistics/pallas_call | solution.py:213
  33.3 3.5 %statistics.7.refs_6_ = f32[64,128]{1,0:T(8,128)S(1)} custom-call(s32[1]{0:T(128)} %bitcast.base_ref.me_ref, bf16[2,32,4096]{2,1,0:T(8,128)(2,1)S(1)} %gather.2.refs_0_, bf16[1,32,3584]{2,1,0:T(8,128)(2,1)S(1)} %collective-permute-done.5.refs_1_, f32[2,1,4096]{2,1,0:T(1,128)S(1)} %reshape.63.refs_2_, f32[2,1,4096]{2,1,0:T(1,128)S(1)} %reshape.64.refs_3_, ...), custom_call_target="tpu_custom_call" | custom-call | tf_op jit(solution)/shard_map/statistics/pallas_call | solution.py:213
  36.8 4.2 %collective-permute-done.4.refs_1_ = bf16[32,8192]{1,0:T(8,128)(2,1)S(1)} collective-permute-done((bf16[32,8192]{1,0:T(8,128)(2,1)S(1)}, bf16[32,8192]{1,0:T(8,128)(2,1)S(1)}, u32[]{:S(2)}, u32[]{:S(2)}) %collective-permute-start.4) | collective-permute-done | bytes 524320 | tf_op jit(solution)/shard_map/ppermute | solution.py:368
  41.0 1.7 %collective-permute-start.14 = (bf16[32,4096]{1,0:T(8,128)(2,1)S(1)}, bf16[32,4096]{1,0:T(8,128)(2,1)S(1)}, u32[]{:S(2)}, u32[]{:S(2)}) collective-permute-start(bf16[32,4096]{1,0:T(8,128)(2,1)S(1)} %get-tuple-element.15), channel_id=1, source_target_pairs={{0,16},{16,0},{1,17},{17,1},{2,18},{18,2},{3,19},{19,3},{4,20},{20... | collective-permute-start | bytes 786440 | tf_op jit(solution)/shard_map/ppermute | solution.py:368
  42.7 1.5 %statistics.8.refs_6_ = f32[64,128]{1,0:T(8,128)S(1)} custom-call(s32[1]{0:T(128)} %bitcast.base_ref.me_ref, bf16[2,32,4096]{2,1,0:T(8,128)(2,1)S(1)} %gather.2.refs_0_, bf16[32,8192]{1,0:T(8,128)(2,1)S(1)} %collective-permute-done.4.refs_1_, f32[2,1,4096]{2,1,0:T(1,128)S(1)} %reshape.63.refs_2_, f32[2,1,4096]{2,1,0:T(1,128)S(1)} %reshape.64.refs_3_, ...), custom_call_target="tpu_custom_call" | custom-call | tf_op jit(solution)/shard_map/statistics/pallas_call | solution.py:213
  44.2 8.0 %collective-permute-done.3.refs_1_.refs_2_ = bf16[32,8192]{1,0:T(8,128)(2,1)S(1)} collective-permute-done((bf16[32,8192]{1,0:T(8,128)(2,1)S(1)}, bf16[32,8192]{1,0:T(8,128)(2,1)S(1)}, u32[]{:S(2)}, u32[]{:S(2)}) %collective-permute-start.3) | collective-permute-done | bytes 524320 | tf_op jit(solution)/shard_map/ppermute | solution.py:368
  52.2 1.7 %collective-permute-start.13 = (bf16[32,8192]{1,0:T(8,128)(2,1)S(1)}, bf16[32,8192]{1,0:T(8,128)(2,1)S(1)}, u32[]{:S(2)}, u32[]{:S(2)}) collective-permute-start(bf16[32,8192]{1,0:T(8,128)(2,1)S(1)} %constant_dynamic-slice_fusion.2), channel_id=1, source_target_pairs={{0,16},{16,0},{1,17},{17,1},{2,18},{18,2},{3,19},{19,3},{4,20},{20... | collective-permute-start | bytes 1572872 | tf_op jit(solution)/shard_map/ppermute | solution.py:368
  54.0 1.5 %statistics.9.refs_6_ = f32[64,128]{1,0:T(8,128)S(1)} custom-call(s32[1]{0:T(128)} %bitcast.base_ref.me_ref, bf16[2,32,4096]{2,1,0:T(8,128)(2,1)S(1)} %gather.2.refs_0_, bf16[32,8192]{1,0:T(8,128)(2,1)S(1)} %collective-permute-done.3.refs_1_.refs_2_, f32[2,1,4096]{2,1,0:T(1,128)S(1)} %reshape.63.refs_2_, f32[2,1,4096]{2,1,0:T(1,128)S(1)} %reshape.64.refs_3_, ...), custom_call_target="tpu_custom_call" | custom-call | tf_op jit(solution)/shard_map/statistics/pallas_call | solution.py:213
  55.5 8.0 %collective-permute-done.2.refs_1_.refs_3_ = bf16[32,8192]{1,0:T(8,128)(2,1)S(1)} collective-permute-done((bf16[32,8192]{1,0:T(8,128)(2,1)S(1)}, bf16[32,8192]{1,0:T(8,128)(2,1)S(1)}, u32[]{:S(2)}, u32[]{:S(2)}) %collective-permute-start.2) | collective-permute-done | bytes 524320 | tf_op jit(solution)/shard_map/ppermute | solution.py:368
  64.9 4.1 %collective-permute-done.1.refs_1_.refs_0_ = bf16[32,4096]{1,0:T(8,128)(2,1)S(1)} collective-permute-done((bf16[32,4096]{1,0:T(8,128)(2,1)S(1)}, bf16[32,4096]{1,0:T(8,128)(2,1)S(1)}, u32[]{:S(2)}, u32[]{:S(2)}) %collective-permute-start.1) | collective-permute-done | bytes 262176 | tf_op jit(solution)/shard_map/ppermute | solution.py:368
  69.8 1.8 %collective-permute-start.12 = (bf16[32,4096]{1,0:T(8,128)(2,1)S(1)}, bf16[32,4096]{1,0:T(8,128)(2,1)S(1)}, u32[]{:S(2)}, u32[]{:S(2)}) collective-permute-start(bf16[32,4096]{1,0:T(8,128)(2,1)S(1)} %constant_dynamic-slice_fusion.3), channel_id=1, source_target_pairs={{0,16},{16,0},{1,17},{17,1},{2,18},{18,2},{3,19},{19,3},{4,20},{20... | collective-permute-start | bytes 786440 | tf_op jit(solution)/shard_map/ppermute | solution.py:368
  71.9 35.5 %collective-permute-done.7 = f32[64,128]{1,0:T(8,128)S(1)} collective-permute-done((f32[64,128]{1,0:T(8,128)S(1)}, f32[64,128]{1,0:T(8,128)S(1)}, u32[]{:S(2)}, u32[]{:S(2)}) %collective-permute-start.7) | collective-permute-done | bytes 32800 | tf_op jit(solution)/shard_map/ppermute | solution.py:448
  108.6 1.5 %collective-permute-start.9 = (f32[64,128]{1,0:T(8,128)S(1)}, f32[64,128]{1,0:T(8,128)S(1)}, u32[]{:S(2)}, u32[]{:S(2)}) collective-permute-start(f32[64,128]{1,0:T(8,128)S(1)} %add.92), channel_id=1, source_target_pairs={{0,2},{1,3},{2,0},{3,1},{4,6},{5,7},{6,4},{7,5},{8,10},{9,11},{10,... | collective-permute-start | bytes 98312 | tf_op jit(solution)/shard_map/ppermute | solution.py:448
  110.1 2.4 %collective-permute-done.9 = f32[64,128]{1,0:T(8,128)S(1)} collective-permute-done((f32[64,128]{1,0:T(8,128)S(1)}, f32[64,128]{1,0:T(8,128)S(1)}, u32[]{:S(2)}, u32[]{:S(2)}) %collective-permute-start.9) | collective-permute-done | bytes 32800 | tf_op jit(solution)/shard_map/ppermute | solution.py:448
  112.5 1.5 %collective-permute-start.10 = (f32[64,128]{1,0:T(8,128)S(1)}, f32[64,128]{1,0:T(8,128)S(1)}, u32[]{:S(2)}, u32[]{:S(2)}) collective-permute-start(f32[64,128]{1,0:T(8,128)S(1)} %add.93), channel_id=1, source_target_pairs={{0,4},{1,5},{2,6},{3,7},{4,0},{5,1},{6,2},{7,3},{8,12},{9,13},{10,... | collective-permute-start | bytes 98312 | tf_op jit(solution)/shard_map/ppermute | solution.py:448
  114.1 2.4 %collective-permute-done.10 = f32[64,128]{1,0:T(8,128)S(1)} collective-permute-done((f32[64,128]{1,0:T(8,128)S(1)}, f32[64,128]{1,0:T(8,128)S(1)}, u32[]{:S(2)}, u32[]{:S(2)}) %collective-permute-start.10) | collective-permute-done | bytes 32800 | tf_op jit(solution)/shard_map/ppermute | solution.py:448
  116.5 2.6 %collective-permute-start.11 = (f32[64,128]{1,0:T(8,128)S(1)}, f32[64,128]{1,0:T(8,128)S(1)}, u32[]{:S(2)}, u32[]{:S(2)}) collective-permute-start(f32[64,128]{1,0:T(8,128)S(1)} %add.94), channel_id=1, source_target_pairs={{0,8},{1,9},{2,10},{3,11},{4,12},{5,13},{6,14},{7,15},{8,0},{9,1},... | collective-permute-start | bytes 98312 | tf_op jit(solution)/shard_map/ppermute | solution.py:448
  119.0 2.3 %collective-permute-done.11 = f32[64,128]{1,0:T(8,128)S(1)} collective-permute-done((f32[64,128]{1,0:T(8,128)S(1)}, f32[64,128]{1,0:T(8,128)S(1)}, u32[]{:S(2)}, u32[]{:S(2)}) %collective-permute-start.11) | collective-permute-done | bytes 32800 | tf_op jit(solution)/shard_map/ppermute | solution.py:448
  121.3 9.8 %transform.1 = (f32[64,64]{1,0:T(8,128)}, bf16[80,64]{1,0:T(8,128)(2,1)S(1)}, f32[64,128]{1,0:T(8,128)S(1)}) custom-call(s32[1]{0:T(128)} %bitcast.base_ref.me_ref, f32[64,128]{1,0:T(8,128)S(1)} %add.95.stats_ref), custom_call_target="tpu_custom_call" | custom-call | tf_op jit(solution)/shard_map/transform/pallas_call | solution.py:276
  131.1 3.6 %analysis.4 = bf16[64,32768]{1,0:T(8,128)(2,1)} custom-call(s32[1]{0:T(128)} %bitcast.base_ref.me_ref, bf16[80,64]{1,0:T(8,128)(2,1)S(1)} %get-tuple-element.11.mixer_ref, f32[64,128]{1,0:T(8,128)S(1)} %get-tuple-element.12.rest_ref, bf16[32,65536]{1,0:T(8,128)(2,1)S(1)} %copy-done.4, bf16[32,8192]{1,0:T(8,128)(2,1)S(1)} %collective-permute-done.6.refs_1_.refs_0_, ...), custom_call_target="tpu_custom_call" | custom-call | tf_op jit(solution)/shard_map/analysis/pallas_call | solution.py:334
  134.8 3.5 %analysis.5.refs_1_ = bf16[64,32768]{1,0:T(8,128)(2,1)} custom-call(s32[1]{0:T(128)} %bitcast.base_ref.me_ref, bf16[80,64]{1,0:T(8,128)(2,1)S(1)} %get-tuple-element.11.mixer_ref, f32[64,128]{1,0:T(8,128)S(1)} %get-tuple-element.12.rest_ref, bf16[32,65536]{1,0:T(8,128)(2,1)S(1)} %copy-done.2, bf16[32,4096]{1,0:T(8,128)(2,1)S(1)} %collective-permute-done.1.refs_1_.refs_0_, ...), custom_call_target="tpu_custom_call" | custom-call | tf_op jit(solution)/shard_map/analysis/pallas_call | solution.py:334
  138.3 1.5 %analysis.6.refs_1_ = bf16[64,32768]{1,0:T(8,128)(2,1)} custom-call(s32[1]{0:T(128)} %bitcast.base_ref.me_ref, bf16[80,64]{1,0:T(8,128)(2,1)S(1)} %get-tuple-element.11.mixer_ref, f32[64,128]{1,0:T(8,128)S(1)} %get-tuple-element.12.rest_ref, bf16[32,65536]{1,0:T(8,128)(2,1)S(1)} %copy-done.2, ...), custom_call_target="tpu_custom_call", output_to_operand_aliasing={{}: (5, {})} | custom-call | tf_op jit(solution)/shard_map/analysis/pallas_call | solution.py:334
  (56 shorter events, 11.4 us)
Async XLA Ops:
  0.6 4.2 %copy-start.6 = (s32[2,256,16]{1,2,0:T(8,128)S(1)}, s32[2,256,16]{1,2,0:T(8,128)}, u32[]{:S(2)}) copy-start(s32[2,256,16]{1,2,0:T(8,128)} %param.8) | copy-start | bytes 98308
  0.6 4.3 %copy-start.8 = (s32[2,256]{1,0:T(2,128)S(1)}, s32[2,256]{1,0:T(2,128)}, u32[]{:S(2)}) copy-start(s32[2,256]{1,0:T(2,128)} %param.9) | copy-start | bytes 6148
  0.7 4.7 %copy-start.7 = (f32[2,256,16]{1,2,0:T(8,128)S(1)}, f32[2,256,16]{1,2,0:T(8,128)}, u32[]{:S(2)}) copy-start(f32[2,256,16]{1,2,0:T(8,128)} %param.11) | copy-start | bytes 98308
  0.7 5.3 %copy-start.5 = (f32[2,256,16]{1,2,0:T(8,128)S(1)}, f32[2,256,16]{1,2,0:T(8,128)}, u32[]{:S(2)}) copy-start(f32[2,256,16]{1,2,0:T(8,128)} %param.10) | copy-start | bytes 98308
  1.8 29.7 %collective-permute-start.6 = (bf16[32,8192]{1,0:T(8,128)(2,1)S(1)}, bf16[32,8192]{1,0:T(8,128)(2,1)S(1)}, u32[]{:S(2)}, u32[]{:S(2)}) collective-permute-start(bf16[32,8192]{1,0:T(8,128)(2,1)S(1)} %cut.1), channel_id=1, source_target_pairs={{0,16},{16,0},{1,17},{17,1},{2,18},{18,2},{3,19},{19,3},{4,20},{20... | collective-permute-start | bytes 1572872 | tf_op jit(solution)/shard_map/ppermute | solution.py:368
  4.8 12.6 %collective-permute-start = (s32[2,256,16]{1,2,0:T(8,128)S(1)}, s32[2,256,16]{1,2,0:T(8,128)S(1)}, u32[]{:S(2)}, u32[]{:S(2)}) collective-permute-start(s32[2,256,16]{1,2,0:T(8,128)S(1)} %copy-done.6), channel_id=1, source_target_pairs={{0,16},{16,0},{1,17},{17,1},{2,18},{18,2},{3,19},{19,3},{4,20},{20... | collective-permute-start | bytes 98312 | tf_op jit(solution)/shard_map/ppermute | solution.py:371
  6.3 2.2 %copy-start = (bf16[32,65536]{1,0:T(8,128)(2,1)S(1)}, bf16[32,65536]{1,0:T(8,128)(2,1)}, u32[]{:S(2)}) copy-start(bf16[32,65536]{1,0:T(8,128)(2,1)} %own_ref.7) | copy-start | bytes 12582916
  8.5 2.2 %copy-start.3 = (bf16[32,65536]{1,0:T(8,128)(2,1)S(1)}, bf16[32,65536]{1,0:T(8,128)(2,1)}, u32[]{:S(2)}) copy-start(bf16[32,65536]{1,0:T(8,128)(2,1)} %own_ref.4) | copy-start | bytes 12582916
  17.7 2.2 %copy-start.1 = (bf16[32,65536]{1,0:T(8,128)(2,1)S(1)}, bf16[32,65536]{1,0:T(8,128)(2,1)}, u32[]{:S(2)}) copy-start(bf16[32,65536]{1,0:T(8,128)(2,1)} %own_ref.7) | copy-start | bytes 12582916
  19.9 7.0 %copy-start.2 = (bf16[32,65536]{1,0:T(8,128)(2,1)S(1)}, bf16[32,65536]{1,0:T(8,128)(2,1)}, u32[]{:S(2)}) copy-start(bf16[32,65536]{1,0:T(8,128)(2,1)} %own_ref.7) | copy-start | bytes 12582916
  21.2 8.5 %collective-permute-start.5 = (bf16[1,32,3584]{2,1,0:T(8,128)(2,1)S(1)}, bf16[1,32,3584]{2,1,0:T(8,128)(2,1)S(1)}, u32[]{:S(2)}, u32[]{:S(2)}) collective-permute-start(bf16[1,32,3584]{2,1,0:T(8,128)(2,1)S(1)} %gather.3), channel_id=1, source_target_pairs={{0,16},{16,0},{1,17},{17,1},{2,18},{18,2},{3,19},{19,3},{4,20},{20... | collective-permute-start | bytes 688136 | tf_op jit(solution)/shard_map/ppermute | solution.py:368
  24.5 16.5 %collective-permute-start.4 = (bf16[32,8192]{1,0:T(8,128)(2,1)S(1)}, bf16[32,8192]{1,0:T(8,128)(2,1)S(1)}, u32[]{:S(2)}, u32[]{:S(2)}) collective-permute-start(bf16[32,8192]{1,0:T(8,128)(2,1)S(1)} %get-tuple-element.17), channel_id=1, source_target_pairs={{0,16},{16,0},{1,17},{17,1},{2,18},{18,2},{3,19},{19,3},{4,20},{20... | collective-permute-start | bytes 1572872 | tf_op jit(solution)/shard_map/ppermute | solution.py:368
  24.8 27.4 %collective-permute-start.3 = (bf16[32,8192]{1,0:T(8,128)(2,1)S(1)}, bf16[32,8192]{1,0:T(8,128)(2,1)S(1)}, u32[]{:S(2)}, u32[]{:S(2)}) collective-permute-start(bf16[32,8192]{1,0:T(8,128)(2,1)S(1)} %get-tuple-element.18), channel_id=1, source_target_pairs={{0,16},{16,0},{1,17},{17,1},{2,18},{18,2},{3,19},{19,3},{4,20},{20... | collective-permute-start | bytes 1572872 | tf_op jit(solution)/shard_map/ppermute | solution.py:368
  26.6 36.9 %collective-permute-start.2 = (bf16[32,8192]{1,0:T(8,128)(2,1)S(1)}, bf16[32,8192]{1,0:T(8,128)(2,1)S(1)}, u32[]{:S(2)}, u32[]{:S(2)}) collective-permute-start(bf16[32,8192]{1,0:T(8,128)(2,1)S(1)} %get-tuple-element.19), channel_id=1, source_target_pairs={{0,16},{16,0},{1,17},{17,1},{2,18},{18,2},{3,19},{19,3},{4,20},{20... | collective-permute-start | bytes 1572872 | tf_op jit(solution)/shard_map/ppermute | solution.py:368
  29.8 39.3 %collective-permute-start.1 = (bf16[32,4096]{1,0:T(8,128)(2,1)S(1)}, bf16[32,4096]{1,0:T(8,128)(2,1)S(1)}, u32[]{:S(2)}, u32[]{:S(2)}) collective-permute-start(bf16[32,4096]{1,0:T(8,128)(2,1)S(1)} %get-tuple-element.16), channel_id=1, source_target_pairs={{0,16},{16,0},{1,17},{17,1},{2,18},{18,2},{3,19},{19,3},{4,20},{20... | collective-permute-start | bytes 786440 | tf_op jit(solution)/shard_map/ppermute | solution.py:368
  31.5 103.3 %collective-permute-start.15 = (bf16[32,12288]{1,0:T(8,128)(2,1)S(1)}, bf16[32,12288]{1,0:T(8,128)(2,1)S(1)}, u32[]{:S(2)}, u32[]{:S(2)}) collective-permute-start(bf16[32,12288]{1,0:T(8,128)(2,1)S(1)} %constant_dynamic-slice_fusion), channel_id=1, source_target_pairs={{0,16},{16,0},{1,17},{17,1},{2,18},{18,2},{3,19},{19,3},{4,20},{20... | collective-permute-start | bytes 2359304 | tf_op jit(solution)/shard_map/ppermute | solution.py:368
  31.8 99.3 %copy-start.4 = (bf16[32,65536]{1,0:T(8,128)(2,1)S(1)}, bf16[32,65536]{1,0:T(8,128)(2,1)}, u32[]{:S(2)}) copy-start(bf16[32,65536]{1,0:T(8,128)(2,1)} %own_ref.4) | copy-start | bytes 12582916
  41.0 93.8 %collective-permute-start.14 = (bf16[32,4096]{1,0:T(8,128)(2,1)S(1)}, bf16[32,4096]{1,0:T(8,128)(2,1)S(1)}, u32[]{:S(2)}, u32[]{:S(2)}) collective-permute-start(bf16[32,4096]{1,0:T(8,128)(2,1)S(1)} %get-tuple-element.15), channel_id=1, source_target_pairs={{0,16},{16,0},{1,17},{17,1},{2,18},{18,2},{3,19},{19,3},{4,20},{20... | collective-permute-start | bytes 786440 | tf_op jit(solution)/shard_map/ppermute | solution.py:368
  52.2 86.0 %collective-permute-start.13 = (bf16[32,8192]{1,0:T(8,128)(2,1)S(1)}, bf16[32,8192]{1,0:T(8,128)(2,1)S(1)}, u32[]{:S(2)}, u32[]{:S(2)}) collective-permute-start(bf16[32,8192]{1,0:T(8,128)(2,1)S(1)} %constant_dynamic-slice_fusion.2), channel_id=1, source_target_pairs={{0,16},{16,0},{1,17},{17,1},{2,18},{18,2},{3,19},{19,3},{4,20},{20... | collective-permute-start | bytes 1572872 | tf_op jit(solution)/shard_map/ppermute | solution.py:368
  69.8 70.0 %collective-permute-start.12 = (bf16[32,4096]{1,0:T(8,128)(2,1)S(1)}, bf16[32,4096]{1,0:T(8,128)(2,1)S(1)}, u32[]{:S(2)}, u32[]{:S(2)}) collective-permute-start(bf16[32,4096]{1,0:T(8,128)(2,1)S(1)} %constant_dynamic-slice_fusion.3), channel_id=1, source_target_pairs={{0,16},{16,0},{1,17},{17,1},{2,18},{18,2},{3,19},{19,3},{4,20},{20... | collective-permute-start | bytes 786440 | tf_op jit(solution)/shard_map/ppermute | solution.py:368
  71.6 35.8 %collective-permute-start.7 = (f32[64,128]{1,0:T(8,128)S(1)}, f32[64,128]{1,0:T(8,128)S(1)}, u32[]{:S(2)}, u32[]{:S(2)}) collective-permute-start(f32[64,128]{1,0:T(8,128)S(1)} %statistics.11), channel_id=1, source_target_pairs={{0,16},{16,0},{1,17},{17,1},{2,18},{18,2},{3,19},{19,3},{4,20},{20... | collective-permute-start | bytes 98312 | tf_op jit(solution)/shard_map/ppermute | solution.py:448
  107.4 1.2 collective-permute-start.8
  108.6 3.9 %collective-permute-start.9 = (f32[64,128]{1,0:T(8,128)S(1)}, f32[64,128]{1,0:T(8,128)S(1)}, u32[]{:S(2)}, u32[]{:S(2)}) collective-permute-start(f32[64,128]{1,0:T(8,128)S(1)} %add.92), channel_id=1, source_target_pairs={{0,2},{1,3},{2,0},{3,1},{4,6},{5,7},{6,4},{7,5},{8,10},{9,11},{10,... | collective-permute-start | bytes 98312 | tf_op jit(solution)/shard_map/ppermute | solution.py:448
  112.5 3.9 %collective-permute-start.10 = (f32[64,128]{1,0:T(8,128)S(1)}, f32[64,128]{1,0:T(8,128)S(1)}, u32[]{:S(2)}, u32[]{:S(2)}) collective-permute-start(f32[64,128]{1,0:T(8,128)S(1)} %add.93), channel_id=1, source_target_pairs={{0,4},{1,5},{2,6},{3,7},{4,0},{5,1},{6,2},{7,3},{8,12},{9,13},{10,... | collective-permute-start | bytes 98312 | tf_op jit(solution)/shard_map/ppermute | solution.py:448
  116.5 4.8 %collective-permute-start.11 = (f32[64,128]{1,0:T(8,128)S(1)}, f32[64,128]{1,0:T(8,128)S(1)}, u32[]{:S(2)}, u32[]{:S(2)}) collective-permute-start(f32[64,128]{1,0:T(8,128)S(1)} %add.94), channel_id=1, source_target_pairs={{0,8},{1,9},{2,10},{3,11},{4,12},{5,13},{6,14},{7,15},{8,0},{9,1},... | collective-permute-start | bytes 98312 | tf_op jit(solution)/shard_map/ppermute | solution.py:448

commit v5 on v4

--- a/solution.py
+++ b/solution.py
@@ -15,15 +15,15 @@
 LANES = 128
 
 MESSAGES = (
-    (0, 0, 2),
-    (0, 2, 4),
-    (0, 4, 6),
-    (0, 6, 8),
-    (1, 0, 1),
-    (1, 1, 2),
-    (1, 2, 5),
-    (1, 5, 7),
-    (1, 7, 8),
+    (0, 0, 8),
+    (0, 8, 16),
+    (0, 16, 24),
+    (0, 24, 32),
+    (1, 0, 4),
+    (1, 4, 6),
+    (1, 6, 20),
+    (1, 20, 28),
+    (1, 28, 32),
 )
 READ = (0, 1, 2, 3, 4)
 SENT = (1, 1)
@@ -256,7 +256,9 @@
         tm = split(1.5 * eye - 0.5 * terms_dot(zn, yn))
         return terms_dot(yn, tm), terms_dot(tm, zn)
 
-    _, zn = lax.fori_loop(0, ITERS, forward_step, (amat / scale, eye))
+    yn = amat / scale
+    tm = 1.5 * eye - 0.5 * yn
+    yn, zn = lax.fori_loop(1, ITERS, forward_step, (terms_dot(split(yn), split(tm)), tm))
     parts = split(zn)
     pmat = terms_dot(parts, parts) / scale
     wide = jnp.broadcast_to(bs, (everyone, LANES))
@@ -312,7 +314,7 @@
     members = state.shape[0]
     everyone = rest.shape[0]
     first, last = messages[0][0], messages[-1][1]
-    width = 2 * piece // 8
+    width = piece // 4
     for lo, hi, _ in messages:
         width = math.gcd(width, lo, hi)
     skip = first // width
@@ -359,7 +361,7 @@
     nblk = obs_index.shape[1]
     slots = obs_index.shape[2]
     observations = nblk * slots
-    unit = piece // 8
+    unit = piece // 32
     me = lax.axis_index("mem")
     me_ref = me[None].astype(jnp.int32)
     shifts = range(1, nmem)
@@ -418,7 +420,7 @@
 
     def read(i, so_far):
         group, lo, hi = MESSAGES[i]
-        lo, hi = (x * observations // 8 for x in (lo, hi))
+        lo, hi = (x * observations // 32 for x in (lo, hi))
         return statistics(
             own_hx, received[i], value, weight, live, me_ref, group, lo, hi, so_far, index, slots
         )
@@ -443,10 +445,8 @@
     send(len(MESSAGES) - 1, pieces)
 
     def all_sum(x, axis, size):
-        step = 1
-        while step < size:
-            x = x + lax.ppermute(x, axis, [(i, i ^ step) for i in range(size)])
-            step *= 2
+        for i in range((size - 1).bit_length()):
+            x = x + lax.ppermute(x, axis, [(j, j ^ (1 << i)) for j in range(size)])
         return x
 
     stats = all_sum(all_sum(stats, "mem", nmem), "col", ncol)

time: 141 us -> 137 us (0.972)
  waiting for transfers between devices: 75.3 us -> 68.9 us
    ppermute x5, waiting for transfers between devices: 43.7 us -> 35.7 us  [all_sum(): x = x + lax.ppermute(x, axis, [(j, j ^ 1 << i) for j in range(size)])]
    ppermute x10, waiting for transfers between devices: 27.1 us -> 28.9 us  [to_lower(): lax.ppermute(array, 'mem', [(i, (i - shift) % nmem) for i in range(nmem)])]
    ppermute x5, starting transfers between devices: 5.88 us -> 7.54 us  [all_sum(): x = x + lax.ppermute(x, axis, [(j, j ^ 1 << i) for j in range(size)])]
    pallas_call x4, Pallas kernels: 9.78 us -> 11.4 us  [analyse(): pl.pallas_call(functools.partial(analysis_kernel, bounds, len(received) /...]
  transfers between devices with their start and end apart: 16 -> 16, of which waited for: 11 -> 10; matrix products, arithmetic and copies ran while one was open for 2% -> 2% of each run, Pallas kernels for 23% -> 25%
where the time goes in v5:
time: 137 us; the launch traced here: 136 us
  waiting for transfers between devices  68.9 us (50%)
  Pallas kernels  35.9 us (26%)
  starting transfers between devices  20.8 us (15%)
  local copies, waits for them, and re-layouts  9.63 us (7%)
    ppermute x5, waiting for transfers between devices, all_sum(): x = x + lax.ppermute(x, axis, [(j, j ^ 1 << i) for j in range(size)])  35.7 us
    ppermute x10, waiting for transfers between devices, to_lower(): lax.ppermute(array, 'mem', [(i, (i - shift) % nmem) for i in range(nmem)])  28.9 us
    ppermute x10, starting transfers between devices, to_lower(): lax.ppermute(array, 'mem', [(i, (i - shift) % nmem) for i in range(nmem)])  13.1 us
    pallas_call x4, Pallas kernels, analyse(): pl.pallas_call(functools.partial(analysis_kernel, bounds, len(received) /...  11.4 us
    pallas_call x6, Pallas kernels, statistics(): pl.pallas_call(functools.partial(statistics_kernel, parts, slots, group,...  10.1 us
    pallas_call x1, Pallas kernels, make_transform(): pl.pallas_call(functools.partial(transform_kernel, members), out_shape=(j...  9.65 us
    ppermute x5, starting transfers between devices, all_sum(): x = x + lax.ppermute(x, axis, [(j, j ^ 1 << i) for j in range(size)])  7.54 us
    unnamed x20, local copies, waits for them, and re-layouts  6.82 us
  transfers between devices with their start and end apart: 16, of which 10 were waited for; matrix products, arithmetic and copies ran while one was open for 2% of the time, Pallas kernels for 25%

profile of v5, /device:TPU:0, one launch (start us, length us, event | category | flops | bytes accessed | tf_op | source)
XLA Modules:
  0.0 136.3 jit_solution(2021682386928397248)
XLA Ops:
  1.8 3.0 %collective-permute-start.6 = (bf16[32,8192]{1,0:T(8,128)(2,1)S(1)}, bf16[32,8192]{1,0:T(8,128)(2,1)S(1)}, u32[]{:S(2)}, u32[]{:S(2)}) collective-permute-start(bf16[32,8192]{1,0:T(8,128)(2,1)S(1)} %cut.1), channel_id=1, source_target_pairs={{0,16},{16,0},{1,17},{17,1},{2,18},{18,2},{3,19},{19,3},{4,20},{20... | collective-permute-start | bytes 1572872 | tf_op jit(solution)/shard_map/ppermute | solution.py:370
  6.3 2.2 %copy-done = bf16[32,65536]{1,0:T(8,128)(2,1)S(1)} copy-done((bf16[32,65536]{1,0:T(8,128)(2,1)S(1)}, bf16[32,65536]{1,0:T(8,128)(2,1)}, u32[]{:S(2)}) %copy-start) | copy-done | bytes 4194328
  8.5 2.2 %copy-done.3 = bf16[32,65536]{1,0:T(8,128)(2,1)S(1)} copy-done((bf16[32,65536]{1,0:T(8,128)(2,1)S(1)}, bf16[32,65536]{1,0:T(8,128)(2,1)}, u32[]{:S(2)}) %copy-start.3) | copy-done | bytes 4194328
  10.7 2.3 %gather.2.refs_0_ = bf16[2,32,4096]{2,1,0:T(8,128)(2,1)S(1)} custom-call(s32[1]{0:T(128)} %bitcast.base_ref.me_ref, s32[2,32,128]{2,1,0:T(8,128)S(1)} %reshape.59.index_ref.refs_5_, bf16[32,65536]{1,0:T(8,128)(2,1)S(1)} %copy-done.3, bf16[32,65536]{1,0:T(8,128)(2,1)S(1)} %copy-done), custom_call_target="tpu_custom_call" | custom-call | tf_op jit(solution)/shard_map/gather/pallas_call | solution.py:105
  13.0 4.4 %collective-permute-done = s32[2,256,16]{1,2,0:T(8,128)S(1)} collective-permute-done((s32[2,256,16]{1,2,0:T(8,128)S(1)}, s32[2,256,16]{1,2,0:T(8,128)S(1)}, u32[]{:S(2)}, u32[]{:S(2)}) %collective-permute-start) | collective-permute-done | bytes 32800 | tf_op jit(solution)/shard_map/ppermute | solution.py:373
  17.7 2.2 %copy-done.1 = bf16[32,65536]{1,0:T(8,128)(2,1)S(1)} copy-done((bf16[32,65536]{1,0:T(8,128)(2,1)S(1)}, bf16[32,65536]{1,0:T(8,128)(2,1)}, u32[]{:S(2)}) %copy-start.1) | copy-done | bytes 4194328
  21.2 1.8 %collective-permute-start.5 = (bf16[1,32,3584]{2,1,0:T(8,128)(2,1)S(1)}, bf16[1,32,3584]{2,1,0:T(8,128)(2,1)S(1)}, u32[]{:S(2)}, u32[]{:S(2)}) collective-permute-start(bf16[1,32,3584]{2,1,0:T(8,128)(2,1)S(1)} %gather.3), channel_id=1, source_target_pairs={{0,16},{16,0},{1,17},{17,1},{2,18},{18,2},{3,19},{19,3},{4,20},{20... | collective-permute-start | bytes 688136 | tf_op jit(solution)/shard_map/ppermute | solution.py:370
  24.8 1.7 %collective-permute-start.3 = (bf16[32,8192]{1,0:T(8,128)(2,1)S(1)}, bf16[32,8192]{1,0:T(8,128)(2,1)S(1)}, u32[]{:S(2)}, u32[]{:S(2)}) collective-permute-start(bf16[32,8192]{1,0:T(8,128)(2,1)S(1)} %get-tuple-element.16), channel_id=1, source_target_pairs={{0,16},{16,0},{1,17},{17,1},{2,18},{18,2},{3,19},{19,3},{4,20},{20... | collective-permute-start | bytes 1572872 | tf_op jit(solution)/shard_map/ppermute | solution.py:370
  27.0 2.8 %collective-permute-done.5.refs_1_ = bf16[1,32,3584]{2,1,0:T(8,128)(2,1)S(1)} collective-permute-done((bf16[1,32,3584]{2,1,0:T(8,128)(2,1)S(1)}, bf16[1,32,3584]{2,1,0:T(8,128)(2,1)S(1)}, u32[]{:S(2)}, u32[]{:S(2)}) %collective-permute-start.5) | collective-permute-done | bytes 229408 | tf_op jit(solution)/shard_map/ppermute | solution.py:370
  29.8 1.7 %collective-permute-start.1 = (bf16[32,4096]{1,0:T(8,128)(2,1)S(1)}, bf16[32,4096]{1,0:T(8,128)(2,1)S(1)}, u32[]{:S(2)}, u32[]{:S(2)}) collective-permute-start(bf16[32,4096]{1,0:T(8,128)(2,1)S(1)} %constant_dynamic-slice_fusion.7), channel_id=1, source_target_pairs={{0,16},{16,0},{1,17},{17,1},{2,18},{18,2},{3,19},{19,3},{4,20},{20... | collective-permute-start | bytes 786440 | tf_op jit(solution)/shard_map/ppermute | solution.py:370
  31.8 1.5 %statistics.6.refs_5_ = f32[64,128]{1,0:T(8,128)S(1)} custom-call(s32[1]{0:T(128)} %bitcast.base_ref.me_ref, bf16[2,32,4096]{2,1,0:T(8,128)(2,1)S(1)} %gather.2.refs_0_, bf16[32,8192]{1,0:T(8,128)(2,1)S(1)} %collective-permute-done.6.refs_1_.refs_0_, f32[2,1,4096]{2,1,0:T(1,128)S(1)} %reshape.63.refs_2_, f32[2,1,4096]{2,1,0:T(1,128)S(1)} %reshape.64.refs_3_, ...), custom_call_target="tpu_custom_call" | custom-call | tf_op jit(solution)/shard_map/statistics/pallas_call | solution.py:213
  33.3 3.5 %statistics.7.refs_6_ = f32[64,128]{1,0:T(8,128)S(1)} custom-call(s32[1]{0:T(128)} %bitcast.base_ref.me_ref, bf16[2,32,4096]{2,1,0:T(8,128)(2,1)S(1)} %gather.2.refs_0_, bf16[1,32,3584]{2,1,0:T(8,128)(2,1)S(1)} %collective-permute-done.5.refs_1_, f32[2,1,4096]{2,1,0:T(1,128)S(1)} %reshape.63.refs_2_, f32[2,1,4096]{2,1,0:T(1,128)S(1)} %reshape.64.refs_3_, ...), custom_call_target="tpu_custom_call" | custom-call | tf_op jit(solution)/shard_map/statistics/pallas_call | solution.py:213
  36.8 4.2 %collective-permute-done.4.refs_1_ = bf16[32,8192]{1,0:T(8,128)(2,1)S(1)} collective-permute-done((bf16[32,8192]{1,0:T(8,128)(2,1)S(1)}, bf16[32,8192]{1,0:T(8,128)(2,1)S(1)}, u32[]{:S(2)}, u32[]{:S(2)}) %collective-permute-start.4) | collective-permute-done | bytes 524320 | tf_op jit(solution)/shard_map/ppermute | solution.py:370
  41.0 1.7 %collective-permute-start.13 = (bf16[32,8192]{1,0:T(8,128)(2,1)S(1)}, bf16[32,8192]{1,0:T(8,128)(2,1)S(1)}, u32[]{:S(2)}, u32[]{:S(2)}) collective-permute-start(bf16[32,8192]{1,0:T(8,128)(2,1)S(1)} %constant_dynamic-slice_fusion.2), channel_id=1, source_target_pairs={{0,16},{16,0},{1,17},{17,1},{2,18},{18,2},{3,19},{19,3},{4,20},{20... | collective-permute-start | bytes 1572872 | tf_op jit(solution)/shard_map/ppermute | solution.py:370
  42.7 1.5 %statistics.8.refs_6_ = f32[64,128]{1,0:T(8,128)S(1)} custom-call(s32[1]{0:T(128)} %bitcast.base_ref.me_ref, bf16[2,32,4096]{2,1,0:T(8,128)(2,1)S(1)} %gather.2.refs_0_, bf16[32,8192]{1,0:T(8,128)(2,1)S(1)} %collective-permute-done.4.refs_1_, f32[2,1,4096]{2,1,0:T(1,128)S(1)} %reshape.63.refs_2_, f32[2,1,4096]{2,1,0:T(1,128)S(1)} %reshape.64.refs_3_, ...), custom_call_target="tpu_custom_call" | custom-call | tf_op jit(solution)/shard_map/statistics/pallas_call | solution.py:213
  44.2 8.0 %collective-permute-done.3.refs_1_.refs_2_ = bf16[32,8192]{1,0:T(8,128)(2,1)S(1)} collective-permute-done((bf16[32,8192]{1,0:T(8,128)(2,1)S(1)}, bf16[32,8192]{1,0:T(8,128)(2,1)S(1)}, u32[]{:S(2)}, u32[]{:S(2)}) %collective-permute-start.3) | collective-permute-done | bytes 524320 | tf_op jit(solution)/shard_map/ppermute | solution.py:370
  52.2 1.5 %statistics.9.refs_6_ = f32[64,128]{1,0:T(8,128)S(1)} custom-call(s32[1]{0:T(128)} %bitcast.base_ref.me_ref, bf16[2,32,4096]{2,1,0:T(8,128)(2,1)S(1)} %gather.2.refs_0_, bf16[32,8192]{1,0:T(8,128)(2,1)S(1)} %collective-permute-done.3.refs_1_.refs_2_, f32[2,1,4096]{2,1,0:T(1,128)S(1)} %reshape.63.refs_2_, f32[2,1,4096]{2,1,0:T(1,128)S(1)} %reshape.64.refs_3_, ...), custom_call_target="tpu_custom_call" | custom-call | tf_op jit(solution)/shard_map/statistics/pallas_call | solution.py:213
  53.7 9.7 %collective-permute-done.2.refs_1_.refs_3_ = bf16[32,8192]{1,0:T(8,128)(2,1)S(1)} collective-permute-done((bf16[32,8192]{1,0:T(8,128)(2,1)S(1)}, bf16[32,8192]{1,0:T(8,128)(2,1)S(1)}, u32[]{:S(2)}, u32[]{:S(2)}) %collective-permute-start.2) | collective-permute-done | bytes 524320 | tf_op jit(solution)/shard_map/ppermute | solution.py:370
  64.9 4.1 %collective-permute-done.1.refs_1_.refs_0_ = bf16[32,4096]{1,0:T(8,128)(2,1)S(1)} collective-permute-done((bf16[32,4096]{1,0:T(8,128)(2,1)S(1)}, bf16[32,4096]{1,0:T(8,128)(2,1)S(1)}, u32[]{:S(2)}, u32[]{:S(2)}) %collective-permute-start.1) | collective-permute-done | bytes 262176 | tf_op jit(solution)/shard_map/ppermute | solution.py:370
  69.8 1.8 %collective-permute-start.7 = (f32[64,128]{1,0:T(8,128)S(1)}, f32[64,128]{1,0:T(8,128)S(1)}, u32[]{:S(2)}, u32[]{:S(2)}) collective-permute-start(f32[64,128]{1,0:T(8,128)S(1)} %statistics.11), channel_id=1, source_target_pairs={{0,16},{16,0},{1,17},{17,1},{2,18},{18,2},{3,19},{19,3},{4,20},{20... | collective-permute-start | bytes 98312 | tf_op jit(solution)/shard_map/ppermute | solution.py:449
  71.9 28.7 %collective-permute-done.7 = f32[64,128]{1,0:T(8,128)S(1)} collective-permute-done((f32[64,128]{1,0:T(8,128)S(1)}, f32[64,128]{1,0:T(8,128)S(1)}, u32[]{:S(2)}, u32[]{:S(2)}) %collective-permute-start.7) | collective-permute-done | bytes 32800 | tf_op jit(solution)/shard_map/ppermute | solution.py:449
  100.7 1.8 %collective-permute-start.14 = (bf16[32,2048]{1,0:T(8,128)(2,1)S(1)}, bf16[32,2048]{1,0:T(8,128)(2,1)S(1)}, u32[]{:S(2)}, u32[]{:S(2)}) collective-permute-start(bf16[32,2048]{1,0:T(8,128)(2,1)S(1)} %constant_dynamic-slice_fusion.1), channel_id=1, source_target_pairs={{0,16},{16,0},{1,17},{17,1},{2,18},{18,2},{3,19},{19,3},{4,20},{20... | collective-permute-start | bytes 393224 | tf_op jit(solution)/shard_map/ppermute | solution.py:370
  102.5 1.6 %collective-permute-start.9 = (f32[64,128]{1,0:T(8,128)S(1)}, f32[64,128]{1,0:T(8,128)S(1)}, u32[]{:S(2)}, u32[]{:S(2)}) collective-permute-start(f32[64,128]{1,0:T(8,128)S(1)} %add.98), channel_id=1, source_target_pairs={{0,2},{1,3},{2,0},{3,1},{4,6},{5,7},{6,4},{7,5},{8,10},{9,11},{10,... | collective-permute-start | bytes 98312 | tf_op jit(solution)/shard_map/ppermute | solution.py:449
  104.1 2.4 %collective-permute-done.9 = f32[64,128]{1,0:T(8,128)S(1)} collective-permute-done((f32[64,128]{1,0:T(8,128)S(1)}, f32[64,128]{1,0:T(8,128)S(1)}, u32[]{:S(2)}, u32[]{:S(2)}) %collective-permute-start.9) | collective-permute-done | bytes 32800 | tf_op jit(solution)/shard_map/ppermute | solution.py:449
  106.5 1.6 %collective-permute-start.10 = (f32[64,128]{1,0:T(8,128)S(1)}, f32[64,128]{1,0:T(8,128)S(1)}, u32[]{:S(2)}, u32[]{:S(2)}) collective-permute-start(f32[64,128]{1,0:T(8,128)S(1)} %add.99), channel_id=1, source_target_pairs={{0,4},{1,5},{2,6},{3,7},{4,0},{5,1},{6,2},{7,3},{8,12},{9,13},{10,... | collective-permute-start | bytes 98312 | tf_op jit(solution)/shard_map/ppermute | solution.py:449
  108.1 2.3 %collective-permute-done.10 = f32[64,128]{1,0:T(8,128)S(1)} collective-permute-done((f32[64,128]{1,0:T(8,128)S(1)}, f32[64,128]{1,0:T(8,128)S(1)}, u32[]{:S(2)}, u32[]{:S(2)}) %collective-permute-start.10) | collective-permute-done | bytes 32800 | tf_op jit(solution)/shard_map/ppermute | solution.py:449
  110.4 2.6 %collective-permute-start.11 = (f32[64,128]{1,0:T(8,128)S(1)}, f32[64,128]{1,0:T(8,128)S(1)}, u32[]{:S(2)}, u32[]{:S(2)}) collective-permute-start(f32[64,128]{1,0:T(8,128)S(1)} %add.100), channel_id=1, source_target_pairs={{0,8},{1,9},{2,10},{3,11},{4,12},{5,13},{6,14},{7,15},{8,0},{9,1},... | collective-permute-start | bytes 98312 | tf_op jit(solution)/shard_map/ppermute | solution.py:449
  113.0 2.2 %collective-permute-done.11 = f32[64,128]{1,0:T(8,128)S(1)} collective-permute-done((f32[64,128]{1,0:T(8,128)S(1)}, f32[64,128]{1,0:T(8,128)S(1)}, u32[]{:S(2)}, u32[]{:S(2)}) %collective-permute-start.11) | collective-permute-done | bytes 32800 | tf_op jit(solution)/shard_map/ppermute | solution.py:449
  115.3 9.6 %transform.1 = (f32[64,64]{1,0:T(8,128)}, bf16[80,64]{1,0:T(8,128)(2,1)S(1)}, f32[64,128]{1,0:T(8,128)S(1)}) custom-call(s32[1]{0:T(128)} %bitcast.base_ref.me_ref, f32[64,128]{1,0:T(8,128)S(1)} %add.101.stats_ref), custom_call_target="tpu_custom_call" | custom-call | tf_op jit(solution)/shard_map/transform/pallas_call | solution.py:278
  124.9 3.6 %analysis.4 = bf16[64,32768]{1,0:T(8,128)(2,1)} custom-call(s32[1]{0:T(128)} %bitcast.base_ref.me_ref, bf16[80,64]{1,0:T(8,128)(2,1)S(1)} %get-tuple-element.11.mixer_ref, f32[64,128]{1,0:T(8,128)S(1)} %get-tuple-element.12.rest_ref, bf16[32,65536]{1,0:T(8,128)(2,1)S(1)} %copy-done.4, bf16[32,8192]{1,0:T(8,128)(2,1)S(1)} %collective-permute-done.6.refs_1_.refs_0_, ...), custom_call_target="tpu_custom_call" | custom-call | tf_op jit(solution)/shard_map/analysis/pallas_call | solution.py:336
  128.6 5.1 %analysis.5.refs_1_ = bf16[64,32768]{1,0:T(8,128)(2,1)} custom-call(s32[1]{0:T(128)} %bitcast.base_ref.me_ref, bf16[80,64]{1,0:T(8,128)(2,1)S(1)} %get-tuple-element.11.mixer_ref, f32[64,128]{1,0:T(8,128)S(1)} %get-tuple-element.12.rest_ref, bf16[32,65536]{1,0:T(8,128)(2,1)S(1)} %copy-done.2, bf16[32,4096]{1,0:T(8,128)(2,1)S(1)} %collective-permute-done.1.refs_1_.refs_0_, ...), custom_call_target="tpu_custom_call" | custom-call | tf_op jit(solution)/shard_map/analysis/pallas_call | solution.py:336
  133.6 1.5 %analysis.6.refs_1_ = bf16[64,32768]{1,0:T(8,128)(2,1)} custom-call(s32[1]{0:T(128)} %bitcast.base_ref.me_ref, bf16[80,64]{1,0:T(8,128)(2,1)S(1)} %get-tuple-element.11.mixer_ref, f32[64,128]{1,0:T(8,128)S(1)} %get-tuple-element.12.rest_ref, bf16[32,65536]{1,0:T(8,128)(2,1)S(1)} %copy-done.2, ...), custom_call_target="tpu_custom_call", output_to_operand_aliasing={{}: (5, {})} | custom-call | tf_op jit(solution)/shard_map/analysis/pallas_call | solution.py:336
  (57 shorter events, 10.3 us)
Async XLA Ops:
  0.6 4.2 %copy-start.6 = (s32[2,256,16]{1,2,0:T(8,128)S(1)}, s32[2,256,16]{1,2,0:T(8,128)}, u32[]{:S(2)}) copy-start(s32[2,256,16]{1,2,0:T(8,128)} %param.8) | copy-start | bytes 98308
  0.6 4.3 %copy-start.8 = (s32[2,256]{1,0:T(2,128)S(1)}, s32[2,256]{1,0:T(2,128)}, u32[]{:S(2)}) copy-start(s32[2,256]{1,0:T(2,128)} %param.9) | copy-start | bytes 6148
  0.7 4.7 %copy-start.7 = (f32[2,256,16]{1,2,0:T(8,128)S(1)}, f32[2,256,16]{1,2,0:T(8,128)}, u32[]{:S(2)}) copy-start(f32[2,256,16]{1,2,0:T(8,128)} %param.11) | copy-start | bytes 98308
  0.7 5.3 %copy-start.5 = (f32[2,256,16]{1,2,0:T(8,128)S(1)}, f32[2,256,16]{1,2,0:T(8,128)}, u32[]{:S(2)}) copy-start(f32[2,256,16]{1,2,0:T(8,128)} %param.10) | copy-start | bytes 98308
  1.8 29.7 %collective-permute-start.6 = (bf16[32,8192]{1,0:T(8,128)(2,1)S(1)}, bf16[32,8192]{1,0:T(8,128)(2,1)S(1)}, u32[]{:S(2)}, u32[]{:S(2)}) collective-permute-start(bf16[32,8192]{1,0:T(8,128)(2,1)S(1)} %cut.1), channel_id=1, source_target_pairs={{0,16},{16,0},{1,17},{17,1},{2,18},{18,2},{3,19},{19,3},{4,20},{20... | collective-permute-start | bytes 1572872 | tf_op jit(solution)/shard_map/ppermute | solution.py:370
  4.8 12.6 %collective-permute-start = (s32[2,256,16]{1,2,0:T(8,128)S(1)}, s32[2,256,16]{1,2,0:T(8,128)S(1)}, u32[]{:S(2)}, u32[]{:S(2)}) collective-permute-start(s32[2,256,16]{1,2,0:T(8,128)S(1)} %copy-done.6), channel_id=1, source_target_pairs={{0,16},{16,0},{1,17},{17,1},{2,18},{18,2},{3,19},{19,3},{4,20},{20... | collective-permute-start | bytes 98312 | tf_op jit(solution)/shard_map/ppermute | solution.py:373
  6.3 2.2 %copy-start = (bf16[32,65536]{1,0:T(8,128)(2,1)S(1)}, bf16[32,65536]{1,0:T(8,128)(2,1)}, u32[]{:S(2)}) copy-start(bf16[32,65536]{1,0:T(8,128)(2,1)} %own_ref.7) | copy-start | bytes 12582916
  8.5 2.2 %copy-start.3 = (bf16[32,65536]{1,0:T(8,128)(2,1)S(1)}, bf16[32,65536]{1,0:T(8,128)(2,1)}, u32[]{:S(2)}) copy-start(bf16[32,65536]{1,0:T(8,128)(2,1)} %own_ref.4) | copy-start | bytes 12582916
  17.7 2.2 %copy-start.1 = (bf16[32,65536]{1,0:T(8,128)(2,1)S(1)}, bf16[32,65536]{1,0:T(8,128)(2,1)}, u32[]{:S(2)}) copy-start(bf16[32,65536]{1,0:T(8,128)(2,1)} %own_ref.7) | copy-start | bytes 12582916
  19.9 7.0 %copy-start.2 = (bf16[32,65536]{1,0:T(8,128)(2,1)S(1)}, bf16[32,65536]{1,0:T(8,128)(2,1)}, u32[]{:S(2)}) copy-start(bf16[32,65536]{1,0:T(8,128)(2,1)} %own_ref.7) | copy-start | bytes 12582916
  21.2 8.5 %collective-permute-start.5 = (bf16[1,32,3584]{2,1,0:T(8,128)(2,1)S(1)}, bf16[1,32,3584]{2,1,0:T(8,128)(2,1)S(1)}, u32[]{:S(2)}, u32[]{:S(2)}) collective-permute-start(bf16[1,32,3584]{2,1,0:T(8,128)(2,1)S(1)} %gather.3), channel_id=1, source_target_pairs={{0,16},{16,0},{1,17},{17,1},{2,18},{18,2},{3,19},{19,3},{4,20},{20... | collective-permute-start | bytes 688136 | tf_op jit(solution)/shard_map/ppermute | solution.py:370
  24.5 16.5 %collective-permute-start.4 = (bf16[32,8192]{1,0:T(8,128)(2,1)S(1)}, bf16[32,8192]{1,0:T(8,128)(2,1)S(1)}, u32[]{:S(2)}, u32[]{:S(2)}) collective-permute-start(bf16[32,8192]{1,0:T(8,128)(2,1)S(1)} %get-tuple-element.15), channel_id=1, source_target_pairs={{0,16},{16,0},{1,17},{17,1},{2,18},{18,2},{3,19},{19,3},{4,20},{20... | collective-permute-start | bytes 1572872 | tf_op jit(solution)/shard_map/ppermute | solution.py:370
  24.8 27.4 %collective-permute-start.3 = (bf16[32,8192]{1,0:T(8,128)(2,1)S(1)}, bf16[32,8192]{1,0:T(8,128)(2,1)S(1)}, u32[]{:S(2)}, u32[]{:S(2)}) collective-permute-start(bf16[32,8192]{1,0:T(8,128)(2,1)S(1)} %get-tuple-element.16), channel_id=1, source_target_pairs={{0,16},{16,0},{1,17},{17,1},{2,18},{18,2},{3,19},{19,3},{4,20},{20... | collective-permute-start | bytes 1572872 | tf_op jit(solution)/shard_map/ppermute | solution.py:370
  26.6 36.9 %collective-permute-start.2 = (bf16[32,8192]{1,0:T(8,128)(2,1)S(1)}, bf16[32,8192]{1,0:T(8,128)(2,1)S(1)}, u32[]{:S(2)}, u32[]{:S(2)}) collective-permute-start(bf16[32,8192]{1,0:T(8,128)(2,1)S(1)} %get-tuple-element.17), channel_id=1, source_target_pairs={{0,16},{16,0},{1,17},{17,1},{2,18},{18,2},{3,19},{19,3},{4,20},{20... | collective-permute-start | bytes 1572872 | tf_op jit(solution)/shard_map/ppermute | solution.py:370
  29.8 39.3 %collective-permute-start.1 = (bf16[32,4096]{1,0:T(8,128)(2,1)S(1)}, bf16[32,4096]{1,0:T(8,128)(2,1)S(1)}, u32[]{:S(2)}, u32[]{:S(2)}) collective-permute-start(bf16[32,4096]{1,0:T(8,128)(2,1)S(1)} %constant_dynamic-slice_fusion.7), channel_id=1, source_target_pairs={{0,16},{16,0},{1,17},{17,1},{2,18},{18,2},{3,19},{19,3},{4,20},{20... | collective-permute-start | bytes 786440 | tf_op jit(solution)/shard_map/ppermute | solution.py:370
  31.5 97.1 %collective-permute-start.15 = (bf16[32,14336]{1,0:T(8,128)(2,1)S(1)}, bf16[32,14336]{1,0:T(8,128)(2,1)S(1)}, u32[]{:S(2)}, u32[]{:S(2)}) collective-permute-start(bf16[32,14336]{1,0:T(8,128)(2,1)S(1)} %constant_dynamic-slice_fusion), channel_id=1, source_target_pairs={{0,16},{16,0},{1,17},{17,1},{2,18},{18,2},{3,19},{19,3},{4,20},{20... | collective-permute-start | bytes 2752520 | tf_op jit(solution)/shard_map/ppermute | solution.py:370
  31.8 93.1 %copy-start.4 = (bf16[32,65536]{1,0:T(8,128)(2,1)S(1)}, bf16[32,65536]{1,0:T(8,128)(2,1)}, u32[]{:S(2)}) copy-start(bf16[32,65536]{1,0:T(8,128)(2,1)} %own_ref.4) | copy-start | bytes 12582916
  41.0 92.7 %collective-permute-start.13 = (bf16[32,8192]{1,0:T(8,128)(2,1)S(1)}, bf16[32,8192]{1,0:T(8,128)(2,1)S(1)}, u32[]{:S(2)}, u32[]{:S(2)}) collective-permute-start(bf16[32,8192]{1,0:T(8,128)(2,1)S(1)} %constant_dynamic-slice_fusion.2), channel_id=1, source_target_pairs={{0,16},{16,0},{1,17},{17,1},{2,18},{18,2},{3,19},{19,3},{4,20},{20... | collective-permute-start | bytes 1572872 | tf_op jit(solution)/shard_map/ppermute | solution.py:370
  69.8 30.9 %collective-permute-start.7 = (f32[64,128]{1,0:T(8,128)S(1)}, f32[64,128]{1,0:T(8,128)S(1)}, u32[]{:S(2)}, u32[]{:S(2)}) collective-permute-start(f32[64,128]{1,0:T(8,128)S(1)} %statistics.11), channel_id=1, source_target_pairs={{0,16},{16,0},{1,17},{17,1},{2,18},{18,2},{3,19},{19,3},{4,20},{20... | collective-permute-start | bytes 98312 | tf_op jit(solution)/shard_map/ppermute | solution.py:449
  71.6 63.6 %collective-permute-start.12 = (bf16[32,4096]{1,0:T(8,128)(2,1)S(1)}, bf16[32,4096]{1,0:T(8,128)(2,1)S(1)}, u32[]{:S(2)}, u32[]{:S(2)}) collective-permute-start(bf16[32,4096]{1,0:T(8,128)(2,1)S(1)} %constant_dynamic-slice_fusion.3), channel_id=1, source_target_pairs={{0,16},{16,0},{1,17},{17,1},{2,18},{18,2},{3,19},{19,3},{4,20},{20... | collective-permute-start | bytes 786440 | tf_op jit(solution)/shard_map/ppermute | solution.py:370
  100.7 1.8 %collective-permute-start.8 = (f32[64,128]{1,0:T(8,128)S(1)}, f32[64,128]{1,0:T(8,128)S(1)}, u32[]{:S(2)}, u32[]{:S(2)}) collective-permute-start(f32[64,128]{1,0:T(8,128)S(1)} %add.97), channel_id=1, source_target_pairs={{0,1},{1,0},{2,3},{3,2},{4,5},{5,4},{6,7},{7,6},{8,9},{9,8},{10,11... | collective-permute-start | bytes 98312 | tf_op jit(solution)/shard_map/ppermute | solution.py:449
  100.7 27.8 %collective-permute-start.14 = (bf16[32,2048]{1,0:T(8,128)(2,1)S(1)}, bf16[32,2048]{1,0:T(8,128)(2,1)S(1)}, u32[]{:S(2)}, u32[]{:S(2)}) collective-permute-start(bf16[32,2048]{1,0:T(8,128)(2,1)S(1)} %constant_dynamic-slice_fusion.1), channel_id=1, source_target_pairs={{0,16},{16,0},{1,17},{17,1},{2,18},{18,2},{3,19},{19,3},{4,20},{20... | collective-permute-start | bytes 393224 | tf_op jit(solution)/shard_map/ppermute | solution.py:370
  102.5 4.0 %collective-permute-start.9 = (f32[64,128]{1,0:T(8,128)S(1)}, f32[64,128]{1,0:T(8,128)S(1)}, u32[]{:S(2)}, u32[]{:S(2)}) collective-permute-start(f32[64,128]{1,0:T(8,128)S(1)} %add.98), channel_id=1, source_target_pairs={{0,2},{1,3},{2,0},{3,1},{4,6},{5,7},{6,4},{7,5},{8,10},{9,11},{10,... | collective-permute-start | bytes 98312 | tf_op jit(solution)/shard_map/ppermute | solution.py:449
  106.5 3.9 %collective-permute-start.10 = (f32[64,128]{1,0:T(8,128)S(1)}, f32[64,128]{1,0:T(8,128)S(1)}, u32[]{:S(2)}, u32[]{:S(2)}) collective-permute-start(f32[64,128]{1,0:T(8,128)S(1)} %add.99), channel_id=1, source_target_pairs={{0,4},{1,5},{2,6},{3,7},{4,0},{5,1},{6,2},{7,3},{8,12},{9,13},{10,... | collective-permute-start | bytes 98312 | tf_op jit(solution)/shard_map/ppermute | solution.py:449
  110.4 4.8 %collective-permute-start.11 = (f32[64,128]{1,0:T(8,128)S(1)}, f32[64,128]{1,0:T(8,128)S(1)}, u32[]{:S(2)}, u32[]{:S(2)}) collective-permute-start(f32[64,128]{1,0:T(8,128)S(1)} %add.100), channel_id=1, source_target_pairs={{0,8},{1,9},{2,10},{3,11},{4,12},{5,13},{6,14},{7,15},{8,0},{9,1},... | collective-permute-start | bytes 98312 | tf_op jit(solution)/shard_map/ppermute | solution.py:449

commit v6 on v5

--- a/solution.py
+++ b/solution.py
@@ -289,19 +289,29 @@
     )(me, stats)
 
 
-def analysis_kernel(bounds, sources, aliased, base_ref, mixer_ref, rest_ref, own_ref, *refs):
+def step_pieces(bounds, start, end):
+    pieces = []
+    for i, (lo, hi) in enumerate(bounds):
+        if lo < end and start < hi:
+            pieces.append((i, max(lo, start) - lo, min(hi, end) - lo))
+    return pieces
+
+
+def analysis_kernel(bounds, sources, skip, aliased, base_ref, mixer_ref, rest_ref, own_ref, *refs):
     out_ref = refs[len(bounds) * sources + aliased]
     everyone, width = out_ref.shape
     members = own_ref.shape[0]
-    step = pl.program_id(0)
     rest = rest_ref[:, 0:1]
-    for i, (lo, hi) in enumerate(bounds):
-
-        @pl.when((step >= lo) & (step < hi))
-        def _(i=i, lo=lo):
-            at = pl.ds(pl.multiple_of((step - lo) * width, width), width)
+    for step in range((bounds[-1][1] - bounds[0][0]) // width):
+
+        @pl.when(pl.program_id(0) == step)
+        def _(step=step):
+            start = (skip + step) * width
+            pieces = step_pieces(bounds, start, start + width)
             cols = [own_ref[...]]
-            cols += [ref[:, at] for ref in refs[i * sources : (i + 1) * sources]]
+            for source in range(sources):
+                parts = [refs[i * sources + source][:, lo:hi] for i, lo, hi in pieces]
+                cols.append(parts[0] if len(parts) == 1 else jnp.concatenate(parts, axis=1))
             if members % 16:
                 cols = [x.astype(jnp.float32) for x in cols]
             cols = jnp.concatenate(cols, axis=0).astype(jnp.bfloat16)
@@ -313,13 +323,11 @@
 def analyse(out, state, messages, mixer, rest, base, piece):
     members = state.shape[0]
     everyone = rest.shape[0]
-    first, last = messages[0][0], messages[-1][1]
-    width = piece // 4
-    for lo, hi, _ in messages:
-        width = math.gcd(width, lo, hi)
+    bounds = tuple((lo, hi) for lo, hi, _ in messages)
+    first, last = bounds[0][0], bounds[-1][1]
+    width = math.gcd(piece // 4, first, last)
     skip = first // width
     whole = piece // width
-    bounds = tuple((lo // width - skip, hi // width - skip) for lo, hi, _ in messages)
     received = [x for _, _, pieces in messages for x in pieces]
     aliased = int(out is not None)
     in_specs = [
@@ -335,7 +343,7 @@
         operands.append(out)
     return pl.pallas_call(
         functools.partial(
-            analysis_kernel, bounds, len(received) // len(messages), aliased
+            analysis_kernel, bounds, len(received) // len(messages), skip, aliased
         ),
         out_shape=jax.ShapeDtypeStruct((everyone, piece), jnp.bfloat16),
         grid_spec=pltpu.PrefetchScalarGridSpec(

time: 137 us -> 135 us (0.985)
  Pallas kernels: 35.9 us -> 34.2 us
    pallas_call x4, Pallas kernels: 11.4 us -> 9.75 us  [analyse(): pl.pallas_call(functools.partial(analysis_kernel, bounds, len(received) /...]
  transfers between devices with their start and end apart: 16 -> 16, of which waited for: 10 -> 10; matrix products, arithmetic and copies ran while one was open for 2% -> 2% of each run, Pallas kernels for 25% -> 24%
where the time goes in v6:
time: 135 us
  waiting for transfers between devices  68.9 us (51%)
  Pallas kernels  34.2 us (25%)
  starting transfers between devices  20.8 us (15%)
  local copies, waits for them, and re-layouts  9.63 us (7%)
    ppermute x5, waiting for transfers between devices, all_sum(): x = x + lax.ppermute(x, axis, [(j, j ^ 1 << i) for j in range(size)])  35.7 us
    ppermute x10, waiting for transfers between devices, to_lower(): lax.ppermute(array, 'mem', [(i, (i - shift) % nmem) for i in range(nmem)])  28.9 us
    ppermute x10, starting transfers between devices, to_lower(): lax.ppermute(array, 'mem', [(i, (i - shift) % nmem) for i in range(nmem)])  13.1 us
    pallas_call x6, Pallas kernels, statistics(): pl.pallas_call(functools.partial(statistics_kernel, parts, slots, group,...  10.1 us
    pallas_call x4, Pallas kernels, analyse(): pl.pallas_call(functools.partial(analysis_kernel, bounds, len(received) /...  9.75 us
    pallas_call x1, Pallas kernels, make_transform(): pl.pallas_call(functools.partial(transform_kernel, members), out_shape=(j...  9.65 us
    ppermute x5, starting transfers between devices, all_sum(): x = x + lax.ppermute(x, axis, [(j, j ^ 1 << i) for j in range(size)])  7.54 us
    unnamed x20, local copies, waits for them, and re-layouts  6.82 us
  transfers between devices with their start and end apart: 16, of which 10 were waited for; matrix products, arithmetic and copies ran while one was open for 2% of the time, Pallas kernels for 24%

profile of v6, /device:TPU:0, one launch (start us, length us, event | category | flops | bytes accessed | tf_op | source)
XLA Modules:
  0.0 134.7 jit_solution(13379642437261857215)
XLA Ops:
  1.8 3.0 %collective-permute-start.6 = (bf16[32,8192]{1,0:T(8,128)(2,1)S(1)}, bf16[32,8192]{1,0:T(8,128)(2,1)S(1)}, u32[]{:S(2)}, u32[]{:S(2)}) collective-permute-start(bf16[32,8192]{1,0:T(8,128)(2,1)S(1)} %cut.1), channel_id=1, source_target_pairs={{0,16},{16,0},{1,17},{17,1},{2,18},{18,2},{3,19},{19,3},{4,20},{20... | collective-permute-start | bytes 1572872 | tf_op jit(solution)/shard_map/ppermute | solution.py:378
  6.3 2.2 %copy-done = bf16[32,65536]{1,0:T(8,128)(2,1)S(1)} copy-done((bf16[32,65536]{1,0:T(8,128)(2,1)S(1)}, bf16[32,65536]{1,0:T(8,128)(2,1)}, u32[]{:S(2)}) %copy-start) | copy-done | bytes 4194328
  8.5 2.2 %copy-done.3 = bf16[32,65536]{1,0:T(8,128)(2,1)S(1)} copy-done((bf16[32,65536]{1,0:T(8,128)(2,1)S(1)}, bf16[32,65536]{1,0:T(8,128)(2,1)}, u32[]{:S(2)}) %copy-start.3) | copy-done | bytes 4194328
  10.7 2.3 %gather.2.refs_0_ = bf16[2,32,4096]{2,1,0:T(8,128)(2,1)S(1)} custom-call(s32[1]{0:T(128)} %bitcast.base_ref.me_ref, s32[2,32,128]{2,1,0:T(8,128)S(1)} %reshape.59.index_ref.refs_5_, bf16[32,65536]{1,0:T(8,128)(2,1)S(1)} %copy-done.3, bf16[32,65536]{1,0:T(8,128)(2,1)S(1)} %copy-done), custom_call_target="tpu_custom_call" | custom-call | tf_op jit(solution)/shard_map/gather/pallas_call | solution.py:105
  13.0 4.4 %collective-permute-done = s32[2,256,16]{1,2,0:T(8,128)S(1)} collective-permute-done((s32[2,256,16]{1,2,0:T(8,128)S(1)}, s32[2,256,16]{1,2,0:T(8,128)S(1)}, u32[]{:S(2)}, u32[]{:S(2)}) %collective-permute-start) | collective-permute-done | bytes 32800 | tf_op jit(solution)/shard_map/ppermute | solution.py:381
  17.7 2.2 %copy-done.1 = bf16[32,65536]{1,0:T(8,128)(2,1)S(1)} copy-done((bf16[32,65536]{1,0:T(8,128)(2,1)S(1)}, bf16[32,65536]{1,0:T(8,128)(2,1)}, u32[]{:S(2)}) %copy-start.1) | copy-done | bytes 4194328
  21.2 1.8 %collective-permute-start.5 = (bf16[1,32,3584]{2,1,0:T(8,128)(2,1)S(1)}, bf16[1,32,3584]{2,1,0:T(8,128)(2,1)S(1)}, u32[]{:S(2)}, u32[]{:S(2)}) collective-permute-start(bf16[1,32,3584]{2,1,0:T(8,128)(2,1)S(1)} %gather.3), channel_id=1, source_target_pairs={{0,16},{16,0},{1,17},{17,1},{2,18},{18,2},{3,19},{19,3},{4,20},{20... | collective-permute-start | bytes 688136 | tf_op jit(solution)/shard_map/ppermute | solution.py:378
  24.8 1.7 %collective-permute-start.3 = (bf16[32,8192]{1,0:T(8,128)(2,1)S(1)}, bf16[32,8192]{1,0:T(8,128)(2,1)S(1)}, u32[]{:S(2)}, u32[]{:S(2)}) collective-permute-start(bf16[32,8192]{1,0:T(8,128)(2,1)S(1)} %get-tuple-element.16), channel_id=1, source_target_pairs={{0,16},{16,0},{1,17},{17,1},{2,18},{18,2},{3,19},{19,3},{4,20},{20... | collective-permute-start | bytes 1572872 | tf_op jit(solution)/shard_map/ppermute | solution.py:378
  27.0 2.8 %collective-permute-done.5.refs_1_ = bf16[1,32,3584]{2,1,0:T(8,128)(2,1)S(1)} collective-permute-done((bf16[1,32,3584]{2,1,0:T(8,128)(2,1)S(1)}, bf16[1,32,3584]{2,1,0:T(8,128)(2,1)S(1)}, u32[]{:S(2)}, u32[]{:S(2)}) %collective-permute-start.5) | collective-permute-done | bytes 229408 | tf_op jit(solution)/shard_map/ppermute | solution.py:378
  29.8 1.7 %collective-permute-start.1 = (bf16[32,4096]{1,0:T(8,128)(2,1)S(1)}, bf16[32,4096]{1,0:T(8,128)(2,1)S(1)}, u32[]{:S(2)}, u32[]{:S(2)}) collective-permute-start(bf16[32,4096]{1,0:T(8,128)(2,1)S(1)} %constant_dynamic-slice_fusion.7), channel_id=1, source_target_pairs={{0,16},{16,0},{1,17},{17,1},{2,18},{18,2},{3,19},{19,3},{4,20},{20... | collective-permute-start | bytes 786440 | tf_op jit(solution)/shard_map/ppermute | solution.py:378
  31.8 1.5 %statistics.6.refs_5_ = f32[64,128]{1,0:T(8,128)S(1)} custom-call(s32[1]{0:T(128)} %bitcast.base_ref.me_ref, bf16[2,32,4096]{2,1,0:T(8,128)(2,1)S(1)} %gather.2.refs_0_, bf16[32,8192]{1,0:T(8,128)(2,1)S(1)} %collective-permute-done.6.refs_1_.refs_0_, f32[2,1,4096]{2,1,0:T(1,128)S(1)} %reshape.63.refs_2_, f32[2,1,4096]{2,1,0:T(1,128)S(1)} %reshape.64.refs_3_, ...), custom_call_target="tpu_custom_call" | custom-call | tf_op jit(solution)/shard_map/statistics/pallas_call | solution.py:213
  33.3 3.5 %statistics.7.refs_6_ = f32[64,128]{1,0:T(8,128)S(1)} custom-call(s32[1]{0:T(128)} %bitcast.base_ref.me_ref, bf16[2,32,4096]{2,1,0:T(8,128)(2,1)S(1)} %gather.2.refs_0_, bf16[1,32,3584]{2,1,0:T(8,128)(2,1)S(1)} %collective-permute-done.5.refs_1_, f32[2,1,4096]{2,1,0:T(1,128)S(1)} %reshape.63.refs_2_, f32[2,1,4096]{2,1,0:T(1,128)S(1)} %reshape.64.refs_3_, ...), custom_call_target="tpu_custom_call" | custom-call | tf_op jit(solution)/shard_map/statistics/pallas_call | solution.py:213
  36.8 4.2 %collective-permute-done.4.refs_1_ = bf16[32,8192]{1,0:T(8,128)(2,1)S(1)} collective-permute-done((bf16[32,8192]{1,0:T(8,128)(2,1)S(1)}, bf16[32,8192]{1,0:T(8,128)(2,1)S(1)}, u32[]{:S(2)}, u32[]{:S(2)}) %collective-permute-start.4) | collective-permute-done | bytes 524320 | tf_op jit(solution)/shard_map/ppermute | solution.py:378
  41.0 1.7 %collective-permute-start.13 = (bf16[32,8192]{1,0:T(8,128)(2,1)S(1)}, bf16[32,8192]{1,0:T(8,128)(2,1)S(1)}, u32[]{:S(2)}, u32[]{:S(2)}) collective-permute-start(bf16[32,8192]{1,0:T(8,128)(2,1)S(1)} %constant_dynamic-slice_fusion.2), channel_id=1, source_target_pairs={{0,16},{16,0},{1,17},{17,1},{2,18},{18,2},{3,19},{19,3},{4,20},{20... | collective-permute-start | bytes 1572872 | tf_op jit(solution)/shard_map/ppermute | solution.py:378
  42.7 1.5 %statistics.8.refs_6_ = f32[64,128]{1,0:T(8,128)S(1)} custom-call(s32[1]{0:T(128)} %bitcast.base_ref.me_ref, bf16[2,32,4096]{2,1,0:T(8,128)(2,1)S(1)} %gather.2.refs_0_, bf16[32,8192]{1,0:T(8,128)(2,1)S(1)} %collective-permute-done.4.refs_1_, f32[2,1,4096]{2,1,0:T(1,128)S(1)} %reshape.63.refs_2_, f32[2,1,4096]{2,1,0:T(1,128)S(1)} %reshape.64.refs_3_, ...), custom_call_target="tpu_custom_call" | custom-call | tf_op jit(solution)/shard_map/statistics/pallas_call | solution.py:213
  44.2 8.0 %collective-permute-done.3.refs_1_.refs_2_ = bf16[32,8192]{1,0:T(8,128)(2,1)S(1)} collective-permute-done((bf16[32,8192]{1,0:T(8,128)(2,1)S(1)}, bf16[32,8192]{1,0:T(8,128)(2,1)S(1)}, u32[]{:S(2)}, u32[]{:S(2)}) %collective-permute-start.3) | collective-permute-done | bytes 524320 | tf_op jit(solution)/shard_map/ppermute | solution.py:378
  52.2 1.5 %statistics.9.refs_6_ = f32[64,128]{1,0:T(8,128)S(1)} custom-call(s32[1]{0:T(128)} %bitcast.base_ref.me_ref, bf16[2,32,4096]{2,1,0:T(8,128)(2,1)S(1)} %gather.2.refs_0_, bf16[32,8192]{1,0:T(8,128)(2,1)S(1)} %collective-permute-done.3.refs_1_.refs_2_, f32[2,1,4096]{2,1,0:T(1,128)S(1)} %reshape.63.refs_2_, f32[2,1,4096]{2,1,0:T(1,128)S(1)} %reshape.64.refs_3_, ...), custom_call_target="tpu_custom_call" | custom-call | tf_op jit(solution)/shard_map/statistics/pallas_call | solution.py:213
  53.7 9.7 %collective-permute-done.2.refs_1_.refs_3_ = bf16[32,8192]{1,0:T(8,128)(2,1)S(1)} collective-permute-done((bf16[32,8192]{1,0:T(8,128)(2,1)S(1)}, bf16[32,8192]{1,0:T(8,128)(2,1)S(1)}, u32[]{:S(2)}, u32[]{:S(2)}) %collective-permute-start.2) | collective-permute-done | bytes 524320 | tf_op jit(solution)/shard_map/ppermute | solution.py:378
  64.9 4.1 %collective-permute-done.1.refs_1_.refs_0_ = bf16[32,4096]{1,0:T(8,128)(2,1)S(1)} collective-permute-done((bf16[32,4096]{1,0:T(8,128)(2,1)S(1)}, bf16[32,4096]{1,0:T(8,128)(2,1)S(1)}, u32[]{:S(2)}, u32[]{:S(2)}) %collective-permute-start.1) | collective-permute-done | bytes 262176 | tf_op jit(solution)/shard_map/ppermute | solution.py:378
  69.8 1.8 %collective-permute-start.7 = (f32[64,128]{1,0:T(8,128)S(1)}, f32[64,128]{1,0:T(8,128)S(1)}, u32[]{:S(2)}, u32[]{:S(2)}) collective-permute-start(f32[64,128]{1,0:T(8,128)S(1)} %statistics.11), channel_id=1, source_target_pairs={{0,16},{16,0},{1,17},{17,1},{2,18},{18,2},{3,19},{19,3},{4,20},{20... | collective-permute-start | bytes 98312 | tf_op jit(solution)/shard_map/ppermute | solution.py:457
  71.9 28.7 %collective-permute-done.7 = f32[64,128]{1,0:T(8,128)S(1)} collective-permute-done((f32[64,128]{1,0:T(8,128)S(1)}, f32[64,128]{1,0:T(8,128)S(1)}, u32[]{:S(2)}, u32[]{:S(2)}) %collective-permute-start.7) | collective-permute-done | bytes 32800 | tf_op jit(solution)/shard_map/ppermute | solution.py:457
  100.7 1.8 %collective-permute-start.14 = (bf16[32,2048]{1,0:T(8,128)(2,1)S(1)}, bf16[32,2048]{1,0:T(8,128)(2,1)S(1)}, u32[]{:S(2)}, u32[]{:S(2)}) collective-permute-start(bf16[32,2048]{1,0:T(8,128)(2,1)S(1)} %constant_dynamic-slice_fusion.1), channel_id=1, source_target_pairs={{0,16},{16,0},{1,17},{17,1},{2,18},{18,2},{3,19},{19,3},{4,20},{20... | collective-permute-start | bytes 393224 | tf_op jit(solution)/shard_map/ppermute | solution.py:378
  102.5 1.6 %collective-permute-start.9 = (f32[64,128]{1,0:T(8,128)S(1)}, f32[64,128]{1,0:T(8,128)S(1)}, u32[]{:S(2)}, u32[]{:S(2)}) collective-permute-start(f32[64,128]{1,0:T(8,128)S(1)} %add.98), channel_id=1, source_target_pairs={{0,2},{1,3},{2,0},{3,1},{4,6},{5,7},{6,4},{7,5},{8,10},{9,11},{10,... | collective-permute-start | bytes 98312 | tf_op jit(solution)/shard_map/ppermute | solution.py:457
  104.1 2.4 %collective-permute-done.9 = f32[64,128]{1,0:T(8,128)S(1)} collective-permute-done((f32[64,128]{1,0:T(8,128)S(1)}, f32[64,128]{1,0:T(8,128)S(1)}, u32[]{:S(2)}, u32[]{:S(2)}) %collective-permute-start.9) | collective-permute-done | bytes 32800 | tf_op jit(solution)/shard_map/ppermute | solution.py:457
  106.5 1.6 %collective-permute-start.10 = (f32[64,128]{1,0:T(8,128)S(1)}, f32[64,128]{1,0:T(8,128)S(1)}, u32[]{:S(2)}, u32[]{:S(2)}) collective-permute-start(f32[64,128]{1,0:T(8,128)S(1)} %add.99), channel_id=1, source_target_pairs={{0,4},{1,5},{2,6},{3,7},{4,0},{5,1},{6,2},{7,3},{8,12},{9,13},{10,... | collective-permute-start | bytes 98312 | tf_op jit(solution)/shard_map/ppermute | solution.py:457
  108.1 2.3 %collective-permute-done.10 = f32[64,128]{1,0:T(8,128)S(1)} collective-permute-done((f32[64,128]{1,0:T(8,128)S(1)}, f32[64,128]{1,0:T(8,128)S(1)}, u32[]{:S(2)}, u32[]{:S(2)}) %collective-permute-start.10) | collective-permute-done | bytes 32800 | tf_op jit(solution)/shard_map/ppermute | solution.py:457
  110.4 2.6 %collective-permute-start.11 = (f32[64,128]{1,0:T(8,128)S(1)}, f32[64,128]{1,0:T(8,128)S(1)}, u32[]{:S(2)}, u32[]{:S(2)}) collective-permute-start(f32[64,128]{1,0:T(8,128)S(1)} %add.100), channel_id=1, source_target_pairs={{0,8},{1,9},{2,10},{3,11},{4,12},{5,13},{6,14},{7,15},{8,0},{9,1},... | collective-permute-start | bytes 98312 | tf_op jit(solution)/shard_map/ppermute | solution.py:457
  113.0 2.2 %collective-permute-done.11 = f32[64,128]{1,0:T(8,128)S(1)} collective-permute-done((f32[64,128]{1,0:T(8,128)S(1)}, f32[64,128]{1,0:T(8,128)S(1)}, u32[]{:S(2)}, u32[]{:S(2)}) %collective-permute-start.11) | collective-permute-done | bytes 32800 | tf_op jit(solution)/shard_map/ppermute | solution.py:457
  115.3 9.6 %transform.1 = (f32[64,64]{1,0:T(8,128)}, bf16[80,64]{1,0:T(8,128)(2,1)S(1)}, f32[64,128]{1,0:T(8,128)S(1)}) custom-call(s32[1]{0:T(128)} %bitcast.base_ref.me_ref, f32[64,128]{1,0:T(8,128)S(1)} %add.101.stats_ref), custom_call_target="tpu_custom_call" | custom-call | tf_op jit(solution)/shard_map/transform/pallas_call | solution.py:278
  124.9 3.6 %analysis.4 = bf16[64,32768]{1,0:T(8,128)(2,1)} custom-call(s32[1]{0:T(128)} %bitcast.base_ref.me_ref, bf16[80,64]{1,0:T(8,128)(2,1)S(1)} %get-tuple-element.11.mixer_ref, f32[64,128]{1,0:T(8,128)S(1)} %get-tuple-element.12.rest_ref, bf16[32,65536]{1,0:T(8,128)(2,1)S(1)} %copy-done.4, bf16[32,8192]{1,0:T(8,128)(2,1)S(1)} %collective-permute-done.6.refs_1_.refs_0_, ...), custom_call_target="tpu_custom_call" | custom-call | tf_op jit(solution)/shard_map/analysis/pallas_call | solution.py:344
  128.6 3.5 %analysis.5.refs_1_ = bf16[64,32768]{1,0:T(8,128)(2,1)} custom-call(s32[1]{0:T(128)} %bitcast.base_ref.me_ref, bf16[80,64]{1,0:T(8,128)(2,1)S(1)} %get-tuple-element.11.mixer_ref, f32[64,128]{1,0:T(8,128)S(1)} %get-tuple-element.12.rest_ref, bf16[32,65536]{1,0:T(8,128)(2,1)S(1)} %copy-done.2, bf16[32,4096]{1,0:T(8,128)(2,1)S(1)} %collective-permute-done.1.refs_1_.refs_0_, ...), custom_call_target="tpu_custom_call" | custom-call | tf_op jit(solution)/shard_map/analysis/pallas_call | solution.py:344
  132.0 1.5 %analysis.6.refs_1_ = bf16[64,32768]{1,0:T(8,128)(2,1)} custom-call(s32[1]{0:T(128)} %bitcast.base_ref.me_ref, bf16[80,64]{1,0:T(8,128)(2,1)S(1)} %get-tuple-element.11.mixer_ref, f32[64,128]{1,0:T(8,128)S(1)} %get-tuple-element.12.rest_ref, bf16[32,65536]{1,0:T(8,128)(2,1)S(1)} %copy-done.2, ...), custom_call_target="tpu_custom_call", output_to_operand_aliasing={{}: (5, {})} | custom-call | tf_op jit(solution)/shard_map/analysis/pallas_call | solution.py:344
  (57 shorter events, 10.3 us)
Async XLA Ops:
  0.6 4.2 %copy-start.6 = (s32[2,256,16]{1,2,0:T(8,128)S(1)}, s32[2,256,16]{1,2,0:T(8,128)}, u32[]{:S(2)}) copy-start(s32[2,256,16]{1,2,0:T(8,128)} %param.8) | copy-start | bytes 98308
  0.6 4.3 %copy-start.8 = (s32[2,256]{1,0:T(2,128)S(1)}, s32[2,256]{1,0:T(2,128)}, u32[]{:S(2)}) copy-start(s32[2,256]{1,0:T(2,128)} %param.9) | copy-start | bytes 6148
  0.7 4.7 %copy-start.7 = (f32[2,256,16]{1,2,0:T(8,128)S(1)}, f32[2,256,16]{1,2,0:T(8,128)}, u32[]{:S(2)}) copy-start(f32[2,256,16]{1,2,0:T(8,128)} %param.11) | copy-start | bytes 98308
  0.7 5.3 %copy-start.5 = (f32[2,256,16]{1,2,0:T(8,128)S(1)}, f32[2,256,16]{1,2,0:T(8,128)}, u32[]{:S(2)}) copy-start(f32[2,256,16]{1,2,0:T(8,128)} %param.10) | copy-start | bytes 98308
  1.8 29.7 %collective-permute-start.6 = (bf16[32,8192]{1,0:T(8,128)(2,1)S(1)}, bf16[32,8192]{1,0:T(8,128)(2,1)S(1)}, u32[]{:S(2)}, u32[]{:S(2)}) collective-permute-start(bf16[32,8192]{1,0:T(8,128)(2,1)S(1)} %cut.1), channel_id=1, source_target_pairs={{0,16},{16,0},{1,17},{17,1},{2,18},{18,2},{3,19},{19,3},{4,20},{20... | collective-permute-start | bytes 1572872 | tf_op jit(solution)/shard_map/ppermute | solution.py:378
  4.8 12.6 %collective-permute-start = (s32[2,256,16]{1,2,0:T(8,128)S(1)}, s32[2,256,16]{1,2,0:T(8,128)S(1)}, u32[]{:S(2)}, u32[]{:S(2)}) collective-permute-start(s32[2,256,16]{1,2,0:T(8,128)S(1)} %copy-done.6), channel_id=1, source_target_pairs={{0,16},{16,0},{1,17},{17,1},{2,18},{18,2},{3,19},{19,3},{4,20},{20... | collective-permute-start | bytes 98312 | tf_op jit(solution)/shard_map/ppermute | solution.py:381
  6.3 2.2 %copy-start = (bf16[32,65536]{1,0:T(8,128)(2,1)S(1)}, bf16[32,65536]{1,0:T(8,128)(2,1)}, u32[]{:S(2)}) copy-start(bf16[32,65536]{1,0:T(8,128)(2,1)} %own_ref.7) | copy-start | bytes 12582916
  8.5 2.2 %copy-start.3 = (bf16[32,65536]{1,0:T(8,128)(2,1)S(1)}, bf16[32,65536]{1,0:T(8,128)(2,1)}, u32[]{:S(2)}) copy-start(bf16[32,65536]{1,0:T(8,128)(2,1)} %own_ref.4) | copy-start | bytes 12582916
  17.7 2.2 %copy-start.1 = (bf16[32,65536]{1,0:T(8,128)(2,1)S(1)}, bf16[32,65536]{1,0:T(8,128)(2,1)}, u32[]{:S(2)}) copy-start(bf16[32,65536]{1,0:T(8,128)(2,1)} %own_ref.7) | copy-start | bytes 12582916
  19.9 7.0 %copy-start.2 = (bf16[32,65536]{1,0:T(8,128)(2,1)S(1)}, bf16[32,65536]{1,0:T(8,128)(2,1)}, u32[]{:S(2)}) copy-start(bf16[32,65536]{1,0:T(8,128)(2,1)} %own_ref.7) | copy-start | bytes 12582916
  21.2 8.5 %collective-permute-start.5 = (bf16[1,32,3584]{2,1,0:T(8,128)(2,1)S(1)}, bf16[1,32,3584]{2,1,0:T(8,128)(2,1)S(1)}, u32[]{:S(2)}, u32[]{:S(2)}) collective-permute-start(bf16[1,32,3584]{2,1,0:T(8,128)(2,1)S(1)} %gather.3), channel_id=1, source_target_pairs={{0,16},{16,0},{1,17},{17,1},{2,18},{18,2},{3,19},{19,3},{4,20},{20... | collective-permute-start | bytes 688136 | tf_op jit(solution)/shard_map/ppermute | solution.py:378
  24.5 16.5 %collective-permute-start.4 = (bf16[32,8192]{1,0:T(8,128)(2,1)S(1)}, bf16[32,8192]{1,0:T(8,128)(2,1)S(1)}, u32[]{:S(2)}, u32[]{:S(2)}) collective-permute-start(bf16[32,8192]{1,0:T(8,128)(2,1)S(1)} %get-tuple-element.15), channel_id=1, source_target_pairs={{0,16},{16,0},{1,17},{17,1},{2,18},{18,2},{3,19},{19,3},{4,20},{20... | collective-permute-start | bytes 1572872 | tf_op jit(solution)/shard_map/ppermute | solution.py:378
  24.8 27.4 %collective-permute-start.3 = (bf16[32,8192]{1,0:T(8,128)(2,1)S(1)}, bf16[32,8192]{1,0:T(8,128)(2,1)S(1)}, u32[]{:S(2)}, u32[]{:S(2)}) collective-permute-start(bf16[32,8192]{1,0:T(8,128)(2,1)S(1)} %get-tuple-element.16), channel_id=1, source_target_pairs={{0,16},{16,0},{1,17},{17,1},{2,18},{18,2},{3,19},{19,3},{4,20},{20... | collective-permute-start | bytes 1572872 | tf_op jit(solution)/shard_map/ppermute | solution.py:378
  26.6 36.9 %collective-permute-start.2 = (bf16[32,8192]{1,0:T(8,128)(2,1)S(1)}, bf16[32,8192]{1,0:T(8,128)(2,1)S(1)}, u32[]{:S(2)}, u32[]{:S(2)}) collective-permute-start(bf16[32,8192]{1,0:T(8,128)(2,1)S(1)} %get-tuple-element.17), channel_id=1, source_target_pairs={{0,16},{16,0},{1,17},{17,1},{2,18},{18,2},{3,19},{19,3},{4,20},{20... | collective-permute-start | bytes 1572872 | tf_op jit(solution)/shard_map/ppermute | solution.py:378
  29.8 39.3 %collective-permute-start.1 = (bf16[32,4096]{1,0:T(8,128)(2,1)S(1)}, bf16[32,4096]{1,0:T(8,128)(2,1)S(1)}, u32[]{:S(2)}, u32[]{:S(2)}) collective-permute-start(bf16[32,4096]{1,0:T(8,128)(2,1)S(1)} %constant_dynamic-slice_fusion.7), channel_id=1, source_target_pairs={{0,16},{16,0},{1,17},{17,1},{2,18},{18,2},{3,19},{19,3},{4,20},{20... | collective-permute-start | bytes 786440 | tf_op jit(solution)/shard_map/ppermute | solution.py:378
  31.5 97.1 %collective-permute-start.15 = (bf16[32,14336]{1,0:T(8,128)(2,1)S(1)}, bf16[32,14336]{1,0:T(8,128)(2,1)S(1)}, u32[]{:S(2)}, u32[]{:S(2)}) collective-permute-start(bf16[32,14336]{1,0:T(8,128)(2,1)S(1)} %constant_dynamic-slice_fusion), channel_id=1, source_target_pairs={{0,16},{16,0},{1,17},{17,1},{2,18},{18,2},{3,19},{19,3},{4,20},{20... | collective-permute-start | bytes 2752520 | tf_op jit(solution)/shard_map/ppermute | solution.py:378
  31.8 93.1 %copy-start.4 = (bf16[32,65536]{1,0:T(8,128)(2,1)S(1)}, bf16[32,65536]{1,0:T(8,128)(2,1)}, u32[]{:S(2)}) copy-start(bf16[32,65536]{1,0:T(8,128)(2,1)} %own_ref.4) | copy-start | bytes 12582916
  41.0 91.0 %collective-permute-start.13 = (bf16[32,8192]{1,0:T(8,128)(2,1)S(1)}, bf16[32,8192]{1,0:T(8,128)(2,1)S(1)}, u32[]{:S(2)}, u32[]{:S(2)}) collective-permute-start(bf16[32,8192]{1,0:T(8,128)(2,1)S(1)} %constant_dynamic-slice_fusion.2), channel_id=1, source_target_pairs={{0,16},{16,0},{1,17},{17,1},{2,18},{18,2},{3,19},{19,3},{4,20},{20... | collective-permute-start | bytes 1572872 | tf_op jit(solution)/shard_map/ppermute | solution.py:378
  69.8 30.9 %collective-permute-start.7 = (f32[64,128]{1,0:T(8,128)S(1)}, f32[64,128]{1,0:T(8,128)S(1)}, u32[]{:S(2)}, u32[]{:S(2)}) collective-permute-start(f32[64,128]{1,0:T(8,128)S(1)} %statistics.11), channel_id=1, source_target_pairs={{0,16},{16,0},{1,17},{17,1},{2,18},{18,2},{3,19},{19,3},{4,20},{20... | collective-permute-start | bytes 98312 | tf_op jit(solution)/shard_map/ppermute | solution.py:457
  71.6 62.0 %collective-permute-start.12 = (bf16[32,4096]{1,0:T(8,128)(2,1)S(1)}, bf16[32,4096]{1,0:T(8,128)(2,1)S(1)}, u32[]{:S(2)}, u32[]{:S(2)}) collective-permute-start(bf16[32,4096]{1,0:T(8,128)(2,1)S(1)} %constant_dynamic-slice_fusion.3), channel_id=1, source_target_pairs={{0,16},{16,0},{1,17},{17,1},{2,18},{18,2},{3,19},{19,3},{4,20},{20... | collective-permute-start | bytes 786440 | tf_op jit(solution)/shard_map/ppermute | solution.py:378
  100.7 1.8 %collective-permute-start.8 = (f32[64,128]{1,0:T(8,128)S(1)}, f32[64,128]{1,0:T(8,128)S(1)}, u32[]{:S(2)}, u32[]{:S(2)}) collective-permute-start(f32[64,128]{1,0:T(8,128)S(1)} %add.97), channel_id=1, source_target_pairs={{0,1},{1,0},{2,3},{3,2},{4,5},{5,4},{6,7},{7,6},{8,9},{9,8},{10,11... | collective-permute-start | bytes 98312 | tf_op jit(solution)/shard_map/ppermute | solution.py:457
  100.7 27.8 %collective-permute-start.14 = (bf16[32,2048]{1,0:T(8,128)(2,1)S(1)}, bf16[32,2048]{1,0:T(8,128)(2,1)S(1)}, u32[]{:S(2)}, u32[]{:S(2)}) collective-permute-start(bf16[32,2048]{1,0:T(8,128)(2,1)S(1)} %constant_dynamic-slice_fusion.1), channel_id=1, source_target_pairs={{0,16},{16,0},{1,17},{17,1},{2,18},{18,2},{3,19},{19,3},{4,20},{20... | collective-permute-start | bytes 393224 | tf_op jit(solution)/shard_map/ppermute | solution.py:378
  102.5 4.0 %collective-permute-start.9 = (f32[64,128]{1,0:T(8,128)S(1)}, f32[64,128]{1,0:T(8,128)S(1)}, u32[]{:S(2)}, u32[]{:S(2)}) collective-permute-start(f32[64,128]{1,0:T(8,128)S(1)} %add.98), channel_id=1, source_target_pairs={{0,2},{1,3},{2,0},{3,1},{4,6},{5,7},{6,4},{7,5},{8,10},{9,11},{10,... | collective-permute-start | bytes 98312 | tf_op jit(solution)/shard_map/ppermute | solution.py:457
  106.5 3.9 %collective-permute-start.10 = (f32[64,128]{1,0:T(8,128)S(1)}, f32[64,128]{1,0:T(8,128)S(1)}, u32[]{:S(2)}, u32[]{:S(2)}) collective-permute-start(f32[64,128]{1,0:T(8,128)S(1)} %add.99), channel_id=1, source_target_pairs={{0,4},{1,5},{2,6},{3,7},{4,0},{5,1},{6,2},{7,3},{8,12},{9,13},{10,... | collective-permute-start | bytes 98312 | tf_op jit(solution)/shard_map/ppermute | solution.py:457
  110.4 4.8 %collective-permute-start.11 = (f32[64,128]{1,0:T(8,128)S(1)}, f32[64,128]{1,0:T(8,128)S(1)}, u32[]{:S(2)}, u32[]{:S(2)}) collective-permute-start(f32[64,128]{1,0:T(8,128)S(1)} %add.100), channel_id=1, source_target_pairs={{0,8},{1,9},{2,10},{3,11},{4,12},{5,13},{6,14},{7,15},{8,0},{9,1},... | collective-permute-start | bytes 98312 | tf_op jit(solution)/shard_map/ppermute | solution.py:457

commit v7 on v6

--- a/solution.py
+++ b/solution.py
@@ -16,18 +16,16 @@
 
 MESSAGES = (
     (0, 0, 8),
-    (0, 8, 16),
-    (0, 16, 24),
-    (0, 24, 32),
+    (0, 8, 32),
     (1, 0, 4),
     (1, 4, 6),
     (1, 6, 20),
     (1, 20, 28),
     (1, 28, 32),
 )
-READ = (0, 1, 2, 3, 4)
+READ = (0, 1, 2)
 SENT = (1, 1)
-CALLS = ((0, 1, 2, 3), (4, 5, 6), (7,), (8,))
+CALLS = ((0, 1), (2, 3, 4), (5,), (6,))
 
 
 def split(x):

time: 135 us -> 135 us (level)
  starting transfers between devices: 20.8 us -> 18.9 us
  waiting for transfers between devices: 68.9 us -> 70.8 us
    ppermute x10 -> x8, waiting for transfers between devices: 28.9 us -> 30.7 us  [to_lower(): lax.ppermute(array, 'mem', [(i, (i - shift) % nmem) for i in range(nmem)])]
    ppermute x10 -> x8, starting transfers between devices: 13.1 us -> 11.3 us  [to_lower(): lax.ppermute(array, 'mem', [(i, (i - shift) % nmem) for i in range(nmem)])]
    pallas_call x6 -> x4, Pallas kernels: 10.1 us -> 10.1 us  [statistics(): pl.pallas_call(functools.partial(statistics_kernel, parts, slots, group,...]
  transfers between devices with their start and end apart: 16 -> 14, of which waited for: 10 -> 7; matrix products, arithmetic and copies ran while one was open for 2% -> 2% of each run, Pallas kernels for 24% -> 24%
where the time goes in v7:
time: 135 us
  waiting for transfers between devices  70.8 us (52%)
  Pallas kernels  34.2 us (25%)
  starting transfers between devices  18.9 us (14%)
  local copies, waits for them, and re-layouts  9.67 us (7%)
    ppermute x5, waiting for transfers between devices, all_sum(): x = x + lax.ppermute(x, axis, [(j, j ^ 1 << i) for j in range(size)])  35.7 us
    ppermute x8, waiting for transfers between devices, to_lower(): lax.ppermute(array, 'mem', [(i, (i - shift) % nmem) for i in range(nmem)])  30.7 us
    ppermute x8, starting transfers between devices, to_lower(): lax.ppermute(array, 'mem', [(i, (i - shift) % nmem) for i in range(nmem)])  11.3 us
    pallas_call x4, Pallas kernels, statistics(): pl.pallas_call(functools.partial(statistics_kernel, parts, slots, group,...  10.1 us
    pallas_call x4, Pallas kernels, analyse(): pl.pallas_call(functools.partial(analysis_kernel, bounds, len(received) /...  9.76 us
    pallas_call x1, Pallas kernels, make_transform(): pl.pallas_call(functools.partial(transform_kernel, members), out_shape=(j...  9.65 us
    ppermute x5, starting transfers between devices, all_sum(): x = x + lax.ppermute(x, axis, [(j, j ^ 1 << i) for j in range(size)])  7.54 us
    unnamed x20, local copies, waits for them, and re-layouts  6.82 us
  transfers between devices with their start and end apart: 14, of which 7 were waited for; matrix products, arithmetic and copies ran while one was open for 2% of the time, Pallas kernels for 24%

profile of v7, /device:TPU:0, one launch (start us, length us, event | category | flops | bytes accessed | tf_op | source)
XLA Modules:
  0.0 134.7 jit_solution(4242256061363536596)
XLA Ops:
  0.7 1.1 cut.1
  1.8 3.0 %collective-permute-start.4 = (bf16[32,8192]{1,0:T(8,128)(2,1)S(1)}, bf16[32,8192]{1,0:T(8,128)(2,1)S(1)}, u32[]{:S(2)}, u32[]{:S(2)}) collective-permute-start(bf16[32,8192]{1,0:T(8,128)(2,1)S(1)} %cut.1), channel_id=1, source_target_pairs={{0,16},{16,0},{1,17},{17,1},{2,18},{18,2},{3,19},{19,3},{4,20},{20... | collective-permute-start | bytes 1572872 | tf_op jit(solution)/shard_map/ppermute | solution.py:376
  6.3 2.2 %copy-done = bf16[32,65536]{1,0:T(8,128)(2,1)S(1)} copy-done((bf16[32,65536]{1,0:T(8,128)(2,1)S(1)}, bf16[32,65536]{1,0:T(8,128)(2,1)}, u32[]{:S(2)}) %copy-start) | copy-done | bytes 4194328
  8.5 2.2 %copy-done.3 = bf16[32,65536]{1,0:T(8,128)(2,1)S(1)} copy-done((bf16[32,65536]{1,0:T(8,128)(2,1)S(1)}, bf16[32,65536]{1,0:T(8,128)(2,1)}, u32[]{:S(2)}) %copy-start.3) | copy-done | bytes 4194328
  10.6 2.3 %gather.2.refs_0_ = bf16[2,32,4096]{2,1,0:T(8,128)(2,1)S(1)} custom-call(s32[1]{0:T(128)} %bitcast.base_ref.me_ref, s32[2,32,128]{2,1,0:T(8,128)S(1)} %reshape.59.index_ref.refs_5_, bf16[32,65536]{1,0:T(8,128)(2,1)S(1)} %copy-done.3, bf16[32,65536]{1,0:T(8,128)(2,1)S(1)} %copy-done), custom_call_target="tpu_custom_call" | custom-call | tf_op jit(solution)/shard_map/gather/pallas_call | solution.py:103
  13.0 4.4 %collective-permute-done = s32[2,256,16]{1,2,0:T(8,128)S(1)} collective-permute-done((s32[2,256,16]{1,2,0:T(8,128)S(1)}, s32[2,256,16]{1,2,0:T(8,128)S(1)}, u32[]{:S(2)}, u32[]{:S(2)}) %collective-permute-start) | collective-permute-done | bytes 32800 | tf_op jit(solution)/shard_map/ppermute | solution.py:379
  17.7 2.2 %copy-done.1 = bf16[32,65536]{1,0:T(8,128)(2,1)S(1)} copy-done((bf16[32,65536]{1,0:T(8,128)(2,1)S(1)}, bf16[32,65536]{1,0:T(8,128)(2,1)}, u32[]{:S(2)}) %copy-start.1) | copy-done | bytes 4194328
  19.9 1.3 gather.3
  21.2 1.8 %collective-permute-start.3 = (bf16[1,32,3584]{2,1,0:T(8,128)(2,1)S(1)}, bf16[1,32,3584]{2,1,0:T(8,128)(2,1)S(1)}, u32[]{:S(2)}, u32[]{:S(2)}) collective-permute-start(bf16[1,32,3584]{2,1,0:T(8,128)(2,1)S(1)} %gather.3), channel_id=1, source_target_pairs={{0,16},{16,0},{1,17},{17,1},{2,18},{18,2},{3,19},{19,3},{4,20},{20... | collective-permute-start | bytes 688136 | tf_op jit(solution)/shard_map/ppermute | solution.py:376
  23.0 1.5 %constant_dynamic-slice_fusion.4 = bf16[32,24576]{1,0:T(8,128)(2,1)S(1)} fusion(bf16[32,65536]{1,0:T(8,128)(2,1)} %own_ref.4, s32[]{:T(128)S(6)} %select_n.19), kind=kLoop, calls=%fused_computation.7 | loop fusion | bytes 3145732 | tf_op jit(solution)/shard_map/dynamic_slice | solution.py:384
  24.9 1.8 %collective-permute-start.1 = (bf16[32,4096]{1,0:T(8,128)(2,1)S(1)}, bf16[32,4096]{1,0:T(8,128)(2,1)S(1)}, u32[]{:S(2)}, u32[]{:S(2)}) collective-permute-start(bf16[32,4096]{1,0:T(8,128)(2,1)S(1)} %constant_dynamic-slice_fusion.5), channel_id=1, source_target_pairs={{0,16},{16,0},{1,17},{17,1},{2,18},{18,2},{3,19},{19,3},{4,20},{20... | collective-permute-start | bytes 786440 | tf_op jit(solution)/shard_map/ppermute | solution.py:376
  27.2 1.8 %collective-permute-start.11 = (bf16[32,8192]{1,0:T(8,128)(2,1)S(1)}, bf16[32,8192]{1,0:T(8,128)(2,1)S(1)}, u32[]{:S(2)}, u32[]{:S(2)}) collective-permute-start(bf16[32,8192]{1,0:T(8,128)(2,1)S(1)} %constant_dynamic-slice_fusion.2), channel_id=1, source_target_pairs={{0,16},{16,0},{1,17},{17,1},{2,18},{18,2},{3,19},{19,3},{4,20},{20... | collective-permute-start | bytes 1572872 | tf_op jit(solution)/shard_map/ppermute | solution.py:376
  29.0 1.5 %statistics.4.refs_5_ = f32[64,128]{1,0:T(8,128)S(1)} custom-call(s32[1]{0:T(128)} %bitcast.base_ref.me_ref, bf16[2,32,4096]{2,1,0:T(8,128)(2,1)S(1)} %gather.2.refs_0_, bf16[32,8192]{1,0:T(8,128)(2,1)S(1)} %collective-permute-done.4.refs_1_.refs_0_, f32[2,1,4096]{2,1,0:T(1,128)S(1)} %reshape.63.refs_2_, f32[2,1,4096]{2,1,0:T(1,128)S(1)} %reshape.64.refs_3_, ...), custom_call_target="tpu_custom_call" | custom-call | tf_op jit(solution)/shard_map/statistics/pallas_call | solution.py:211
  30.5 3.5 %statistics.5.refs_6_ = f32[64,128]{1,0:T(8,128)S(1)} custom-call(s32[1]{0:T(128)} %bitcast.base_ref.me_ref, bf16[2,32,4096]{2,1,0:T(8,128)(2,1)S(1)} %gather.2.refs_0_, bf16[1,32,3584]{2,1,0:T(8,128)(2,1)S(1)} %collective-permute-done.3.refs_1_, f32[2,1,4096]{2,1,0:T(1,128)S(1)} %reshape.63.refs_2_, f32[2,1,4096]{2,1,0:T(1,128)S(1)} %reshape.64.refs_3_, ...), custom_call_target="tpu_custom_call" | custom-call | tf_op jit(solution)/shard_map/statistics/pallas_call | solution.py:211
  33.9 29.5 %collective-permute-done.2.refs_1_ = bf16[32,24576]{1,0:T(8,128)(2,1)S(1)} collective-permute-done((bf16[32,24576]{1,0:T(8,128)(2,1)S(1)}, bf16[32,24576]{1,0:T(8,128)(2,1)S(1)}, u32[]{:S(2)}, u32[]{:S(2)}) %collective-permute-start.2) | collective-permute-done | bytes 1572896 | tf_op jit(solution)/shard_map/ppermute | solution.py:376
  63.5 4.4 %statistics.6.refs_6_ = f32[64,128]{1,0:T(8,128)S(1)} custom-call(s32[1]{0:T(128)} %bitcast.base_ref.me_ref, bf16[2,32,4096]{2,1,0:T(8,128)(2,1)S(1)} %gather.2.refs_0_, bf16[32,24576]{1,0:T(8,128)(2,1)S(1)} %collective-permute-done.2.refs_1_, f32[2,1,4096]{2,1,0:T(1,128)S(1)} %reshape.63.refs_2_, f32[2,1,4096]{2,1,0:T(1,128)S(1)} %reshape.64.refs_3_, ...), custom_call_target="tpu_custom_call" | custom-call | tf_op jit(solution)/shard_map/statistics/pallas_call | solution.py:211
  67.9 1.2 collective-permute-done.1.refs_1_.refs_0_
  69.1 0.7 statistics.7
  69.8 1.8 %collective-permute-start.5 = (f32[64,128]{1,0:T(8,128)S(1)}, f32[64,128]{1,0:T(8,128)S(1)}, u32[]{:S(2)}, u32[]{:S(2)}) collective-permute-start(f32[64,128]{1,0:T(8,128)S(1)} %statistics.7), channel_id=1, source_target_pairs={{0,16},{16,0},{1,17},{17,1},{2,18},{18,2},{3,19},{19,3},{4,20},{20... | collective-permute-start | bytes 98312 | tf_op jit(solution)/shard_map/ppermute | solution.py:455
  71.9 28.7 %collective-permute-done.5 = f32[64,128]{1,0:T(8,128)S(1)} collective-permute-done((f32[64,128]{1,0:T(8,128)S(1)}, f32[64,128]{1,0:T(8,128)S(1)}, u32[]{:S(2)}, u32[]{:S(2)}) %collective-permute-start.5) | collective-permute-done | bytes 32800 | tf_op jit(solution)/shard_map/ppermute | solution.py:455
  100.7 1.8 %collective-permute-start.12 = (bf16[32,2048]{1,0:T(8,128)(2,1)S(1)}, bf16[32,2048]{1,0:T(8,128)(2,1)S(1)}, u32[]{:S(2)}, u32[]{:S(2)}) collective-permute-start(bf16[32,2048]{1,0:T(8,128)(2,1)S(1)} %constant_dynamic-slice_fusion.1), channel_id=1, source_target_pairs={{0,16},{16,0},{1,17},{17,1},{2,18},{18,2},{3,19},{19,3},{4,20},{20... | collective-permute-start | bytes 393224 | tf_op jit(solution)/shard_map/ppermute | solution.py:376
  102.5 1.6 %collective-permute-start.7 = (f32[64,128]{1,0:T(8,128)S(1)}, f32[64,128]{1,0:T(8,128)S(1)}, u32[]{:S(2)}, u32[]{:S(2)}) collective-permute-start(f32[64,128]{1,0:T(8,128)S(1)} %add.76), channel_id=1, source_target_pairs={{0,2},{1,3},{2,0},{3,1},{4,6},{5,7},{6,4},{7,5},{8,10},{9,11},{10,... | collective-permute-start | bytes 98312 | tf_op jit(solution)/shard_map/ppermute | solution.py:455
  104.1 2.4 %collective-permute-done.7 = f32[64,128]{1,0:T(8,128)S(1)} collective-permute-done((f32[64,128]{1,0:T(8,128)S(1)}, f32[64,128]{1,0:T(8,128)S(1)}, u32[]{:S(2)}, u32[]{:S(2)}) %collective-permute-start.7) | collective-permute-done | bytes 32800 | tf_op jit(solution)/shard_map/ppermute | solution.py:455
  106.5 1.6 %collective-permute-start.8 = (f32[64,128]{1,0:T(8,128)S(1)}, f32[64,128]{1,0:T(8,128)S(1)}, u32[]{:S(2)}, u32[]{:S(2)}) collective-permute-start(f32[64,128]{1,0:T(8,128)S(1)} %add.77), channel_id=1, source_target_pairs={{0,4},{1,5},{2,6},{3,7},{4,0},{5,1},{6,2},{7,3},{8,12},{9,13},{10,... | collective-permute-start | bytes 98312 | tf_op jit(solution)/shard_map/ppermute | solution.py:455
  108.1 2.3 %collective-permute-done.8 = f32[64,128]{1,0:T(8,128)S(1)} collective-permute-done((f32[64,128]{1,0:T(8,128)S(1)}, f32[64,128]{1,0:T(8,128)S(1)}, u32[]{:S(2)}, u32[]{:S(2)}) %collective-permute-start.8) | collective-permute-done | bytes 32800 | tf_op jit(solution)/shard_map/ppermute | solution.py:455
  110.4 2.6 %collective-permute-start.9 = (f32[64,128]{1,0:T(8,128)S(1)}, f32[64,128]{1,0:T(8,128)S(1)}, u32[]{:S(2)}, u32[]{:S(2)}) collective-permute-start(f32[64,128]{1,0:T(8,128)S(1)} %add.78), channel_id=1, source_target_pairs={{0,8},{1,9},{2,10},{3,11},{4,12},{5,13},{6,14},{7,15},{8,0},{9,1},... | collective-permute-start | bytes 98312 | tf_op jit(solution)/shard_map/ppermute | solution.py:455
  113.0 2.2 %collective-permute-done.9 = f32[64,128]{1,0:T(8,128)S(1)} collective-permute-done((f32[64,128]{1,0:T(8,128)S(1)}, f32[64,128]{1,0:T(8,128)S(1)}, u32[]{:S(2)}, u32[]{:S(2)}) %collective-permute-start.9) | collective-permute-done | bytes 32800 | tf_op jit(solution)/shard_map/ppermute | solution.py:455
  115.3 9.6 %transform.1 = (f32[64,64]{1,0:T(8,128)}, bf16[80,64]{1,0:T(8,128)(2,1)S(1)}, f32[64,128]{1,0:T(8,128)S(1)}) custom-call(s32[1]{0:T(128)} %bitcast.base_ref.me_ref, f32[64,128]{1,0:T(8,128)S(1)} %add.79.stats_ref), custom_call_target="tpu_custom_call" | custom-call | tf_op jit(solution)/shard_map/transform/pallas_call | solution.py:276
  124.9 3.6 %analysis.4 = bf16[64,32768]{1,0:T(8,128)(2,1)} custom-call(s32[1]{0:T(128)} %bitcast.base_ref.me_ref, bf16[80,64]{1,0:T(8,128)(2,1)S(1)} %get-tuple-element.11.mixer_ref, f32[64,128]{1,0:T(8,128)S(1)} %get-tuple-element.12.rest_ref, bf16[32,65536]{1,0:T(8,128)(2,1)S(1)} %copy-done.4, bf16[32,8192]{1,0:T(8,128)(2,1)S(1)} %collective-permute-done.4.refs_1_.refs_0_, ...), custom_call_target="tpu_custom_call" | custom-call | tf_op jit(solution)/shard_map/analysis/pallas_call | solution.py:342
  128.6 3.5 %analysis.5.refs_1_ = bf16[64,32768]{1,0:T(8,128)(2,1)} custom-call(s32[1]{0:T(128)} %bitcast.base_ref.me_ref, bf16[80,64]{1,0:T(8,128)(2,1)S(1)} %get-tuple-element.11.mixer_ref, f32[64,128]{1,0:T(8,128)S(1)} %get-tuple-element.12.rest_ref, bf16[32,65536]{1,0:T(8,128)(2,1)S(1)} %copy-done.2, bf16[32,4096]{1,0:T(8,128)(2,1)S(1)} %collective-permute-done.1.refs_1_.refs_0_, ...), custom_call_target="tpu_custom_call" | custom-call | tf_op jit(solution)/shard_map/analysis/pallas_call | solution.py:342
  132.0 1.5 %analysis.6.refs_1_ = bf16[64,32768]{1,0:T(8,128)(2,1)} custom-call(s32[1]{0:T(128)} %bitcast.base_ref.me_ref, bf16[80,64]{1,0:T(8,128)(2,1)S(1)} %get-tuple-element.11.mixer_ref, f32[64,128]{1,0:T(8,128)S(1)} %get-tuple-element.12.rest_ref, bf16[32,65536]{1,0:T(8,128)(2,1)S(1)} %copy-done.2, ...), custom_call_target="tpu_custom_call", output_to_operand_aliasing={{}: (5, {})} | custom-call | tf_op jit(solution)/shard_map/analysis/pallas_call | solution.py:342
  133.6 1.1 analysis.7
  (51 shorter events, 2.9 us)
Async XLA Ops:
  0.6 4.2 %copy-start.6 = (s32[2,256,16]{1,2,0:T(8,128)S(1)}, s32[2,256,16]{1,2,0:T(8,128)}, u32[]{:S(2)}) copy-start(s32[2,256,16]{1,2,0:T(8,128)} %param.8) | copy-start | bytes 98308
  0.6 4.3 %copy-start.8 = (s32[2,256]{1,0:T(2,128)S(1)}, s32[2,256]{1,0:T(2,128)}, u32[]{:S(2)}) copy-start(s32[2,256]{1,0:T(2,128)} %param.9) | copy-start | bytes 6148
  0.7 4.7 %copy-start.7 = (f32[2,256,16]{1,2,0:T(8,128)S(1)}, f32[2,256,16]{1,2,0:T(8,128)}, u32[]{:S(2)}) copy-start(f32[2,256,16]{1,2,0:T(8,128)} %param.11) | copy-start | bytes 98308
  0.7 5.3 %copy-start.5 = (f32[2,256,16]{1,2,0:T(8,128)S(1)}, f32[2,256,16]{1,2,0:T(8,128)}, u32[]{:S(2)}) copy-start(f32[2,256,16]{1,2,0:T(8,128)} %param.10) | copy-start | bytes 98308
  1.8 25.4 %collective-permute-start.4 = (bf16[32,8192]{1,0:T(8,128)(2,1)S(1)}, bf16[32,8192]{1,0:T(8,128)(2,1)S(1)}, u32[]{:S(2)}, u32[]{:S(2)}) collective-permute-start(bf16[32,8192]{1,0:T(8,128)(2,1)S(1)} %cut.1), channel_id=1, source_target_pairs={{0,16},{16,0},{1,17},{17,1},{2,18},{18,2},{3,19},{19,3},{4,20},{20... | collective-permute-start | bytes 1572872 | tf_op jit(solution)/shard_map/ppermute | solution.py:376
  4.8 12.6 %collective-permute-start = (s32[2,256,16]{1,2,0:T(8,128)S(1)}, s32[2,256,16]{1,2,0:T(8,128)S(1)}, u32[]{:S(2)}, u32[]{:S(2)}) collective-permute-start(s32[2,256,16]{1,2,0:T(8,128)S(1)} %copy-done.6), channel_id=1, source_target_pairs={{0,16},{16,0},{1,17},{17,1},{2,18},{18,2},{3,19},{19,3},{4,20},{20... | collective-permute-start | bytes 98312 | tf_op jit(solution)/shard_map/ppermute | solution.py:379
  6.3 2.2 %copy-start = (bf16[32,65536]{1,0:T(8,128)(2,1)S(1)}, bf16[32,65536]{1,0:T(8,128)(2,1)}, u32[]{:S(2)}) copy-start(bf16[32,65536]{1,0:T(8,128)(2,1)} %own_ref.7) | copy-start | bytes 12582916
  8.5 2.2 %copy-start.3 = (bf16[32,65536]{1,0:T(8,128)(2,1)S(1)}, bf16[32,65536]{1,0:T(8,128)(2,1)}, u32[]{:S(2)}) copy-start(bf16[32,65536]{1,0:T(8,128)(2,1)} %own_ref.4) | copy-start | bytes 12582916
  17.7 2.2 %copy-start.1 = (bf16[32,65536]{1,0:T(8,128)(2,1)S(1)}, bf16[32,65536]{1,0:T(8,128)(2,1)}, u32[]{:S(2)}) copy-start(bf16[32,65536]{1,0:T(8,128)(2,1)} %own_ref.7) | copy-start | bytes 12582916
  19.9 5.0 %copy-start.2 = (bf16[32,65536]{1,0:T(8,128)(2,1)S(1)}, bf16[32,65536]{1,0:T(8,128)(2,1)}, u32[]{:S(2)}) copy-start(bf16[32,65536]{1,0:T(8,128)(2,1)} %own_ref.7) | copy-start | bytes 12582916
  21.2 9.3 %collective-permute-start.3 = (bf16[1,32,3584]{2,1,0:T(8,128)(2,1)S(1)}, bf16[1,32,3584]{2,1,0:T(8,128)(2,1)S(1)}, u32[]{:S(2)}, u32[]{:S(2)}) collective-permute-start(bf16[1,32,3584]{2,1,0:T(8,128)(2,1)S(1)} %gather.3), channel_id=1, source_target_pairs={{0,16},{16,0},{1,17},{17,1},{2,18},{18,2},{3,19},{19,3},{4,20},{20... | collective-permute-start | bytes 688136 | tf_op jit(solution)/shard_map/ppermute | solution.py:376
  24.5 38.9 %collective-permute-start.2 = (bf16[32,24576]{1,0:T(8,128)(2,1)S(1)}, bf16[32,24576]{1,0:T(8,128)(2,1)S(1)}, u32[]{:S(2)}, u32[]{:S(2)}) collective-permute-start(bf16[32,24576]{1,0:T(8,128)(2,1)S(1)} %constant_dynamic-slice_fusion.4), channel_id=1, source_target_pairs={{0,16},{16,0},{1,17},{17,1},{2,18},{18,2},{3,19},{19,3},{4,20},{20... | collective-permute-start | bytes 4718600 | tf_op jit(solution)/shard_map/ppermute | solution.py:376
  24.9 44.2 %collective-permute-start.1 = (bf16[32,4096]{1,0:T(8,128)(2,1)S(1)}, bf16[32,4096]{1,0:T(8,128)(2,1)S(1)}, u32[]{:S(2)}, u32[]{:S(2)}) collective-permute-start(bf16[32,4096]{1,0:T(8,128)(2,1)S(1)} %constant_dynamic-slice_fusion.5), channel_id=1, source_target_pairs={{0,16},{16,0},{1,17},{17,1},{2,18},{18,2},{3,19},{19,3},{4,20},{20... | collective-permute-start | bytes 786440 | tf_op jit(solution)/shard_map/ppermute | solution.py:376
  26.8 98.1 %copy-start.4 = (bf16[32,65536]{1,0:T(8,128)(2,1)S(1)}, bf16[32,65536]{1,0:T(8,128)(2,1)}, u32[]{:S(2)}) copy-start(bf16[32,65536]{1,0:T(8,128)(2,1)} %own_ref.4) | copy-start | bytes 12582916
  26.8 101.8 %collective-permute-start.13 = (bf16[32,14336]{1,0:T(8,128)(2,1)S(1)}, bf16[32,14336]{1,0:T(8,128)(2,1)S(1)}, u32[]{:S(2)}, u32[]{:S(2)}) collective-permute-start(bf16[32,14336]{1,0:T(8,128)(2,1)S(1)} %constant_dynamic-slice_fusion), channel_id=1, source_target_pairs={{0,16},{16,0},{1,17},{17,1},{2,18},{18,2},{3,19},{19,3},{4,20},{20... | collective-permute-start | bytes 2752520 | tf_op jit(solution)/shard_map/ppermute | solution.py:376
  27.2 104.8 %collective-permute-start.11 = (bf16[32,8192]{1,0:T(8,128)(2,1)S(1)}, bf16[32,8192]{1,0:T(8,128)(2,1)S(1)}, u32[]{:S(2)}, u32[]{:S(2)}) collective-permute-start(bf16[32,8192]{1,0:T(8,128)(2,1)S(1)} %constant_dynamic-slice_fusion.2), channel_id=1, source_target_pairs={{0,16},{16,0},{1,17},{17,1},{2,18},{18,2},{3,19},{19,3},{4,20},{20... | collective-permute-start | bytes 1572872 | tf_op jit(solution)/shard_map/ppermute | solution.py:376
  69.8 30.9 %collective-permute-start.5 = (f32[64,128]{1,0:T(8,128)S(1)}, f32[64,128]{1,0:T(8,128)S(1)}, u32[]{:S(2)}, u32[]{:S(2)}) collective-permute-start(f32[64,128]{1,0:T(8,128)S(1)} %statistics.7), channel_id=1, source_target_pairs={{0,16},{16,0},{1,17},{17,1},{2,18},{18,2},{3,19},{19,3},{4,20},{20... | collective-permute-start | bytes 98312 | tf_op jit(solution)/shard_map/ppermute | solution.py:455
  71.6 62.0 %collective-permute-start.10 = (bf16[32,4096]{1,0:T(8,128)(2,1)S(1)}, bf16[32,4096]{1,0:T(8,128)(2,1)S(1)}, u32[]{:S(2)}, u32[]{:S(2)}) collective-permute-start(bf16[32,4096]{1,0:T(8,128)(2,1)S(1)} %constant_dynamic-slice_fusion.3), channel_id=1, source_target_pairs={{0,16},{16,0},{1,17},{17,1},{2,18},{18,2},{3,19},{19,3},{4,20},{20... | collective-permute-start | bytes 786440 | tf_op jit(solution)/shard_map/ppermute | solution.py:376
  100.7 1.8 %collective-permute-start.6 = (f32[64,128]{1,0:T(8,128)S(1)}, f32[64,128]{1,0:T(8,128)S(1)}, u32[]{:S(2)}, u32[]{:S(2)}) collective-permute-start(f32[64,128]{1,0:T(8,128)S(1)} %add.75), channel_id=1, source_target_pairs={{0,1},{1,0},{2,3},{3,2},{4,5},{5,4},{6,7},{7,6},{8,9},{9,8},{10,11... | collective-permute-start | bytes 98312 | tf_op jit(solution)/shard_map/ppermute | solution.py:455
  100.7 27.8 %collective-permute-start.12 = (bf16[32,2048]{1,0:T(8,128)(2,1)S(1)}, bf16[32,2048]{1,0:T(8,128)(2,1)S(1)}, u32[]{:S(2)}, u32[]{:S(2)}) collective-permute-start(bf16[32,2048]{1,0:T(8,128)(2,1)S(1)} %constant_dynamic-slice_fusion.1), channel_id=1, source_target_pairs={{0,16},{16,0},{1,17},{17,1},{2,18},{18,2},{3,19},{19,3},{4,20},{20... | collective-permute-start | bytes 393224 | tf_op jit(solution)/shard_map/ppermute | solution.py:376
  102.5 4.0 %collective-permute-start.7 = (f32[64,128]{1,0:T(8,128)S(1)}, f32[64,128]{1,0:T(8,128)S(1)}, u32[]{:S(2)}, u32[]{:S(2)}) collective-permute-start(f32[64,128]{1,0:T(8,128)S(1)} %add.76), channel_id=1, source_target_pairs={{0,2},{1,3},{2,0},{3,1},{4,6},{5,7},{6,4},{7,5},{8,10},{9,11},{10,... | collective-permute-start | bytes 98312 | tf_op jit(solution)/shard_map/ppermute | solution.py:455
  106.5 3.9 %collective-permute-start.8 = (f32[64,128]{1,0:T(8,128)S(1)}, f32[64,128]{1,0:T(8,128)S(1)}, u32[]{:S(2)}, u32[]{:S(2)}) collective-permute-start(f32[64,128]{1,0:T(8,128)S(1)} %add.77), channel_id=1, source_target_pairs={{0,4},{1,5},{2,6},{3,7},{4,0},{5,1},{6,2},{7,3},{8,12},{9,13},{10,... | collective-permute-start | bytes 98312 | tf_op jit(solution)/shard_map/ppermute | solution.py:455
  110.4 4.8 %collective-permute-start.9 = (f32[64,128]{1,0:T(8,128)S(1)}, f32[64,128]{1,0:T(8,128)S(1)}, u32[]{:S(2)}, u32[]{:S(2)}) collective-permute-start(f32[64,128]{1,0:T(8,128)S(1)} %add.78), channel_id=1, source_target_pairs={{0,8},{1,9},{2,10},{3,11},{4,12},{5,13},{6,14},{7,15},{8,0},{9,1},... | collective-permute-start | bytes 98312 | tf_op jit(solution)/shard_map/ppermute | solution.py:455

commit v8 on v7

--- a/solution.py
+++ b/solution.py
@@ -20,8 +20,8 @@
     (1, 0, 4),
     (1, 4, 6),
     (1, 6, 20),
-    (1, 20, 28),
-    (1, 28, 32),
+    (1, 20, 30),
+    (1, 30, 32),
 )
 READ = (0, 1, 2)
 SENT = (1, 1)
@@ -50,7 +50,7 @@
     out_ref[...] = state_ref[...]
 
 
-def cut_first(state, base, lo, hi, piece):
+def cut_out(state, base, lo, hi, piece, vmem):
     members, length = state.shape[0], hi - lo
     whole = piece // length
     return pl.pallas_call(
@@ -64,7 +64,7 @@
             ],
             out_specs=pl.BlockSpec(memory_space=pltpu.VMEM),
         ),
-        compiler_params=pltpu.CompilerParams(vmem_limit_bytes=MOST_VMEM),
+        compiler_params=pltpu.CompilerParams(vmem_limit_bytes=vmem),
         name="cut",
     )(base, state)
 
@@ -396,7 +396,14 @@
 
     group, lo, hi = MESSAGES[0]
     first_pieces = [
-        cut_first(states[group], lax.rem(me_ref + nmem - shift, nmem), lo * unit, hi * unit, piece)
+        cut_out(
+            states[group],
+            lax.rem(me_ref + nmem - shift, nmem),
+            lo * unit,
+            hi * unit,
+            piece,
+            MOST_VMEM,
+        )
         for shift in shifts
     ]
     own_hx = gather(states, (0, 1), index, me_ref, slots, piece)
@@ -447,7 +454,12 @@
     for i in READ[1:]:
         stats = read(i, stats)
 
-    pieces = cut(MESSAGES[-1], lax.optimization_barrier((*states, stats)))
+    group, lo, hi = MESSAGES[-1]
+    source = lax.optimization_barrier((states[group], stats))[0]
+    pieces = [
+        cut_out(source, lax.rem(me_ref + nmem - shift, nmem), lo * unit, hi * unit, piece, VMEM)
+        for shift in shifts
+    ]
     send(len(MESSAGES) - 1, pieces)
 
     def all_sum(x, axis, size):

time: 135 us -> 138 us (1.022)
  local copies, waits for them, and re-layouts: 9.67 us -> 22.9 us
  waiting for transfers between devices: 70.8 us -> 58.6 us
  Pallas kernels: 34.2 us -> 37.6 us
    ppermute x8, waiting for transfers between devices: 30.7 us -> 18.9 us  [to_lower(): lax.ppermute(array, 'mem', [(i, (i - shift) % nmem) for i in range(nmem)])]
    dynamic_slice x6 -> x5, local copies, waits for them, and re-layouts: 1.66 us -> 9.4 us  [cut(): lax.dynamic_slice(source[group], (0, lax.rem(me + nmem - shift, nmem) * p...]
    ppermute x1, waiting for transfers between devices: 4.41 us -> 0.49 us  [to_upper(): lax.ppermute(array, 'mem', [(i, (i + shift) % nmem) for i in range(nmem)])]
    ppermute x5, waiting for transfers between devices: 35.7 us -> 39.2 us  [all_sum(): x = x + lax.ppermute(x, axis, [(j, j ^ 1 << i) for j in range(size)])]
    pallas_call x4, Pallas kernels: 9.76 us -> 13.2 us  [analyse(): pl.pallas_call(functools.partial(analysis_kernel, bounds, len(received) /...]
    ppermute x1, starting transfers between devices: 0.09 us -> 3.03 us  [to_upper(): lax.ppermute(array, 'mem', [(i, (i + shift) % nmem) for i in range(nmem)])]
    unnamed x20 -> x22, local copies, waits for them, and re-layouts: 6.82 us -> 9.73 us
    ppermute x8, starting transfers between devices: 11.3 us -> 8.73 us  [to_lower(): lax.ppermute(array, 'mem', [(i, (i - shift) % nmem) for i in range(nmem)])]
  transfers between devices with their start and end apart: 14 -> 14, of which waited for: 7 -> 7; matrix products, arithmetic and copies ran while one was open for 2% -> 10% of each run, Pallas kernels for 24% -> 27%
where the time goes in v8:
time: 138 us
  waiting for transfers between devices  58.6 us (42%)
  Pallas kernels  37.6 us (27%)
  local copies, waits for them, and re-layouts  22.9 us (17%)
  starting transfers between devices  17.6 us (13%)
    ppermute x5, waiting for transfers between devices, all_sum(): x = x + lax.ppermute(x, axis, [(j, j ^ 1 << i) for j in range(size)])  39.2 us
    ppermute x8, waiting for transfers between devices, to_lower(): lax.ppermute(array, 'mem', [(i, (i - shift) % nmem) for i in range(nmem)])  18.9 us
    pallas_call x4, Pallas kernels, analyse(): pl.pallas_call(functools.partial(analysis_kernel, bounds, len(received) /...  13.2 us
    pallas_call x4, Pallas kernels, statistics(): pl.pallas_call(functools.partial(statistics_kernel, parts, slots, group,...  10.1 us
    unnamed x22, local copies, waits for them, and re-layouts  9.73 us
    pallas_call x1, Pallas kernels, make_transform(): pl.pallas_call(functools.partial(transform_kernel, members), out_shape=(j...  9.65 us
    dynamic_slice x5, local copies, waits for them, and re-layouts, cut(): lax.dynamic_slice(source[group], (0, lax.rem(me + nmem - shift, nmem) * p...  9.4 us
    ppermute x8, starting transfers between devices, to_lower(): lax.ppermute(array, 'mem', [(i, (i - shift) % nmem) for i in range(nmem)])  8.73 us
  transfers between devices with their start and end apart: 14, of which 7 were waited for; matrix products, arithmetic and copies ran while one was open for 10% of the time, Pallas kernels for 27%

profile of v8, /device:TPU:0, one launch (start us, length us, event | category | flops | bytes accessed | tf_op | source)
XLA Modules:
  0.0 137.7 jit_solution(1132183635779938370)
XLA Ops:
  0.6 3.0 %collective-permute-start = (s32[2,256,16]{1,2,0:T(8,128)}, s32[2,256,16]{1,2,0:T(8,128)S(1)}, u32[]{:S(2)}, u32[]{:S(2)}) collective-permute-start(s32[2,256,16]{1,2,0:T(8,128)} %param.8), channel_id=1, source_target_pairs={{0,16},{16,0},{1,17},{17,1},{2,18},{18,2},{3,19},{19,3},{4,20},{20... | collective-permute-start | bytes 98312 | tf_op jit(solution)/shard_map/ppermute | solution.py:379
  6.1 2.2 %copy-done = bf16[32,65536]{1,0:T(8,128)(2,1)S(1)} copy-done((bf16[32,65536]{1,0:T(8,128)(2,1)S(1)}, bf16[32,65536]{1,0:T(8,128)(2,1)}, u32[]{:S(2)}) %copy-start) | copy-done | bytes 4194328
  8.2 1.3 gather.3
  9.6 2.4 %collective-permute-start.3 = (bf16[1,32,3584]{2,1,0:T(8,128)(2,1)S(1)}, bf16[1,32,3584]{2,1,0:T(8,128)(2,1)S(1)}, u32[]{:S(2)}, u32[]{:S(2)}) collective-permute-start(bf16[1,32,3584]{2,1,0:T(8,128)(2,1)S(1)} %gather.3), channel_id=1, source_target_pairs={{0,16},{16,0},{1,17},{17,1},{2,18},{18,2},{3,19},{19,3},{4,20},{20... | collective-permute-start | bytes 688136 | tf_op jit(solution)/shard_map/ppermute | solution.py:376
  12.0 2.7 %constant_dynamic-slice_fusion.3 = bf16[32,24576]{1,0:T(8,128)(2,1)} fusion(bf16[32,65536]{1,0:T(8,128)(2,1)} %own_ref.4, s32[]{:T(128)S(6)} %select_n.16), kind=kLoop, calls=%fused_computation.6 | loop fusion | bytes 3145732 | tf_op jit(solution)/shard_map/dynamic_slice | solution.py:384
  14.7 1.7 %constant_dynamic-slice_fusion.4 = bf16[32,4096]{1,0:T(8,128)(2,1)} fusion(bf16[32,65536]{1,0:T(8,128)(2,1)} %own_ref.7, s32[]{:T(128)S(6)} %select_n.15), kind=kLoop, calls=%fused_computation.7 | loop fusion | bytes 524292 | tf_op jit(solution)/shard_map/dynamic_slice | solution.py:384
  16.3 2.0 %collective-permute-start.1 = (bf16[32,4096]{1,0:T(8,128)(2,1)}, bf16[32,4096]{1,0:T(8,128)(2,1)S(1)}, u32[]{:S(2)}, u32[]{:S(2)}) collective-permute-start(bf16[32,4096]{1,0:T(8,128)(2,1)} %constant_dynamic-slice_fusion.4), channel_id=1, source_target_pairs={{0,16},{16,0},{1,17},{17,1},{2,18},{18,2},{3,19},{19,3},{4,20},{20... | collective-permute-start | bytes 786440 | tf_op jit(solution)/shard_map/ppermute | solution.py:376
  18.3 2.2 %constant_dynamic-slice_fusion = bf16[32,14336]{1,0:T(8,128)(2,1)} fusion(bf16[32,65536]{1,0:T(8,128)(2,1)} %own_ref.7, s32[]{:T(128)S(6)} %select_n.19), kind=kLoop, calls=%fused_computation.3 | loop fusion | bytes 1835012 | tf_op jit(solution)/shard_map/dynamic_slice | solution.py:384
  20.5 2.0 %constant_dynamic-slice_fusion.2 = bf16[32,10240]{1,0:T(8,128)(2,1)} fusion(bf16[32,65536]{1,0:T(8,128)(2,1)} %own_ref.7, s32[]{:T(128)S(6)} %select_n.17), kind=kLoop, calls=%fused_computation.5 | loop fusion | bytes 1310724 | tf_op jit(solution)/shard_map/dynamic_slice | solution.py:384
  22.5 2.0 %collective-permute-start.11 = (bf16[32,10240]{1,0:T(8,128)(2,1)}, bf16[32,10240]{1,0:T(8,128)(2,1)}, u32[]{:S(2)}, u32[]{:S(2)}) collective-permute-start(bf16[32,10240]{1,0:T(8,128)(2,1)} %constant_dynamic-slice_fusion.2), channel_id=1, source_target_pairs={{0,16},{16,0},{1,17},{17,1},{2,18},{18,2},{3,19},{19,3},{4,20},{20... | collective-permute-start | bytes 1966088 | tf_op jit(solution)/shard_map/ppermute | solution.py:376
  24.9 2.2 %copy-done.1 = bf16[32,65536]{1,0:T(8,128)(2,1)S(1)} copy-done((bf16[32,65536]{1,0:T(8,128)(2,1)S(1)}, bf16[32,65536]{1,0:T(8,128)(2,1)}, u32[]{:S(2)}) %copy-start.1) | copy-done | bytes 4194328
  27.1 2.2 %copy-done.4 = bf16[32,65536]{1,0:T(8,128)(2,1)S(1)} copy-done((bf16[32,65536]{1,0:T(8,128)(2,1)S(1)}, bf16[32,65536]{1,0:T(8,128)(2,1)}, u32[]{:S(2)}) %copy-start.4) | copy-done | bytes 4194328
  29.3 2.3 %gather.2.refs_0_ = bf16[2,32,4096]{2,1,0:T(8,128)(2,1)S(1)} custom-call(s32[1]{0:T(128)} %bitcast.base_ref.me_ref, s32[2,32,128]{2,1,0:T(8,128)S(1)} %reshape.59.index_ref.refs_5_, bf16[32,65536]{1,0:T(8,128)(2,1)S(1)} %copy-done.4, bf16[32,65536]{1,0:T(8,128)(2,1)S(1)} %copy-done.1), custom_call_target="tpu_custom_call" | custom-call | tf_op jit(solution)/shard_map/gather/pallas_call | solution.py:103
  32.5 1.1 reshape.64.refs_3_
  35.5 1.5 %statistics.4.refs_5_ = f32[64,128]{1,0:T(8,128)S(1)} custom-call(s32[1]{0:T(128)} %bitcast.base_ref.me_ref, bf16[2,32,4096]{2,1,0:T(8,128)(2,1)S(1)} %gather.2.refs_0_, bf16[32,8192]{1,0:T(8,128)(2,1)S(1)} %collective-permute-done.4.refs_1_.refs_0_, f32[2,1,4096]{2,1,0:T(1,128)S(1)} %reshape.63.refs_2_, f32[2,1,4096]{2,1,0:T(1,128)S(1)} %reshape.64.refs_3_, ...), custom_call_target="tpu_custom_call" | custom-call | tf_op jit(solution)/shard_map/statistics/pallas_call | solution.py:211
  37.0 3.5 %statistics.5.refs_6_ = f32[64,128]{1,0:T(8,128)S(1)} custom-call(s32[1]{0:T(128)} %bitcast.base_ref.me_ref, bf16[2,32,4096]{2,1,0:T(8,128)(2,1)S(1)} %gather.2.refs_0_, bf16[1,32,3584]{2,1,0:T(8,128)(2,1)S(1)} %collective-permute-done.3.refs_1_, f32[2,1,4096]{2,1,0:T(1,128)S(1)} %reshape.63.refs_2_, f32[2,1,4096]{2,1,0:T(1,128)S(1)} %reshape.64.refs_3_, ...), custom_call_target="tpu_custom_call" | custom-call | tf_op jit(solution)/shard_map/statistics/pallas_call | solution.py:211
  40.5 17.8 %collective-permute-done.2.refs_1_ = bf16[32,24576]{1,0:T(8,128)(2,1)S(1)} collective-permute-done((bf16[32,24576]{1,0:T(8,128)(2,1)}, bf16[32,24576]{1,0:T(8,128)(2,1)S(1)}, u32[]{:S(2)}, u32[]{:S(2)}) %collective-permute-start.2) | collective-permute-done | bytes 1572896 | tf_op jit(solution)/shard_map/ppermute | solution.py:376
  58.2 4.4 %statistics.6.refs_6_ = f32[64,128]{1,0:T(8,128)S(1)} custom-call(s32[1]{0:T(128)} %bitcast.base_ref.me_ref, bf16[2,32,4096]{2,1,0:T(8,128)(2,1)S(1)} %gather.2.refs_0_, bf16[32,24576]{1,0:T(8,128)(2,1)S(1)} %collective-permute-done.2.refs_1_, f32[2,1,4096]{2,1,0:T(1,128)S(1)} %reshape.63.refs_2_, f32[2,1,4096]{2,1,0:T(1,128)S(1)} %reshape.64.refs_3_, ...), custom_call_target="tpu_custom_call" | custom-call | tf_op jit(solution)/shard_map/statistics/pallas_call | solution.py:211
  62.7 1.2 collective-permute-done.1.refs_1_.refs_0_
  64.6 32.2 %collective-permute-done.5 = f32[64,128]{1,0:T(8,128)S(1)} collective-permute-done((f32[64,128]{1,0:T(8,128)S(1)}, f32[64,128]{1,0:T(8,128)S(1)}, u32[]{:S(2)}, u32[]{:S(2)}) %collective-permute-start.5) | collective-permute-done | bytes 32800 | tf_op jit(solution)/shard_map/ppermute | solution.py:467
  98.5 2.2 %copy-done.2 = bf16[32,65536]{1,0:T(8,128)(2,1)S(1)} copy-done((bf16[32,65536]{1,0:T(8,128)(2,1)S(1)}, bf16[32,65536]{1,0:T(8,128)(2,1)}, u32[]{:S(2)}) %copy-start.2) | copy-done | bytes 4194328
  100.7 1.4 %collective-permute-start.10 = (bf16[32,2048]{1,0:T(8,128)(2,1)S(1)}, bf16[32,2048]{1,0:T(8,128)(2,1)S(1)}, u32[]{:S(2)}, u32[]{:S(2)}) collective-permute-start(bf16[32,2048]{1,0:T(8,128)(2,1)S(1)} %cut.3), channel_id=1, source_target_pairs={{0,16},{16,0},{1,17},{17,1},{2,18},{18,2},{3,19},{19,3},{4,20},{20... | collective-permute-start | bytes 393224 | tf_op jit(solution)/shard_map/ppermute | solution.py:376
  102.2 1.6 %collective-permute-start.7 = (f32[64,128]{1,0:T(8,128)S(1)}, f32[64,128]{1,0:T(8,128)S(1)}, u32[]{:S(2)}, u32[]{:S(2)}) collective-permute-start(f32[64,128]{1,0:T(8,128)S(1)} %add.68), channel_id=1, source_target_pairs={{0,2},{1,3},{2,0},{3,1},{4,6},{5,7},{6,4},{7,5},{8,10},{9,11},{10,... | collective-permute-start | bytes 98312 | tf_op jit(solution)/shard_map/ppermute | solution.py:467
  103.7 2.4 %collective-permute-done.7 = f32[64,128]{1,0:T(8,128)S(1)} collective-permute-done((f32[64,128]{1,0:T(8,128)S(1)}, f32[64,128]{1,0:T(8,128)S(1)}, u32[]{:S(2)}, u32[]{:S(2)}) %collective-permute-start.7) | collective-permute-done | bytes 32800 | tf_op jit(solution)/shard_map/ppermute | solution.py:467
  106.1 1.6 %collective-permute-start.8 = (f32[64,128]{1,0:T(8,128)S(1)}, f32[64,128]{1,0:T(8,128)S(1)}, u32[]{:S(2)}, u32[]{:S(2)}) collective-permute-start(f32[64,128]{1,0:T(8,128)S(1)} %add.69), channel_id=1, source_target_pairs={{0,4},{1,5},{2,6},{3,7},{4,0},{5,1},{6,2},{7,3},{8,12},{9,13},{10,... | collective-permute-start | bytes 98312 | tf_op jit(solution)/shard_map/ppermute | solution.py:467
  107.7 2.3 %collective-permute-done.8 = f32[64,128]{1,0:T(8,128)S(1)} collective-permute-done((f32[64,128]{1,0:T(8,128)S(1)}, f32[64,128]{1,0:T(8,128)S(1)}, u32[]{:S(2)}, u32[]{:S(2)}) %collective-permute-start.8) | collective-permute-done | bytes 32800 | tf_op jit(solution)/shard_map/ppermute | solution.py:467
  110.1 2.6 %collective-permute-start.9 = (f32[64,128]{1,0:T(8,128)S(1)}, f32[64,128]{1,0:T(8,128)S(1)}, u32[]{:S(2)}, u32[]{:S(2)}) collective-permute-start(f32[64,128]{1,0:T(8,128)S(1)} %add.70), channel_id=1, source_target_pairs={{0,8},{1,9},{2,10},{3,11},{4,12},{5,13},{6,14},{7,15},{8,0},{9,1},... | collective-permute-start | bytes 98312 | tf_op jit(solution)/shard_map/ppermute | solution.py:467
  112.7 2.2 %collective-permute-done.9 = f32[64,128]{1,0:T(8,128)S(1)} collective-permute-done((f32[64,128]{1,0:T(8,128)S(1)}, f32[64,128]{1,0:T(8,128)S(1)}, u32[]{:S(2)}, u32[]{:S(2)}) %collective-permute-start.9) | collective-permute-done | bytes 32800 | tf_op jit(solution)/shard_map/ppermute | solution.py:467
  114.9 9.7 %transform.1 = (f32[64,64]{1,0:T(8,128)}, bf16[80,64]{1,0:T(8,128)(2,1)S(1)}, f32[64,128]{1,0:T(8,128)S(1)}) custom-call(s32[1]{0:T(128)} %bitcast.base_ref.me_ref, f32[64,128]{1,0:T(8,128)S(1)} %add.71.stats_ref), custom_call_target="tpu_custom_call" | custom-call | tf_op jit(solution)/shard_map/transform/pallas_call | solution.py:276
  124.5 3.6 %analysis.4 = bf16[64,32768]{1,0:T(8,128)(2,1)} custom-call(s32[1]{0:T(128)} %bitcast.base_ref.me_ref, bf16[80,64]{1,0:T(8,128)(2,1)S(1)} %get-tuple-element.11.mixer_ref, f32[64,128]{1,0:T(8,128)S(1)} %get-tuple-element.12.rest_ref, bf16[32,65536]{1,0:T(8,128)(2,1)S(1)} %copy-done.5, bf16[32,8192]{1,0:T(8,128)(2,1)S(1)} %collective-permute-done.4.refs_1_.refs_0_, ...), custom_call_target="tpu_custom_call" | custom-call | tf_op jit(solution)/shard_map/analysis/pallas_call | solution.py:342
  128.2 4.7 %analysis.5.refs_1_ = bf16[64,32768]{1,0:T(8,128)(2,1)} custom-call(s32[1]{0:T(128)} %bitcast.base_ref.me_ref, bf16[80,64]{1,0:T(8,128)(2,1)S(1)} %get-tuple-element.11.mixer_ref, f32[64,128]{1,0:T(8,128)S(1)} %get-tuple-element.12.rest_ref, bf16[32,65536]{1,0:T(8,128)(2,1)S(1)} %copy-done.3, bf16[32,4096]{1,0:T(8,128)(2,1)S(1)} %collective-permute-done.1.refs_1_.refs_0_, ...), custom_call_target="tpu_custom_call" | custom-call | tf_op jit(solution)/shard_map/analysis/pallas_call | solution.py:342
  132.8 4.0 %analysis.6.refs_1_ = bf16[64,32768]{1,0:T(8,128)(2,1)} custom-call(s32[1]{0:T(128)} %bitcast.base_ref.me_ref, bf16[80,64]{1,0:T(8,128)(2,1)S(1)} %get-tuple-element.11.mixer_ref, f32[64,128]{1,0:T(8,128)S(1)} %get-tuple-element.12.rest_ref, bf16[32,65536]{1,0:T(8,128)(2,1)S(1)} %copy-done.3, ...), custom_call_target="tpu_custom_call", output_to_operand_aliasing={{}: (5, {})} | custom-call | tf_op jit(solution)/shard_map/analysis/pallas_call | solution.py:342
  (53 shorter events, 8.9 us)
Async XLA Ops:
  0.6 4.2 %copy-start.9 = (s32[2,256]{1,0:T(2,128)S(1)}, s32[2,256]{1,0:T(2,128)}, u32[]{:S(2)}) copy-start(s32[2,256]{1,0:T(2,128)} %param.9) | copy-start | bytes 6148
  0.6 5.1 %collective-permute-start = (s32[2,256,16]{1,2,0:T(8,128)}, s32[2,256,16]{1,2,0:T(8,128)S(1)}, u32[]{:S(2)}, u32[]{:S(2)}) collective-permute-start(s32[2,256,16]{1,2,0:T(8,128)} %param.8), channel_id=1, source_target_pairs={{0,16},{16,0},{1,17},{17,1},{2,18},{18,2},{3,19},{19,3},{4,20},{20... | collective-permute-start | bytes 98312 | tf_op jit(solution)/shard_map/ppermute | solution.py:379
  4.8 17.8 %collective-permute-start.4 = (bf16[32,8192]{1,0:T(8,128)(2,1)S(1)}, bf16[32,8192]{1,0:T(8,128)(2,1)S(1)}, u32[]{:S(2)}, u32[]{:S(2)}) collective-permute-start(bf16[32,8192]{1,0:T(8,128)(2,1)S(1)} %cut.2), channel_id=1, source_target_pairs={{0,16},{16,0},{1,17},{17,1},{2,18},{18,2},{3,19},{19,3},{4,20},{20... | collective-permute-start | bytes 1572872 | tf_op jit(solution)/shard_map/ppermute | solution.py:376
  6.0 2.2 %copy-start = (bf16[32,65536]{1,0:T(8,128)(2,1)S(1)}, bf16[32,65536]{1,0:T(8,128)(2,1)}, u32[]{:S(2)}) copy-start(bf16[32,65536]{1,0:T(8,128)(2,1)} %own_ref.7) | copy-start | bytes 12582916
  9.6 15.0 %copy-start.6 = (s32[2,256,16]{1,2,0:T(8,128)S(1)}, s32[2,256,16]{1,2,0:T(8,128)}, u32[]{:S(2)}) copy-start(s32[2,256,16]{1,2,0:T(8,128)} %param.8) | copy-start | bytes 98308
  9.6 27.4 %collective-permute-start.3 = (bf16[1,32,3584]{2,1,0:T(8,128)(2,1)S(1)}, bf16[1,32,3584]{2,1,0:T(8,128)(2,1)S(1)}, u32[]{:S(2)}, u32[]{:S(2)}) collective-permute-start(bf16[1,32,3584]{2,1,0:T(8,128)(2,1)S(1)} %gather.3), channel_id=1, source_target_pairs={{0,16},{16,0},{1,17},{17,1},{2,18},{18,2},{3,19},{19,3},{4,20},{20... | collective-permute-start | bytes 688136 | tf_op jit(solution)/shard_map/ppermute | solution.py:376
  14.7 43.6 %collective-permute-start.2 = (bf16[32,24576]{1,0:T(8,128)(2,1)}, bf16[32,24576]{1,0:T(8,128)(2,1)S(1)}, u32[]{:S(2)}, u32[]{:S(2)}) collective-permute-start(bf16[32,24576]{1,0:T(8,128)(2,1)} %constant_dynamic-slice_fusion.3), channel_id=1, source_target_pairs={{0,16},{16,0},{1,17},{17,1},{2,18},{18,2},{3,19},{19,3},{4,20},{20... | collective-permute-start | bytes 4718600 | tf_op jit(solution)/shard_map/ppermute | solution.py:376
  16.3 47.5 %collective-permute-start.1 = (bf16[32,4096]{1,0:T(8,128)(2,1)}, bf16[32,4096]{1,0:T(8,128)(2,1)S(1)}, u32[]{:S(2)}, u32[]{:S(2)}) collective-permute-start(bf16[32,4096]{1,0:T(8,128)(2,1)} %constant_dynamic-slice_fusion.4), channel_id=1, source_target_pairs={{0,16},{16,0},{1,17},{17,1},{2,18},{18,2},{3,19},{19,3},{4,20},{20... | collective-permute-start | bytes 786440 | tf_op jit(solution)/shard_map/ppermute | solution.py:376
  20.5 107.7 %collective-permute-start.13 = (bf16[32,14336]{1,0:T(8,128)(2,1)}, bf16[32,14336]{1,0:T(8,128)(2,1)}, u32[]{:S(2)}, u32[]{:S(2)}) collective-permute-start(bf16[32,14336]{1,0:T(8,128)(2,1)} %constant_dynamic-slice_fusion), channel_id=1, source_target_pairs={{0,16},{16,0},{1,17},{17,1},{2,18},{18,2},{3,19},{19,3},{4,20},{20... | collective-permute-start | bytes 2752520 | tf_op jit(solution)/shard_map/ppermute | solution.py:376
  22.5 110.3 %collective-permute-start.11 = (bf16[32,10240]{1,0:T(8,128)(2,1)}, bf16[32,10240]{1,0:T(8,128)(2,1)}, u32[]{:S(2)}, u32[]{:S(2)}) collective-permute-start(bf16[32,10240]{1,0:T(8,128)(2,1)} %constant_dynamic-slice_fusion.2), channel_id=1, source_target_pairs={{0,16},{16,0},{1,17},{17,1},{2,18},{18,2},{3,19},{19,3},{4,20},{20... | collective-permute-start | bytes 1966088 | tf_op jit(solution)/shard_map/ppermute | solution.py:376
  24.9 2.2 %copy-start.1 = (bf16[32,65536]{1,0:T(8,128)(2,1)S(1)}, bf16[32,65536]{1,0:T(8,128)(2,1)}, u32[]{:S(2)}) copy-start(bf16[32,65536]{1,0:T(8,128)(2,1)} %own_ref.7) | copy-start | bytes 12582916
  27.1 2.2 %copy-start.4 = (bf16[32,65536]{1,0:T(8,128)(2,1)S(1)}, bf16[32,65536]{1,0:T(8,128)(2,1)}, u32[]{:S(2)}) copy-start(bf16[32,65536]{1,0:T(8,128)(2,1)} %own_ref.4) | copy-start | bytes 12582916
  29.2 2.3 %copy-start.8 = (f32[2,256,16]{1,2,0:T(8,128)S(1)}, f32[2,256,16]{1,2,0:T(8,128)}, u32[]{:S(2)}) copy-start(f32[2,256,16]{1,2,0:T(8,128)} %param.11) | copy-start | bytes 98308
  29.2 4.3 %copy-start.7 = (f32[2,256,16]{1,2,0:T(8,128)S(1)}, f32[2,256,16]{1,2,0:T(8,128)}, u32[]{:S(2)}) copy-start(f32[2,256,16]{1,2,0:T(8,128)} %param.10) | copy-start | bytes 98308
  64.6 32.3 %collective-permute-start.5 = (f32[64,128]{1,0:T(8,128)S(1)}, f32[64,128]{1,0:T(8,128)S(1)}, u32[]{:S(2)}, u32[]{:S(2)}) collective-permute-start(f32[64,128]{1,0:T(8,128)S(1)} %statistics.7), channel_id=1, source_target_pairs={{0,16},{16,0},{1,17},{17,1},{2,18},{18,2},{3,19},{19,3},{4,20},{20... | collective-permute-start | bytes 98312 | tf_op jit(solution)/shard_map/ppermute | solution.py:467
  96.9 5.3 %collective-permute-start.6 = (f32[64,128]{1,0:T(8,128)S(1)}, f32[64,128]{1,0:T(8,128)S(1)}, u32[]{:S(2)}, u32[]{:S(2)}) collective-permute-start(f32[64,128]{1,0:T(8,128)S(1)} %add.67), channel_id=1, source_target_pairs={{0,1},{1,0},{2,3},{3,2},{4,5},{5,4},{6,7},{7,6},{8,9},{9,8},{10,11... | collective-permute-start | bytes 98312 | tf_op jit(solution)/shard_map/ppermute | solution.py:467
  97.8 30.4 %collective-permute-start.12 = (bf16[32,2048]{1,0:T(8,128)(2,1)S(1)}, bf16[32,2048]{1,0:T(8,128)(2,1)S(1)}, u32[]{:S(2)}, u32[]{:S(2)}) collective-permute-start(bf16[32,2048]{1,0:T(8,128)(2,1)S(1)} %constant_dynamic-slice_fusion.1), channel_id=1, source_target_pairs={{0,16},{16,0},{1,17},{17,1},{2,18},{18,2},{3,19},{19,3},{4,20},{20... | collective-permute-start | bytes 393224 | tf_op jit(solution)/shard_map/ppermute | solution.py:376
  98.5 2.2 %copy-start.2 = (bf16[32,65536]{1,0:T(8,128)(2,1)S(1)}, bf16[32,65536]{1,0:T(8,128)(2,1)}, u32[]{:S(2)}) copy-start(bf16[32,65536]{1,0:T(8,128)(2,1)} %own_ref.7) | copy-start | bytes 12582916
  100.7 23.8 %copy-start.5 = (bf16[32,65536]{1,0:T(8,128)(2,1)S(1)}, bf16[32,65536]{1,0:T(8,128)(2,1)}, u32[]{:S(2)}) copy-start(bf16[32,65536]{1,0:T(8,128)(2,1)} %own_ref.4) | copy-start | bytes 12582916
  100.7 36.1 %collective-permute-start.10 = (bf16[32,2048]{1,0:T(8,128)(2,1)S(1)}, bf16[32,2048]{1,0:T(8,128)(2,1)S(1)}, u32[]{:S(2)}, u32[]{:S(2)}) collective-permute-start(bf16[32,2048]{1,0:T(8,128)(2,1)S(1)} %cut.3), channel_id=1, source_target_pairs={{0,16},{16,0},{1,17},{17,1},{2,18},{18,2},{3,19},{19,3},{4,20},{20... | collective-permute-start | bytes 393224 | tf_op jit(solution)/shard_map/ppermute | solution.py:376
  102.2 4.0 %collective-permute-start.7 = (f32[64,128]{1,0:T(8,128)S(1)}, f32[64,128]{1,0:T(8,128)S(1)}, u32[]{:S(2)}, u32[]{:S(2)}) collective-permute-start(f32[64,128]{1,0:T(8,128)S(1)} %add.68), channel_id=1, source_target_pairs={{0,2},{1,3},{2,0},{3,1},{4,6},{5,7},{6,4},{7,5},{8,10},{9,11},{10,... | collective-permute-start | bytes 98312 | tf_op jit(solution)/shard_map/ppermute | solution.py:467
  106.1 3.9 %collective-permute-start.8 = (f32[64,128]{1,0:T(8,128)S(1)}, f32[64,128]{1,0:T(8,128)S(1)}, u32[]{:S(2)}, u32[]{:S(2)}) collective-permute-start(f32[64,128]{1,0:T(8,128)S(1)} %add.69), channel_id=1, source_target_pairs={{0,4},{1,5},{2,6},{3,7},{4,0},{5,1},{6,2},{7,3},{8,12},{9,13},{10,... | collective-permute-start | bytes 98312 | tf_op jit(solution)/shard_map/ppermute | solution.py:467
  110.1 4.8 %collective-permute-start.9 = (f32[64,128]{1,0:T(8,128)S(1)}, f32[64,128]{1,0:T(8,128)S(1)}, u32[]{:S(2)}, u32[]{:S(2)}) collective-permute-start(f32[64,128]{1,0:T(8,128)S(1)} %add.70), channel_id=1, source_target_pairs={{0,8},{1,9},{2,10},{3,11},{4,12},{5,13},{6,14},{7,15},{8,0},{9,1},... | collective-permute-start | bytes 98312 | tf_op jit(solution)/shard_map/ppermute | solution.py:467
  124.5 3.6 %copy-start.3 = (bf16[32,65536]{1,0:T(8,128)(2,1)S(1)}, bf16[32,65536]{1,0:T(8,128)(2,1)}, u32[]{:S(2)}) copy-start(bf16[32,65536]{1,0:T(8,128)(2,1)} %own_ref.7) | copy-start | bytes 12582916
